TPU v7x, 32 devices: a whole 2x2x4 slice. The times are simulated.
32 devices in a mesh: seq: 4 (over z), shard: 8 (over y, x, core).
Axes of the slice: x: 2, y: 2, z: 4, core: 2. Of those that a mesh axis runs over, the one named last changes fastest.
Arguments:
- tokens: bfloat16 [8, 2048, 1024], P('shard', 'seq'), may hold values from -6 to 6
- ln1_gain: bfloat16 [1024], P(('seq', 'shard')), may hold values from 0.5 to 1.5
- ln1_bias: bfloat16 [1024], P(('seq', 'shard')), may hold values from -3 to 3
- w_qkv: bfloat16 [1024, 3072], P(('seq', 'shard')), may hold values from -0.1875 to 0.1875
- bias_query: bfloat16 [1024], P(('seq', 'shard')), may hold values from -3 to 3
- bias_value: bfloat16 [1024], P(('seq', 'shard')), may hold values from -3 to 3
- w_out: bfloat16 [1024, 1024], P(('seq', 'shard')), may hold values from -1 to 1
- bias_out: bfloat16 [1024], P(('seq', 'shard')), may hold values from -3 to 3
- ln2_gain: bfloat16 [1024], P(('seq', 'shard')), may hold values from 0.5 to 1.5
- ln2_bias: bfloat16 [1024], P(('seq', 'shard')), may hold values from -3 to 3
- w_in: bfloat16 [1024, 4096], P(('seq', 'shard')), may hold values from -0.1875 to 0.1875
- bias_in: bfloat16 [4096], P(('seq', 'shard')), may hold values from -3 to 3
- w_back: bfloat16 [4096, 1024], P(('seq', 'shard')), may hold values from -0.09375 to 0.09375
- bias_back: bfloat16 [1024], P(('seq', 'shard')), may hold values from -3 to 3
- cotangent: bfloat16 [8, 2048, 1024], P('shard', 'seq'), may hold values from -6 to 6
Outputs:
- result: bfloat16 [8, 2048, 1024], P('shard', 'seq')
- grad_tokens: float32 [8, 2048, 1024], P('shard', 'seq')
- grad_ln1_gain: float32 [1024], P(('seq', 'shard'))
- grad_ln1_bias: float32 [1024], P(('seq', 'shard'))
- grad_w_qkv: float32 [1024, 3072], P(('seq', 'shard'))
- grad_bias_query: float32 [1024], P(('seq', 'shard'))
- grad_bias_value: float32 [1024], P(('seq', 'shard'))
- grad_w_out: float32 [1024, 1024], P(('seq', 'shard'))
- grad_bias_out: float32 [1024], P(('seq', 'shard'))
- grad_ln2_gain: float32 [1024], P(('seq', 'shard'))
- grad_ln2_bias: float32 [1024], P(('seq', 'shard'))
- grad_w_in: float32 [1024, 4096], P(('seq', 'shard'))
- grad_bias_in: float32 [4096], P(('seq', 'shard'))
- grad_w_back: float32 [4096, 1024], P(('seq', 'shard'))
- grad_bias_back: float32 [1024], P(('seq', 'shard'))
All inputs are finite; a program needn't handle non-finite values.
Results may differ from a plain program's by a relative error of at most 0.014.
The roundings to bfloat16 on the way count: a program that leaves them out, or rounds other values in their place, can miss the bound.
Values may be sent and summed in bfloat16 or wider, within the bound.
A program may use at most 192 MiB of HBM per device.

v0:
```python
import math

import jax
import jax.numpy as jnp
from jax import lax
from jax.sharding import PartitionSpec as P

HEAD_DIM = 64


norm_eps = 1e-05
gelu_c = math.sqrt(2.0 / math.pi)


def normalize(values):
    mean_row = jnp.mean(values, axis=-1, keepdims=True)
    centred = values - mean_row
    var_row = jnp.mean(centred * centred, axis=-1, keepdims=True)
    scale_row = lax.rsqrt(var_row + norm_eps)
    return (centred * scale_row, scale_row)


def norm_back(dnormed, normed, scale_row):
    return scale_row * (
        dnormed
        - jnp.mean(dnormed, axis=-1, keepdims=True)
        - normed * jnp.mean(dnormed * normed, axis=-1, keepdims=True)
    )


def gelu_pair(inputs):
    inner = gelu_c * (inputs + 0.044715 * inputs * inputs * inputs)
    tanh_val = jnp.tanh(inner)
    value = 0.5 * inputs * (1.0 + tanh_val)
    slope = 0.5 * (1.0 + tanh_val) + 0.5 * inputs * (1.0 - tanh_val * tanh_val) * gelu_c * (
        1.0 + 3.0 * 0.044715 * inputs * inputs
    )
    return (value, slope)


def masked_scores(query_block, keys, start, scale):
    block = query_block.shape[0]
    length = keys.shape[0]
    scores = (
        jnp.einsum("qgd,kgd->gqk", query_block, keys, preferred_element_type=jnp.float32) * scale
    )
    q_pos = start + jnp.arange(block, dtype=jnp.int32)
    k_pos = jnp.arange(length, dtype=jnp.int32)
    allowed = k_pos[None, None, :] <= q_pos[None, :, None]
    return jnp.where(allowed, scores, -1e30)


def attend_forward(query, keys, values):
    length, groups, width = query.shape
    block = min(512, length)
    scale = 1.0 / math.sqrt(width)

    def one_block(index):
        start = index * block
        q_blk = lax.dynamic_slice_in_dim(query, start, block, 0)
        scores = masked_scores(q_blk, keys, start, scale)
        log_total = jnp.log(jnp.sum(jnp.exp(scores), axis=-1))
        probs = jnp.exp(scores - log_total[:, :, None]).astype(jnp.bfloat16)
        attended = jnp.einsum("gqk,kgd->qgd", probs, values, preferred_element_type=jnp.float32)
        return (attended.astype(jnp.bfloat16), log_total)

    outs, logs = lax.map(one_block, jnp.arange(length // block, dtype=jnp.int32))
    return (outs.reshape(length, groups, width), logs)


def attend_backward(query, keys, values, attended, logs, d_att):
    length, groups, width = query.shape
    block = min(512, length)
    scale = 1.0 / math.sqrt(width)

    def one_block(carry, index):
        d_keys, d_values = carry
        start = index * block
        q_blk = lax.dynamic_slice_in_dim(query, start, block, 0)
        o_blk = lax.dynamic_slice_in_dim(attended, start, block, 0)
        do_blk = lax.dynamic_slice_in_dim(d_att, start, block, 0)
        scores = masked_scores(q_blk, keys, start, scale)
        log_total = lax.dynamic_index_in_dim(logs, index, 0, keepdims=False)
        probs = jnp.exp(scores - log_total[:, :, None])
        probs_b = probs.astype(jnp.bfloat16)
        d_values = d_values + jnp.einsum(
            "gqk,qgd->kgd", probs_b, do_blk, preferred_element_type=jnp.float32
        )
        d_probs = jnp.einsum("qgd,kgd->gqk", do_blk, values, preferred_element_type=jnp.float32)
        delta = jnp.swapaxes(
            jnp.sum(do_blk.astype(jnp.float32) * o_blk.astype(jnp.float32), axis=-1), 0, 1
        )
        d_scores = (probs * (d_probs - delta[:, :, None]) * scale).astype(jnp.bfloat16)
        d_query = jnp.einsum(
            "gqk,kgd->qgd", d_scores, keys, preferred_element_type=jnp.float32
        ).astype(jnp.bfloat16)
        d_keys = d_keys + jnp.einsum(
            "gqk,qgd->kgd", d_scores, q_blk, preferred_element_type=jnp.float32
        )
        return ((d_keys, d_values), d_query)

    zeros = jnp.zeros((length, groups, width), jnp.float32)
    (d_keys, d_values), d_queries = lax.scan(
        one_block, (zeros, zeros), jnp.arange(length // block, dtype=jnp.int32)
    )
    return (
        d_queries.reshape(length, groups, width),
        d_keys.astype(jnp.bfloat16),
        d_values.astype(jnp.bfloat16),
    )


def col_dot(left, right):
    return lax.dot_general(
        left, right, (((0,), (0,)), ((), ())), preferred_element_type=jnp.float32
    )


def row_dot(left, right):
    return lax.dot_general(
        left, right, (((1,), (1,)), ((), ())), preferred_element_type=jnp.float32
    )


def per_device(
    tokens,
    ln1_gain,
    ln1_bias,
    w_qkv,
    bias_query,
    bias_value,
    w_out,
    bias_out,
    ln2_gain,
    ln2_bias,
    w_in,
    bias_in,
    w_back,
    bias_back,
    cotangent,
):
    f32 = jnp.float32
    params = (
        lax.all_gather(ln1_gain, ("seq", "shard"), axis=0, tiled=True),
        lax.all_gather(ln1_bias, ("seq", "shard"), axis=0, tiled=True),
        lax.all_gather(w_qkv, ("seq", "shard"), axis=0, tiled=True),
        lax.all_gather(bias_query, ("seq", "shard"), axis=0, tiled=True),
        lax.all_gather(bias_value, ("seq", "shard"), axis=0, tiled=True),
        lax.all_gather(w_out, ("seq", "shard"), axis=0, tiled=True),
        lax.all_gather(bias_out, ("seq", "shard"), axis=0, tiled=True),
        lax.all_gather(ln2_gain, ("seq", "shard"), axis=0, tiled=True),
        lax.all_gather(ln2_bias, ("seq", "shard"), axis=0, tiled=True),
        lax.all_gather(w_in, ("seq", "shard"), axis=0, tiled=True),
        lax.all_gather(bias_in, ("seq", "shard"), axis=0, tiled=True),
        lax.all_gather(w_back, ("seq", "shard"), axis=0, tiled=True),
        lax.all_gather(bias_back, ("seq", "shard"), axis=0, tiled=True),
    )
    (
        g_one,
        s_one,
        full_qkv,
        full_bq,
        full_bv,
        full_out,
        full_bo,
        g_two,
        s_two,
        full_in,
        full_bin,
        full_back,
        full_bback,
    ) = params
    rows = tokens.shape[1]
    width = tokens.shape[2]
    x_f = tokens[0].astype(f32)
    normed1, scale1 = normalize(x_f)
    h_one = (normed1 * g_one.astype(f32) + s_one.astype(f32)).astype(jnp.bfloat16)
    bias_qkv = jnp.concatenate([full_bq.astype(f32), jnp.zeros((width,), f32), full_bv.astype(f32)])
    qkv = (jnp.dot(h_one, full_qkv, preferred_element_type=f32) + bias_qkv).astype(jnp.bfloat16)
    grouped = lax.all_to_all(
        qkv.reshape(rows, 3, width), "seq", split_axis=2, concat_axis=0, tiled=True
    )
    length = grouped.shape[0]
    local_width = grouped.shape[2]
    groups = local_width // HEAD_DIM
    query = grouped[:, 0].reshape(length, groups, HEAD_DIM)
    keys = grouped[:, 1].reshape(length, groups, HEAD_DIM)
    values = grouped[:, 2].reshape(length, groups, HEAD_DIM)
    attended, logs = attend_forward(query, keys, values)
    att_tok = lax.all_to_all(
        attended.reshape(length, local_width), "seq", split_axis=0, concat_axis=1, tiled=True
    )
    resid = x_f + jnp.dot(att_tok, full_out, preferred_element_type=f32) + full_bo.astype(f32)
    normed2, scale2 = normalize(resid)
    h_two = (normed2 * g_two.astype(f32) + s_two.astype(f32)).astype(jnp.bfloat16)
    pre = jnp.dot(h_two, full_in, preferred_element_type=f32) + full_bin.astype(f32)
    act_val, slope = gelu_pair(pre)
    act = act_val.astype(jnp.bfloat16)
    result = (
        resid + jnp.dot(act, full_back, preferred_element_type=f32) + full_bback.astype(f32)
    ).astype(jnp.bfloat16)
    cot_b = cotangent[0]
    cot_f = cot_b.astype(f32)
    g_w_back = col_dot(act, cot_b)
    g_b_back = jnp.sum(cot_f, axis=0)
    d_pre = (row_dot(cot_b, full_back) * slope).astype(jnp.bfloat16)
    g_w_in = col_dot(h_two, d_pre)
    g_b_in = jnp.sum(d_pre.astype(f32), axis=0)
    d_h2 = row_dot(d_pre, full_in)
    g_g2 = jnp.sum(d_h2 * normed2, axis=0)
    g_s2 = jnp.sum(d_h2, axis=0)
    d_resid = cot_f + norm_back(d_h2 * g_two.astype(f32), normed2, scale2)
    d_resid_b = d_resid.astype(jnp.bfloat16)
    g_w_out = col_dot(att_tok, d_resid_b)
    g_b_out = jnp.sum(d_resid, axis=0)
    d_att_tok = row_dot(d_resid_b, full_out).astype(jnp.bfloat16)
    d_att = lax.all_to_all(d_att_tok, "seq", split_axis=1, concat_axis=0, tiled=True).reshape(
        length, groups, HEAD_DIM
    )
    d_query, d_keys, d_values = attend_backward(query, keys, values, attended, logs, d_att)
    stacked = jnp.stack(
        [
            d_query.reshape(length, local_width),
            d_keys.reshape(length, local_width),
            d_values.reshape(length, local_width),
        ],
        axis=1,
    )
    d_qkv = lax.all_to_all(stacked, "seq", split_axis=0, concat_axis=2, tiled=True).reshape(
        rows, 3 * width
    )
    g_w_qkv = col_dot(h_one, d_qkv)
    g_bq = jnp.sum(d_qkv[:, :width].astype(f32), axis=0)
    g_bv = jnp.sum(d_qkv[:, 2 * width :].astype(f32), axis=0)
    d_h1 = row_dot(d_qkv, full_qkv)
    g_g1 = jnp.sum(d_h1 * normed1, axis=0)
    g_s1 = jnp.sum(d_h1, axis=0)
    d_tokens = d_resid + norm_back(d_h1 * g_one.astype(f32), normed1, scale1)
    summed = (
        lax.psum_scatter(g_g1, ("seq", "shard"), scatter_dimension=0, tiled=True),
        lax.psum_scatter(g_s1, ("seq", "shard"), scatter_dimension=0, tiled=True),
        lax.psum_scatter(g_w_qkv, ("seq", "shard"), scatter_dimension=0, tiled=True),
        lax.psum_scatter(g_bq, ("seq", "shard"), scatter_dimension=0, tiled=True),
        lax.psum_scatter(g_bv, ("seq", "shard"), scatter_dimension=0, tiled=True),
        lax.psum_scatter(g_w_out, ("seq", "shard"), scatter_dimension=0, tiled=True),
        lax.psum_scatter(g_b_out, ("seq", "shard"), scatter_dimension=0, tiled=True),
        lax.psum_scatter(g_g2, ("seq", "shard"), scatter_dimension=0, tiled=True),
        lax.psum_scatter(g_s2, ("seq", "shard"), scatter_dimension=0, tiled=True),
        lax.psum_scatter(g_w_in, ("seq", "shard"), scatter_dimension=0, tiled=True),
        lax.psum_scatter(g_b_in, ("seq", "shard"), scatter_dimension=0, tiled=True),
        lax.psum_scatter(g_w_back, ("seq", "shard"), scatter_dimension=0, tiled=True),
        lax.psum_scatter(g_b_back, ("seq", "shard"), scatter_dimension=0, tiled=True),
    )
    (
        r_g1,
        r_s1,
        r_w_qkv,
        r_bq,
        r_bv,
        r_w_out,
        r_b_out,
        r_g2,
        r_s2,
        r_w_in,
        r_b_in,
        r_w_back,
        r_b_back,
    ) = summed
    return (
        result[None],
        d_tokens[None],
        r_g1,
        r_s1,
        r_w_qkv,
        r_bq,
        r_bv,
        r_w_out,
        r_b_out,
        r_g2,
        r_s2,
        r_w_in,
        r_b_in,
        r_w_back,
        r_b_back,
    )


def solution(mesh):
    return jax.shard_map(
        per_device,
        mesh=mesh,
        in_specs=(
            P("shard", "seq", None),
            P(("seq", "shard")),
            P(("seq", "shard")),
            P(("seq", "shard"), None),
            P(("seq", "shard")),
            P(("seq", "shard")),
            P(("seq", "shard"), None),
            P(("seq", "shard")),
            P(("seq", "shard")),
            P(("seq", "shard")),
            P(("seq", "shard"), None),
            P(("seq", "shard")),
            P(("seq", "shard"), None),
            P(("seq", "shard")),
            P("shard", "seq", None),
        ),
        out_specs=(
            P("shard", "seq", None),
            P("shard", "seq", None),
            P(("seq", "shard")),
            P(("seq", "shard")),
            P(("seq", "shard"), None),
            P(("seq", "shard")),
            P(("seq", "shard")),
            P(("seq", "shard"), None),
            P(("seq", "shard")),
            P(("seq", "shard")),
            P(("seq", "shard")),
            P(("seq", "shard"), None),
            P(("seq", "shard")),
            P(("seq", "shard"), None),
            P(("seq", "shard")),
        ),
        check_vma=False,
    )
```

profile of v0, /device:TPU:1, one launch (start us, length us, event | category | flops | bytes accessed | tf_op | source)
XLA Modules:
  0.0 1236.0 jit_solution(11690931587588916261)
XLA Ops:
  16.1 41.4 %all-reduce.18 = (bf16[1024]{0:T(1024)(128)(2,1)S(1)}, bf16[1024]{0:T(1024)(128)(2,1)S(1)}, bf16[1024]{0:T(1024)(128)(2,1)S(1)}, bf16[1024]{0:T(1024)(128)(2,1)S...) all-reduce(bf16[1024]{0:T(1024)(128)(2,1)S(1)} %dynamic-update-slic, ...), channel_id=1, replica_groups=mesh['seq'=4,'shard'=8] {'seq','shard'}, use_global_device_ids=true, to_apply=%add.3 | all-reduce | flops 8192 | bytes 32768
  60.7 21.9 %all-gather.6.cloned.1.call-done = bf16[1024,3072]{1,0:T(8,128)(2,1)} async-done(((bf16[32,3072]{1,0:T(8,128)(2,1)}), bf16[1024,3072]{1,0:T(8,128)(2,1)}) %all-gather.6.cloned.1.call-update) | async-done | bytes 6291472 | tf_op jit(solution)/shard_map/all_gather | solution.py:146
  104.3 104.5 %all-to-all-done = bf16[512,3,1024]{0,1,2:T(4,128)(2,1)} async-done(((bf16[512,3,1024]{0,1,2:T(4,128)(2,1)}), bf16[512,3,1024]{0,1,2:T(4,128)(2,1)}, u32[]{:S(2)}, u32[]{:S(2)}) %all-to-all-start) | async-done | bytes 3145760 | tf_op jit(solution)/shard_map/all_to_all | solution.py:180
  220.6 50.8 %while.27 = (s32[]{:T(128)}, bf16[4,512,4,64]{1,3,2,0:T(8,128)(2,1)}, f32[4,4,512]{2,1,0:T(4,128)}, s32[4]{0:T(128)S(1)}, bf16[2048,4,64]{0,2,1:T(8,128)(2,1)S(1...) while((s32[]{:T(128)}, ...), condition=%wide.region_4.5_spmd, body=%wide.region_2.4_spmd.sunk | while | flops 1104280064 | bytes 43569372 | solution.py:67
  276.0 58.0 %all-gather = bf16[32,1,128]{2,1,0:T(2,128)(2,1)S(1)} all-gather(bf16[1,1,128]{2,1,0:T(2,128)(2,1)S(1)} %bitcast.188), channel_id=1, replica_groups=mesh['seq'=4,'shard'=8] {'seq','shard'}, dimensions={0}, use_global_device_ids=true | all-gather | bytes 8448 | tf_op jit(solution)/shard_map/all_gather | solution.py:154
  339.2 10.6 fusion.83
  349.7 8.8 all-gather.12.cloned.1.call-done
  358.5 14.9 %convert_reduce_fusion = (f32[4096]{0:T(1024)}, bf16[512,4096]{1,0:T(8,128)(2,1)}) fusion(f32[512,4096]{1,0:T(8,128)} %fusion.83, f32[4096]{0:T(1024)S(1)} %bitcast.185, bf16[4096,1024]{1,0:T(8,128)(2,1)} %all-gather.12.cloned.1.call-done, bf16[1,512,1024]{2,1,0:T(8,128)(2,1)} %param.33), kind=kOutput, calls=%fused_computation.52 | convolution fusion | flops 4341100544 | bytes 22052864 | tf_op jit(solution)/shard_map/dot_general | solution.py:120
  398.1 20.2 %all-to-all-done.2 = bf16[512,4,256]{2,0,1:T(8,128)(2,1)} async-done(((bf16[512,4,256]{2,0,1:T(8,128)(2,1)}), bf16[512,4,256]{2,0,1:T(8,128)(2,1)}, u32[]{:S(2)}, u32[]{:S(2)}) %all-to-all-start.2) | async-done | bytes 1048608 | tf_op jit(solution)/shard_map/all_to_all | solution.py:217
  422.1 156.0 %while.28 = (s32[]{:T(128)}, f32[2048,4,64]{0,2,1:T(8,128)}, f32[2048,4,64]{0,2,1:T(8,128)}, bf16[4,512,4,64]{1,3,2,0:T(8,128)(2,1)}, s32[4]{0:T(128)S(1)}, /*in...) while((s32[]{:T(128)}, f32[2048,4,64]{0,2,1:T(8,128)}, ...), condition=%wide.region_11.12_spmd.clone, body=%wide.region_9.11_spmd.clone.sunk | while | flops 2734291456 | bytes 138236336 | solution.py:103
  438.8 10.5 multiply_convert_fusion.5
  477.2 10.5 multiply_convert_fusion.5
  516.3 10.5 multiply_convert_fusion.5
  555.5 10.5 multiply_convert_fusion.5
  589.1 96.0 %all_to_all.68 = bf16[2048,3,256]{2,1,0:T(4,128)(2,1)S(1)} all-to-all(bf16[2048,3,256]{2,1,0:T(4,128)(2,1)} %copy.82), channel_id=1, replica_groups=mesh['seq'=4,'shard'=8] {'seq'}, dimensions={0} | all-to-all | bytes 6291456 | tf_op jit(solution)/shard_map/all_to_all | solution.py:229
  692.0 8.7 fusion.65
  701.9 16.2 %fusion.68 = f32[4096,1024]{1,0:T(8,128)} fusion(bf16[1,512,1024]{2,1,0:T(8,128)(2,1)S(1)} %copy-done.16, f32[512,4096]{1,0:T(8,128)} %fusion.83, f32[4096]{0:T(1024)S(1)} %bitcast.186), kind=kOutput, calls=%fused_computation.98 | convolution fusion | flops 4315938816 | bytes 26230784 | tf_op jit(solution)/shard_map/dot_general | solution.py:114
  719.8 11.4 fusion.82
  731.9 13.2 %fusion.63 = bf16[1,512,1024]{2,1,0:T(8,128)(2,1)} fusion(f32[512,1024]{1,0:T(8,128)S(1)} %copy-done.6, bf16[4096,1024]{1,0:T(8,128)(2,1)} %all-gather.12.cloned.1.call-done, f32[1024]{0:T(1024)S(1)} %convert_element_type.124, f32[512,4096]{1,0:T(8,128)} %fusion.83, f32[4096]{0:T(1024)S(1)} %bitcast.187), kind=kOutput, calls=%fused_computation.94 | convolution fusion | flops 4317511680 | bytes 19943424 | tf_op jit(solution)/shard_map/dot_general | solution.py:200
  745.5 8.5 fusion.56
  754.0 44.3 %all-reduce.17 = (f32[1024]{0:T(1024)S(1)}, f32[1024]{0:T(1024)S(1)}, f32[1024]{0:T(1024)S(1)}, f32[1024]{0:T(1024)S(1)}, f32[1024]{0:T(1024)S(1)}, /*index=5*/f...) all-reduce(f32[1024]{0:T(1024)S(1)} %get-tuple-element.184, ...), channel_id=2, replica_groups=mesh['seq'=4,'shard'=8] {'seq','shard'}, use_global_device_ids=true, to_apply=%region_15.16.clone | all-reduce | flops 12288 | bytes 98304
  807.2 47.2 %reduce-scatter.5.cloned.1.call-done = f32[32,3072]{1,0:T(8,128)} async-done(((f32[1024,3072]{1,0:T(8,128)}), f32[32,3072]{1,0:T(8,128)}) %reduce-scatter.5.cloned.1.call-update) | async-done | bytes 393232 | tf_op jit(solution)/shard_map/reduce_scatter | solution.py:242
  854.4 187.1 %reduce-scatter.11.cloned.1.call-done = f32[128,1024]{1,0:T(8,128)} async-done(((f32[4096,1024]{1,0:T(8,128)}), f32[128,1024]{1,0:T(8,128)}) %reduce-scatter.11.cloned.1.call-update) | async-done | bytes 524304 | tf_op jit(solution)/shard_map/reduce_scatter | solution.py:251
  1041.5 187.5 %reduce-scatter.9.cloned.1.call-done = f32[32,4096]{1,0:T(8,128)} async-done(((f32[1024,4096]{1,0:T(8,128)}), f32[32,4096]{1,0:T(8,128)}) %reduce-scatter.9.cloned.1.call-update) | async-done | bytes 524304 | tf_op jit(solution)/shard_map/reduce_scatter | solution.py:249
  (294 shorter events, 264.6 us)
Async XLA Ops:
  7.2 75.4 %all-gather.6.cloned.1.call-start = ((), (), s32[]{:S(2)}) async-start(), calls=%async_computation.8 | async-start | bytes 6488064 | tf_op jit(solution)/shard_map/all_gather | solution.py:146
  7.9 326.2 %all-gather.8.cloned.1.call-start = ((), (), s32[]{:S(2)}) async-start(), calls=%async_computation.9 | async-start | bytes 2162688 | tf_op jit(solution)/shard_map/all_gather | solution.py:149
  8.7 330.5 %all-gather.10.cloned.1.call-start = ((), (), s32[]{:S(2)}) async-start(), calls=%async_computation.10 | async-start | bytes 8650752 | tf_op jit(solution)/shard_map/all_gather | solution.py:153
  57.6 25.1 %copy-start.25 = (f32[1024]{0:T(1024)}, f32[1024]{0:T(1024)S(1)}, u32[]{:S(2)}) copy-start(f32[1024]{0:T(1024)S(1)} %convert_element_type.112) | copy-start | bytes 12292
  57.6 25.1 %copy-start.38 = (f32[1024]{0:T(1024)}, f32[1024]{0:T(1024)S(1)}, u32[]{:S(2)}) copy-start(f32[1024]{0:T(1024)S(1)} %convert_element_type.113) | copy-start | bytes 12292
  59.1 23.6 %copy-start.21 = (f32[512]{0:T(512)}, f32[512]{0:T(512)S(1)}, u32[]{:S(2)}) copy-start(f32[512]{0:T(512)S(1)} %broadcast_multiply_fusion.5) | copy-start | bytes 6148
  60.7 21.9 %copy-start.34 = (f32[512]{0:T(512)}, f32[512]{0:T(512)S(1)}, u32[]{:S(2)}) copy-start(f32[512]{0:T(512)S(1)} %add_rsqrt_fusion.1) | copy-start | bytes 6148
  98.8 110.0 %all-to-all-start = ((bf16[512,3,1024]{0,1,2:T(4,128)(2,1)}), bf16[512,3,1024]{0,1,2:T(4,128)(2,1)}, u32[]{:S(2)}, u32[]{:S(2)}) async-start(bf16[512,3,1024]{0,1,2:T(4,128)(2,1)} %copy.72), calls=%async_computation | async-start | bytes 8388608 | tf_op jit(solution)/shard_map/all_to_all | solution.py:180
  103.7 254.8 %all-gather.12.cloned.1.call-start = ((), (), s32[]{:S(2)}) async-start(), calls=%async_computation.11 | async-start | bytes 8650752 | tf_op jit(solution)/shard_map/all_gather | solution.py:155
  220.6 55.4 %copy-start.43 = (bf16[128]{0:T(256)(128)(2,1)S(1)}, bf16[128]{0:T(256)(128)(2,1)}, u32[]{:S(2)}) copy-start(bf16[128]{0:T(256)(128)(2,1)} %param.30) | copy-start | bytes 772
  272.4 61.7 %all-to-all-start.1 = ((bf16[4,512,256]{1,2,0:T(8,128)(2,1)}), bf16[4,512,256]{1,2,0:T(8,128)(2,1)S(1)}, u32[]{:S(2)}, u32[]{:S(2)}) async-start(bf16[4,512,256]{1,2,0:T(8,128)(2,1)} %bitcast.12), calls=%async_computation.1 | async-start | bytes 2097152 | tf_op jit(solution)/shard_map/all_to_all | solution.py:190
  276.0 105.1 %copy-start.27 = (f32[1024]{0:T(1024)}, f32[1024]{0:T(1024)S(1)}, u32[]{:S(2)}) copy-start(f32[1024]{0:T(1024)S(1)} %convert_element_type.119) | copy-start | bytes 12292
  276.0 63.2 %copy-start.40 = (f32[1024]{0:T(1024)}, f32[1024]{0:T(1024)S(1)}, u32[]{:S(2)}) copy-start(f32[1024]{0:T(1024)S(1)} %convert_element_type.120) | copy-start | bytes 12292
  334.1 24.4 %copy-start.30 = (f32[32,1,128]{2,1,0:T(1,128)}, f32[32,1,128]{2,1,0:T(1,128)S(1)}, u32[]{:S(2)}) copy-start(f32[32,1,128]{2,1,0:T(1,128)S(1)} %convert_element_type.137) | copy-start | bytes 49156
  338.7 34.7 %copy-start.5 = (f32[512,1024]{1,0:T(8,128)}, f32[512,1024]{1,0:T(8,128)S(1)}, u32[]{:S(2)}) copy-start(f32[512,1024]{1,0:T(8,128)S(1)} %get-tuple-element.254) | copy-start | bytes 6291460
  338.8 42.4 %copy-start.19 = (f32[512]{0:T(512)}, f32[512]{0:T(512)S(1)}, u32[]{:S(2)}) copy-start(f32[512]{0:T(512)S(1)} %broadcast_multiply_fusion.4) | copy-start | bytes 6148
  339.1 42.0 %copy-start.32 = (f32[512]{0:T(512)}, f32[512]{0:T(512)S(1)}, u32[]{:S(2)}) copy-start(f32[512]{0:T(512)S(1)} %add_rsqrt_fusion) | copy-start | bytes 6148
  358.5 14.9 %copy-start.44 = (bf16[1024,4096]{1,0:T(8,128)(2,1)S(1)}, bf16[1024,4096]{1,0:T(8,128)(2,1)}, u32[]{:S(2)}) copy-start(bf16[1024,4096]{1,0:T(8,128)(2,1)} %all-gather.10.cloned.1.call-done) | copy-start | bytes 25165828
  386.9 31.4 %all-to-all-start.2 = ((bf16[512,4,256]{2,0,1:T(8,128)(2,1)}), bf16[512,4,256]{2,0,1:T(8,128)(2,1)}, u32[]{:S(2)}, u32[]{:S(2)}) async-start(bf16[512,4,256]{2,0,1:T(8,128)(2,1)} %bitcast.179), calls=%async_computation.2 | async-start | bytes 2097152 | tf_op jit(solution)/shard_map/all_to_all | solution.py:217
  391.1 416.1 %reduce-scatter.7.cloned.1.call-start = ((), (), s32[]{:S(2)}) async-start(), calls=%async_computation.13 | async-start | bytes 4325376 | tf_op jit(solution)/shard_map/reduce_scatter | solution.py:245
  398.1 456.3 %reduce-scatter.5.cloned.1.call-start = ((), (), s32[]{:S(2)}) async-start(), calls=%async_computation.12 | async-start | bytes 12976128 | tf_op jit(solution)/shard_map/reduce_scatter | solution.py:242
  700.7 340.8 %reduce-scatter.11.cloned.1.call-start = ((), (), s32[]{:S(2)}) async-start(), calls=%async_computation.15 | async-start | bytes 17301504 | tf_op jit(solution)/shard_map/reduce_scatter | solution.py:251
  718.1 510.9 %reduce-scatter.9.cloned.1.call-start = ((), (), s32[]{:S(2)}) async-start(), calls=%async_computation.14 | async-start | bytes 17301504 | tf_op jit(solution)/shard_map/reduce_scatter | solution.py:249
  745.5 58.1 %copy-start.4 = (f32[512,1024]{1,0:T(8,128)S(1)}, f32[512,1024]{1,0:T(8,128)}, u32[]{:S(2)}) copy-start(f32[512,1024]{1,0:T(8,128)} %copy-done.3) | copy-start | bytes 6291460
  (50 other events, 240.0 us)
Sparse Core Ops, SparseCore 0:
  10.8 71.7 all-gather.5
  85.5 74.7 all-gather.7
  163.1 106.1 all-gather.9
  272.0 86.4 all-gather.11
  398.2 137.9 reduce-scatter.6
  700.8 153.5 reduce-scatter.4
  857.2 184.1 reduce-scatter.10
  1044.3 184.6 reduce-scatter.8
where the time goes:
time: 1250 us; the launch traced here: 1240 us
  waiting for transfers between devices  579 us (46%)
  matrix products  282 us (23%)
  blocking collectives  240 us (19%)
  local copies, waits for them, and re-layouts  70.1 us (6%)
  other arithmetic  22.5 us (2%)
  between operations  14.9 us (1%)
  loops' own time  14 us (1%)
  starting transfers between devices  13.4 us (1%)
    reduce_scatter x1, waiting for transfers between devices, per_device(): lax.psum_scatter(g_w_in, ('seq', 'shard'), scatter_dimension=0, tiled=True)  188 us
    reduce_scatter x1, waiting for transfers between devices, per_device(): lax.psum_scatter(g_w_back, ('seq', 'shard'), scatter_dimension=0, tiled=T...  187 us
    all_to_all x1, waiting for transfers between devices, per_device(): lax.all_to_all(qkv.reshape(rows, 3, width), 'seq', split_axis=2, concat_a...  105 us
    all_to_all x1, blocking collectives, per_device(): lax.all_to_all(stacked, 'seq', split_axis=0, concat_axis=2, tiled=True)  96 us
    unnamed x2, blocking collectives  85.8 us
    all_gather x1, blocking collectives, per_device(): lax.all_gather(bias_in, ('seq', 'shard'), axis=0, tiled=True)  58 us
    reduce_scatter x1, waiting for transfers between devices, per_device(): lax.psum_scatter(g_w_qkv, ('seq', 'shard'), scatter_dimension=0, tiled=True)  47.2 us
    dot_general x4, matrix products, one_block(): jnp.einsum('qgd,kgd->gqk', do_blk, values, preferred_element_type=jnp.flo...  42 us
  transfers between devices with their start and end apart: 11, of which 7 were waited for; matrix products, arithmetic and copies ran while one was open for 28% of the time, Pallas kernels for 0%

commit v1 on v0

v1 whole, which is shorter than its diff:
```python
import math

import jax
import jax.numpy as jnp
from jax import lax
from jax.experimental import pallas as pl
from jax.experimental.pallas import tpu as pltpu
from jax.sharding import PartitionSpec as P

HEAD_DIM = 64
LANES = 128
MESH = pl.DeviceIdType.MESH
NT = (((1,), (1,)), ((), ()))
TN = (((0,), (0,)), ((), ()))
f32 = jnp.float32
bf16 = jnp.bfloat16

norm_eps = 1e-05
gelu_c = math.sqrt(2.0 / math.pi)
scale = 1.0 / math.sqrt(HEAD_DIM)

VM = pl.BlockSpec(memory_space=pltpu.VMEM)
HB = pl.BlockSpec(memory_space=pl.ANY)


def dot(a, b):
    return jnp.dot(a, b, preferred_element_type=f32)


def row_dot(a, b):
    return lax.dot_general(a, b, NT, preferred_element_type=f32)


def col_dot(a, b):
    return lax.dot_general(a, b, TN, preferred_element_type=f32)


def normalize(values):
    mean_row = jnp.mean(values, axis=-1, keepdims=True)
    centred = values - mean_row
    var_row = jnp.mean(centred * centred, axis=-1, keepdims=True)
    scale_row = lax.rsqrt(var_row + norm_eps)
    return (centred * scale_row, scale_row)


def norm_back(dnormed, normed, scale_row):
    return scale_row * (
        dnormed
        - jnp.mean(dnormed, axis=-1, keepdims=True)
        - normed * jnp.mean(dnormed * normed, axis=-1, keepdims=True)
    )


def gelu_pair(inputs):
    inner = gelu_c * (inputs + 0.044715 * inputs * inputs * inputs)
    tanh_val = jnp.tanh(inner)
    value = 0.5 * inputs * (1.0 + tanh_val)
    slope = 0.5 * (1.0 + tanh_val) + 0.5 * inputs * (1.0 - tanh_val * tanh_val) * gelu_c * (
        1.0 + 3.0 * 0.044715 * inputs * inputs
    )
    return (value, slope)


def block_rows(index, size, count=1):
    return pl.ds(pl.multiple_of(index * size, size), size * count)


def head_lanes(shape, head):
    return lax.broadcasted_iota(jnp.int32, shape, len(shape) - 1) // HEAD_DIM == head


def only_head(values, head):
    return jnp.where(head_lanes(values.shape, head), values, jnp.zeros_like(values))


def spread_heads(columns, rows, width):
    out = None
    for head in range(width // HEAD_DIM):
        one = jnp.broadcast_to(columns[:, head : head + 1], (rows, width))
        out = one if out is None else jnp.where(head_lanes((rows, width), head), one, out)
    return out


class Place:
    def __init__(self, n, m):
        self.n, self.m, self.half, self.planes = n, m, n // 2, m // 2
        self.s, self.k = lax.axis_index("seq"), lax.axis_index("shard")
        self.core, self.plane = lax.rem(self.k, 2), self.k // 2
        self.team, self.low = self.s // self.half, lax.rem(self.s, self.half)
        self.rank = self.low + self.half * self.core
        self.index = self.s * m + self.k

    def member(self, rank):
        return (self.team * self.half + lax.rem(rank, self.half), 2 * self.plane + rank // self.half)

    def across(self):
        return (lax.rem(self.s + self.half, self.n), self.k)

    def swap(self):
        return (lax.rem(self.s + self.half, self.n), 2 * self.plane + 1 - self.core)

    def partner(self):
        return (self.s, 2 * self.plane + 1 - self.core)

    def along(self, step):
        return lax.rem(self.s + step, self.n)

    def beside(self, step):
        return lax.rem(self.plane + step, self.planes)

    def greet(self):
        barrier = pltpu.get_barrier_semaphore()
        count = 0

        def signal(device):
            pl.semaphore_signal(barrier, inc=1, device_id=device, device_id_type=MESH)

        for step in range(1, self.n):
            signal((self.along(step), self.k))
            count += 1
        for step in range(self.n):
            signal((self.along(step), 2 * self.plane + 1 - self.core))
            count += 1
        for step in range(1, self.planes):
            signal((self.s, 2 * self.beside(step) + self.core))
            count += 1
        pl.semaphore_wait(barrier, count)


def send(src, dst, sems, at, device):
    pltpu.make_async_remote_copy(
        src_ref=src,
        dst_ref=dst,
        send_sem=sems[0].at[at],
        recv_sem=sems[1].at[at],
        device_id=device,
        device_id_type=MESH,
    ).start()


def settle(view, sem):
    pltpu.make_async_copy(view, view, sem).wait()


def attend_row(i, q_ref, k_ref, v_ref, o_ref, lse_ref, qm, m_s, l_s, acc, size):
    width = q_ref.shape[1]
    heads = width // HEAD_DIM
    rows = block_rows(i, size)
    q = q_ref[rows, :] * jnp.asarray(scale, bf16)
    for h in range(heads):
        qm[h] = only_head(q, h)

    def step(j, diagonal):
        at = block_rows(j, size)
        k = k_ref[at, :]
        v = v_ref[at, :]
        old = m_s[...]
        tops, sums, total = [], [], None
        for h in range(heads):
            s = row_dot(k, qm[h])
            if diagonal:
                k_pos = lax.broadcasted_iota(jnp.int32, (size, size), 0)
                q_pos = lax.broadcasted_iota(jnp.int32, (size, size), 1)
                s = jnp.where(k_pos <= q_pos, s, -1e30)
            top = jnp.max(s, axis=0, keepdims=True)
            if not diagonal:
                top = jnp.maximum(old[h : h + 1], top)
            p = jnp.exp(s - top)
            tops.append(top)
            sums.append(jnp.sum(p, axis=0, keepdims=True))
            part = col_dot(p.astype(bf16), only_head(v, h))
            total = part if total is None else total + part
        rest = [jnp.zeros((8 - heads, size), f32)] if heads < 8 else []
        top = jnp.concatenate(tops + rest, 0)
        add = jnp.concatenate(sums + rest, 0)
        if diagonal:
            l_s[...] = add
            acc[...] = total
        else:
            fade = jnp.exp(old - top)
            l_s[...] = l_s[...] * fade + add
            acc[...] = acc[...] * spread_heads(jnp.transpose(fade), size, width) + total
        m_s[...] = top

    step(i, True)

    def body(j, carry):
        step(j, False)
        return carry

    lax.fori_loop(0, i, body, 0)
    l = l_s[...]
    lse_ref[:, rows] = m_s[...] + jnp.log(l)
    o_ref[rows, :] = (acc[...] * spread_heads(jnp.transpose(1.0 / l), size, width)).astype(bf16)


def forward_call(n, m, tok, cot, wq_s, sm_s, wo_s, wi_s, wb_s):
    size, d = tok.shape
    nd = n * m
    length = n * size
    width = d // n
    rq = wq_s.shape[1]
    chunks = []
    chunks.append((0, wo_s.shape[0], 0, wo_s.shape[0], 0, wo_s.shape[1]))
    for part in range(2):
        columns = wi_s.shape[1] // 2
        chunks.append((1, wi_s.shape[0], 0, wi_s.shape[0], part * columns, columns))
    for part in range(2):
        rows = wb_s.shape[0] // 2
        chunks.append((2, wb_s.shape[0], part * rows, rows, 0, wb_s.shape[1]))
    nc = len(chunks)

    def kernel(
        tok_r, cot_r, wqs_r, sms_r, wos_r, wis_r, wbs_r,
        wo_r, wi_r, wb_r, q_r, k_r, v_r, o_r, lse_r, att_r, h1_r, wq_r, tb_r, cb_r, sv_r,
        tokf, sma, qm, m_s, l_s, acc, vec,
        t_send, t_recv, w_send, w_recv, a_send, a_recv, z_send, z_recv, p_send, p_recv, c_send, c_recv, loc,
    ):
        at = Place(n, m)
        half, planes, rank, core = at.half, at.planes, at.rank, at.core
        fulls, shards = (wo_r, wi_r, wb_r), (wos_r, wis_r, wbs_r)
        ts, ws, zs, ps, cs = (t_send, t_recv), (w_send, w_recv), (z_send, z_recv), (p_send, p_recv), (c_send, c_recv)
        at.greet()
        away = core != at.team

        own_w = pltpu.make_async_copy(wqs_r.at[rank], wq_r.at[block_rows(at.index, rq)], loc.at[0])
        own_s = pltpu.make_async_copy(sms_r, sma.at[at.index], loc.at[1])
        own_w.start()
        own_s.start()
        for step in range(1, n):
            other = lax.rem(rank + step, n)
            send(wqs_r.at[other], wq_r.at[block_rows(at.index, rq)], ws, 0, at.member(other))
            send(sms_r, sma.at[at.index], ws, 1, at.member(other))

        @pl.when(away)
        def _():
            send(tok_r, tokf.at[at.low + half * (1 - core)], ts, 0, at.swap())

        @pl.when(jnp.logical_not(away))
        def _():
            pltpu.make_async_copy(tok_r, tokf.at[rank], loc.at[2]).start()

        own_w.wait()
        own_s.wait()
        settle(wq_r.at[pl.ds(0, (n - 1) * rq)], w_recv.at[0])
        settle(sma.at[pl.ds(0, n - 1)], w_recv.at[1])
        for low in range(half):
            row = (at.team * half + low) * m + 2 * at.plane
            send(wq_r.at[block_rows(row, rq, 2)], wq_r.at[block_rows(row, rq, 2)], ws, 2, at.across())
            send(sma.at[pl.ds(row, 2)], sma.at[pl.ds(row, 2)], ws, 3, at.across())

        @pl.when(away)
        def _():
            settle(tokf.at[0], t_recv.at[0])

        @pl.when(jnp.logical_not(away))
        def _():
            settle(tokf.at[0], loc.at[2])

        for step in range(1, half):
            low = lax.rem(at.low + step, half)
            send(tokf.at[rank], tokf.at[rank], ts, 1, (at.team * half + low, at.k))
        send(tokf.at[rank], tokf.at[rank], ts, 2, at.partner())

        @pl.when(away)
        def _():
            send(cot_r, cb_r, ts, 4, at.swap())

        @pl.when(jnp.logical_not(away))
        def _():
            pltpu.make_async_copy(cot_r, cb_r, loc.at[3]).start()

        def piece(c, device):
            which, rs, r0, nr, c0, ncol = chunks[c]
            return fulls[which].at[pl.ds(pl.multiple_of(device * rs + r0, 8), nr), pl.ds(c0, ncol)]

        def some(c, count):
            which, rs, r0, nr, c0, ncol = chunks[c]
            return fulls[which].at[pl.ds(0, count * nr), pl.ds(c0, ncol)]

        def mine(c):
            which, rs, r0, nr, c0, ncol = chunks[c]
            return shards[which].at[pl.ds(r0, nr), pl.ds(c0, ncol)]

        for c in range(nc):
            pltpu.make_async_copy(mine(c), piece(c, at.index), loc.at[4 + c]).start()
            for step in range(1, n):
                send(mine(c), piece(c, at.index), zs, c, (at.along(step), at.k))

        settle(wq_r.at[pl.ds(0, half * 2 * rq)], w_recv.at[2])
        settle(sma.at[pl.ds(0, half * 2)], w_recv.at[3])
        for step in range(1, planes):
            there = (at.s, 2 * at.beside(step) + core)
            for other in range(n):
                row = other * m + 2 * at.plane
                send(wq_r.at[block_rows(row, rq, 2)], wq_r.at[block_rows(row, rq, 2)], ws, 4, there)
                send(sma.at[pl.ds(row, 2)], sma.at[pl.ds(row, 2)], ws, 5, there)

        def z_to_p(c):
            settle(some(c, 1), loc.at[4 + c])
            settle(some(c, n - 1), z_recv.at[c])
            for step in range(1, planes):
                there = (at.s, 2 * at.beside(step) + core)
                for other in range(n):
                    view = piece(c, other * m + at.k)
                    send(view, view, ps, c, there)

        def p_to_c(c):
            settle(some(c, (planes - 1) * n), p_recv.at[c])
            for other in range(n * planes):
                view = piece(c, other * 2 + core)
                send(view, view, cs, c, at.partner())

        settle(wq_r.at[pl.ds(0, (planes - 1) * n * 2 * rq)], w_recv.at[4])
        settle(sma.at[pl.ds(0, (planes - 1) * n * 2)], w_recv.at[5])
        per = LANES // (d // nd)
        for group in range(d // LANES):
            total = sma[group * per].astype(f32)
            for other in range(1, per):
                total = total + sma[group * per + other].astype(f32)
            sv_r[:, group * LANES : (group + 1) * LANES] = total
            vec[0, group : group + 1, :] = total[2:3]
            vec[1, group : group + 1, :] = total[3:4]

        def norm_block(b):
            def body(t, carry):
                part = pl.ds(pl.multiple_of(t * 128, 128), 128)
                x = tokf[b, part, :].astype(f32)
                normed, _ = normalize(x)
                h1_r[pl.ds(pl.multiple_of(b * size + t * 128, 128), 128), :] = (
                    normed * sv_r[0:1, :] + sv_r[1:2, :]
                ).astype(bf16)
                return carry

            lax.fori_loop(0, size // 128, body, 0)

        groups = width // LANES
        bias_q = jnp.concatenate([vec[0, pl.ds(rank * groups + g, 1), :] for g in range(groups)], 1)
        bias_v = jnp.concatenate([vec[1, pl.ds(rank * groups + g, 1), :] for g in range(groups)], 1)

        def project_block(b):
            def body(t, carry):
                part = pl.ds(pl.multiple_of(b * size + t * 256, 256), 256)
                h = h1_r[part, :]
                q_r[part, :] = (dot(h, wq_r[:, 0:width]) + bias_q).astype(bf16)
                k_r[part, :] = dot(h, wq_r[:, width : 2 * width]).astype(bf16)
                v_r[part, :] = (dot(h, wq_r[:, 2 * width : 3 * width]) + bias_v).astype(bf16)
                return carry

            lax.fori_loop(0, size // 256, body, 0)

        def take_block(b):
            norm_block(b)
            project_block(b)

        take_block(rank)
        settle(tokf.at[0], t_recv.at[2])
        take_block(lax.rem(rank + half, n))
        if half > 1:
            settle(tokf.at[pl.ds(0, half - 1)], t_recv.at[1])
            for step in range(1, half):
                b = lax.rem(at.low + step, half) + half * core
                send(tokf.at[b], tokf.at[b], ts, 3, at.partner())
        z_to_p(0)
        for step in range(1, half):
            take_block(lax.rem(at.low + step, half) + half * core)
        if half > 1:
            settle(tokf.at[pl.ds(0, half - 1)], t_recv.at[3])
            for step in range(1, half):
                take_block(lax.rem(at.low + step, half) + half * (1 - core))
        tb_r[...] = tokf[rank]
        z_to_p(1)

        def row(i, carry):
            attend_row(i, q_r, k_r, v_r, o_r, lse_r, qm, m_s, l_s, acc, size)
            src = o_r.at[block_rows(i, size)]
            dst = att_r.at[:, block_rows(rank, width)]

            @pl.when(i != rank)
            def _():
                send(src, dst, (a_send, a_recv), 0, at.member(i))

            @pl.when(i == rank)
            def _():
                pltpu.make_async_copy(src, dst, loc.at[2]).start()

            for c, when in ((2, 1), (3, 2), (4, n - 1)):

                @pl.when(i == when)
                def _(c=c):
                    z_to_p(c)
                    if c == 4:
                        p_to_c(0)

            return carry

        lax.fori_loop(0, n, row, 0)
        settle(tokf.at[0, :, pl.ds(0, width)], loc.at[2])
        others = tokf.at[0, :, pl.ds(0, (n - 1) * width)]
        settle(others, a_recv.at[0])
        for c in range(1, nc):
            p_to_c(c)
        for c in range(nc):
            settle(some(c, n * planes), c_recv.at[c])

        settle(others, a_send.at[0])
        for c in range(nc):
            settle(some(c, n - 1), z_send.at[c])
            settle(some(c, (planes - 1) * n), p_send.at[c])
            settle(some(c, n * planes), c_send.at[c])
        for at_sem, count in ((0, n - 1), (2, half * 2), (4, (planes - 1) * n * 2)):
            settle(wq_r.at[pl.ds(0, count * rq)], w_send.at[at_sem])
            settle(sma.at[pl.ds(0, count)], w_send.at[at_sem + 1])

        @pl.when(away)
        def _():
            settle(tokf.at[0], t_send.at[0])
            settle(cb_r, t_recv.at[4])
            settle(cb_r, t_send.at[4])

        @pl.when(jnp.logical_not(away))
        def _():
            settle(cb_r, loc.at[3])

        settle(tokf.at[0], t_send.at[2])
        if half > 1:
            settle(tokf.at[pl.ds(0, half - 1)], t_send.at[1])
            settle(tokf.at[pl.ds(0, half - 1)], t_send.at[3])

    def sds(shape, dtype=bf16):
        return jax.ShapeDtypeStruct(shape, dtype)

    sems = pltpu.SemaphoreType.DMA
    return pl.pallas_call(
        kernel,
        name="gather_attend",
        out_shape=(
            sds((nd * wo_s.shape[0], wo_s.shape[1])),
            sds((nd * wi_s.shape[0], wi_s.shape[1])),
            sds((nd * wb_s.shape[0], wb_s.shape[1])),
            sds((length, width)), sds((length, width)), sds((length, width)), sds((length, width)),
            sds((8, length), f32),
            sds((size, d)),
            sds((length, d)),
            sds((d, 3 * width)),
            sds((size, d)), sds((size, d)),
            sds((16, d), f32),
        ),
        in_specs=[HB] * 7,
        out_specs=(HB,) * 3 + (VM,) * 11,
        scratch_shapes=[
            pltpu.VMEM((n, size, d), bf16),
            pltpu.VMEM((nd, 16, LANES), bf16),
            pltpu.VMEM((width // HEAD_DIM, size, width), bf16),
            pltpu.VMEM((8, size), f32),
            pltpu.VMEM((8, size), f32),
            pltpu.VMEM((size, width), f32),
            pltpu.VMEM((2, max(8, d // LANES), LANES), f32),
            sems((5,)), sems((5,)),
            sems((6,)), sems((6,)),
            sems((1,)), sems((1,)),
            sems((nc,)), sems((nc,)),
            sems((nc,)), sems((nc,)),
            sems((nc,)), sems((nc,)),
            sems((4 + nc,)),
        ],
        compiler_params=pltpu.CompilerParams(
            collective_id=0, has_side_effects=True, vmem_limit_bytes=62 << 20
        ),
    )(tok, cot, wq_s, sm_s, wo_s, wi_s, wb_s)


def small_pack(index, vectors):
    per = vectors[0].shape[0]
    rows = [part for v in vectors for part in v.reshape(-1, per)]
    rows = jnp.stack(rows + [jnp.zeros_like(rows[0])] * (16 - len(rows)))
    lane = lax.broadcasted_iota(jnp.int32, (16, LANES), 1)
    spread = jnp.tile(rows, (1, LANES // per))
    return jnp.where(lane // per == lax.rem(index, LANES // per), spread, jnp.zeros_like(spread))


def backward_call(n, m, res, dat, dres, q, k, v, o, lse, h1, wq, tb, sv, gsm, gwo, gwi, gwb):
    size, d = res.shape
    nd = n * m
    length = n * size
    width = d // n
    heads = width // HEAD_DIM
    half, planes = n // 2, m // 2
    rq = d // nd
    ro, ri, rb = gwo.shape[0] // nd, gwi.shape[0] // nd, gwb.shape[0] // nd
    chunks = [(0, ro, 0, ro, 0, gwo.shape[1])]
    for part in range(2):
        columns = gwi.shape[1] // 2
        chunks.append((1, ri, 0, ri, part * columns, columns))
    for part in range(2):
        rows = rb // 2
        chunks.append((2, rb, part * rows, rows, 0, gwb.shape[1]))
    chunks = chunks[3:] + chunks[1:3] + chunks[:1]
    nc = len(chunks)
    lanes_s = d // n

    def kernel(*refs):
        (res_r, dat_r, dres_r, q_r, k_r, v_r, o_r, lse_r, h1_r, wq_r, tb_r, sv_r, gsm_r, gwo_r, gwi_r, gwb_r) = refs[:16]
        (reso_r, gt_r, gq_r, go_r, gi_r, gb_r, small_r) = refs[16:23]
        (do, delta, dqa, dka, dva, dqkv, gacc, rqp, rqh, pf, sd, rd, rzd, rg, sm, smz, smp, smc) = refs[23:41]
        rest = refs[41:]
        ga, rc, rp, rz = (rest[i * nc : (i + 1) * nc] for i in range(4))
        (d_s, d_r, x_s, x_r, y_s, y_r, e_s, e_r, c_s, c_r, p_s, p_r, z_s, z_r, m_s, m_r, loc) = rest[4 * nc :]
        gqb, hb, sg = rc[0].at[:, pl.ds(0, 3 * width)], rc[1], rc[4]
        tb_v, o_v = rc[2].at[:, pl.ds(0, d)], rc[3]
        at = Place(n, m)
        rank, core, low = at.rank, at.core, at.low
        grads = (gwo_r, gwi_r, gwb_r)
        outs = (go_r, gi_r, gb_r)
        at.greet()
        away = core != at.team

        for step in range(1, n):
            other = lax.rem(rank + step, n)
            send(dat_r.at[:, block_rows(other, width)], do.at[block_rows(rank, size)], (d_s, d_r), 0, at.member(other))
        own_do = pltpu.make_async_copy(dat_r.at[:, block_rows(rank, width)], do.at[block_rows(rank, size)], loc.at[0])
        own_do.start()

        def piece(c, device):
            which, rs, r0, nr, c0, ncol = chunks[c]
            return grads[which].at[pl.ds(pl.multiple_of(device * rs + r0, 8), nr), pl.ds(c0, ncol)]

        def cells(ref, c, index, count=1):
            nr = chunks[c][3]
            return ref.at[pl.ds(pl.multiple_of(index * nr, nr), count * nr)]

        for c in range(nc):
            for other in range(n * planes):
                send(piece(c, 2 * other + 1 - core), cells(rc[c], c, other), (c_s, c_r), c, at.partner())
                pltpu.make_async_copy(piece(c, 2 * other + core), cells(ga[c], c, other), loc.at[4 + c]).start()

        @pl.when(away)
        def _():
            send(res_r, reso_r, (x_s, x_r), 0, at.swap())

        @pl.when(jnp.logical_not(away))
        def _():
            pltpu.make_async_copy(res_r, reso_r, loc.at[1]).start()

        own_dres = pltpu.make_async_copy(dres_r, gt_r, loc.at[2])
        own_dres.start()

        def fetch_h1(b):
            return pltpu.make_async_copy(h1_r.at[block_rows(b, size)], hb.at[block_rows(lax.rem(b, 2), size)], loc.at[3])

        def c_to_p(c):
            nr = chunks[c][3]
            settle(ga[c], loc.at[4 + c])
            settle(rc[c], c_r.at[c])

            def add(t, carry):
                rows = block_rows(t, nr)
                ga[c][rows, :] = (ga[c][rows, :].astype(f32) + rc[c][rows, :].astype(f32)).astype(bf16)
                return carry

            lax.fori_loop(0, n * planes, add, 0)
            for step in range(1, planes):
                other = at.beside(step)
                for s in range(n):
                    send(
                        cells(ga[c], c, s * planes + other),
                        cells(rp[c], c, (step - 1) * n + s),
                        (p_s, p_r), c, (at.s, 2 * other + core),
                    )

        def p_to_z(c):
            nr = chunks[c][3]
            settle(rp[c], p_r.at[c])

            def add(s, carry):
                rows = block_rows(s * planes + at.plane, nr)
                total = ga[c][rows, :].astype(f32)
                for step in range(1, planes):
                    total = total + rp[c][block_rows((step - 1) * n + s, nr), :].astype(f32)
                ga[c][rows, :] = total.astype(bf16)
                return carry

            lax.fori_loop(0, n, add, 0)
            for step in range(1, n):
                s = at.along(step)
                send(cells(ga[c], c, s * planes + at.plane), cells(rz[c], c, step - 1), (z_s, z_r), c, (s, at.k))

        def z_to_out(c):
            which, rs, r0, nr, c0, ncol = chunks[c]
            settle(rz[c], z_r.at[c])
            total = ga[c][block_rows(at.s * planes + at.plane, nr), :].astype(f32)
            for step in range(1, n):
                total = total + rz[c][(step - 1) * nr : step * nr, :].astype(f32)
            outs[which][r0 : r0 + nr, c0 : c0 + ncol] = total

        for c in range(nc):
            c_to_p(c)
        fetch_h1(0).start()
        fetch_tb = pltpu.make_async_copy(tb_r, tb_v, loc.at[4])
        fetch_tb.start()
        for i in range(n):
            pltpu.make_async_copy(o_r.at[pl.ds(i * size, size)], o_v.at[:, pl.ds(i * width, width)], loc.at[5]).start()

        own_do.wait()
        settle(do.at[pl.ds(0, (n - 1) * size)], d_r.at[0])

        settle(o_v.at[:, pl.ds(0, n * width)], loc.at[5])
        pick = (
            lax.broadcasted_iota(jnp.int32, (8, width), 1) // HEAD_DIM
            == lax.broadcasted_iota(jnp.int32, (8, width), 0)
        ).astype(f32)

        def prepare(i, carry):
            rows = block_rows(i, size)
            product = do[rows, :].astype(f32) * o_v[:, block_rows(i, width)].astype(f32)
            delta[:, rows] = lax.dot_general(
                pick, product, NT, preferred_element_type=f32, precision=lax.Precision.HIGHEST
            )
            dqa[rows, :] = jnp.zeros((size, width), f32)
            return carry

        lax.fori_loop(0, n, prepare, 0)
        gacc[...] = jnp.zeros_like(gacc)
        sm[...] = jnp.zeros_like(sm)
        sm[4:12, :] = gsm_r[...]

        def pair(i, j, diagonal):
            rows, at_k = block_rows(i, size), block_rows(j, size)
            kk, vv = k_r[at_k, :], v_r[at_k, :]
            qs, dd = q_r[rows, :] * jnp.asarray(scale, bf16), do[rows, :]
            dq = dk = dv = None
            for h in range(heads):
                qh, dh_, kh = only_head(qs, h), only_head(dd, h), only_head(kk, h)
                p = jnp.exp(row_dot(kk, qh) - lse_r[h : h + 1, rows])
                if diagonal:
                    k_pos = lax.broadcasted_iota(jnp.int32, (size, size), 0)
                    q_pos = lax.broadcasted_iota(jnp.int32, (size, size), 1)
                    p = jnp.where(k_pos <= q_pos, p, 0.0)
                dp = row_dot(vv, dh_)
                ds = (p * (dp - delta[h : h + 1, rows])).astype(bf16)
                one, two, three = dot(p.astype(bf16), dh_), dot(ds, qh), col_dot(ds, kh)
                dv = one if dv is None else dv + one
                dk = two if dk is None else dk + two
                dq = three if dq is None else dq + three
            dva[...] += dv
            dka[...] += dk
            dqa[rows, :] += dq

        def owner(j):
            return j // half, lax.rem(j, half)

        def finish_block(j):
            core_j, low_j = owner(j)

            @pl.when(core_j == core)
            def _():
                settle(rd.at[0], y_r.at[low_j])

                def add(t, carry):
                    rows = pl.ds(pl.multiple_of(t * 128, 128), 128)
                    rd[low_j, rows, :] = (pf[rows, :] + rd[low_j, rows, :].astype(f32)).astype(bf16)
                    return carry

                lax.fori_loop(0, size // 128, add, 0)

                @pl.when(low_j != low)
                def _():
                    slot = lax.rem(low_j - low + half, half) - 1
                    send(rd.at[low_j], rzd.at[slot], (e_s, e_r), 0, (at.team * half + low_j, at.k))

        def column(j, carry):
            fetch_h1(j).wait()

            @pl.when(j + 1 < n)
            def _():
                fetch_h1(j + 1).start()

            dka[...] = jnp.zeros_like(dka)
            dva[...] = jnp.zeros_like(dva)
            pair(j, j, True)

            def inner(i, c2):
                pair(i, j, False)
                return c2

            lax.fori_loop(j + 1, n, inner, 0)
            dqb = (dqa[block_rows(j, size), :] * scale).astype(bf16)
            dkb, dvb = dka[...].astype(bf16), dva[...].astype(bf16)
            dqkv[:, 0:width] = dqb
            dqkv[:, width : 2 * width] = dkb
            dqkv[:, 2 * width : 3 * width] = dvb
            mine = block_rows(rank, width)
            sm[2:3, mine] += jnp.sum(dqb.astype(f32), axis=0, keepdims=True)
            sm[3:4, mine] += jnp.sum(dvb.astype(f32), axis=0, keepdims=True)

            @pl.when(j > 0)
            def _():
                finish_block(j - 1)

            core_j, low_j = owner(j)

            def project(t, c2):
                rows = pl.ds(pl.multiple_of(t * 256, 256), 256)
                part = row_dot(dqkv[rows, :], wq_r[...])

                @pl.when(core_j == core)
                def _():
                    pf[rows, :] = part

                @pl.when(core_j != core)
                def _():
                    sd[low_j, rows, :] = part.astype(bf16)

                return c2

            lax.fori_loop(0, size // 256, project, 0)

            @pl.when(core_j != core)
            def _():
                send(sd.at[low_j], rd.at[low_j], (y_s, y_r), low_j, at.partner())

            slot = lax.rem(j, 2)
            for t in range(3):
                cols = slice(t * width, (t + 1) * width)
                gacc[:, cols] += col_dot(hb[block_rows(slot, size), :], dqkv[:, cols])
            for c in range(nc):

                @pl.when(j == min(c + 1, n - 1))
                def _(c=c):
                    p_to_z(c)

            return carry

        lax.fori_loop(0, n, column, 0)
        gqb[...] = gacc[...].astype(bf16)
        for step in range(1, planes):
            other = at.beside(step)
            for s in range(n):
                send(
                    gqb.at[block_rows(s * m + 2 * other, rq, 2)],
                    rqp.at[block_rows((step - 1) * n + s, 2 * rq)],
                    (m_s, m_r), 0, (at.s, 2 * other + core),
                )
        finish_block(jnp.int32(n - 1))
        own_dres.wait()
        fetch_tb.wait()
        if half > 1:
            settle(rzd, e_r.at[0])

        def norm_step(t, carry):
            sum_g, sum_s = carry
            rows = pl.ds(pl.multiple_of(t * 128, 128), 128)
            dh1 = rd[low, rows, :].astype(f32)
            for slot in range(half - 1):
                dh1 = dh1 + rzd[slot, rows, :].astype(f32)
            normed, inv = normalize(tb_v[rows, :].astype(f32))
            grad = gt_r[rows, :] + norm_back(dh1 * sv_r[0:1, :], normed, inv)
            gt_r[rows, :] = grad
            sg[rows, :] = grad.astype(bf16)

            @pl.when(away)
            def _():
                send(sg.at[rows], rg.at[rows], (x_s, x_r), 1, at.swap())

            return (
                sum_g + jnp.sum(dh1 * normed, axis=0, keepdims=True),
                sum_s + jnp.sum(dh1, axis=0, keepdims=True),
            )

        zero = jnp.zeros((1, d), f32)
        sum_g, sum_s = lax.fori_loop(0, size // 128, norm_step, (zero, zero))
        sm[0:1, :] = sum_g
        sm[1:2, :] = sum_s

        for step in range(1, n):
            s = at.along(step)
            send(sm.at[:, block_rows(s, lanes_s)], smz.at[step - 1], (m_s, m_r), 1, (s, at.k))

        settle(rqp, m_r.at[0])

        def add_q(s, carry):
            rows = block_rows(s * m + 2 * at.plane, rq, 2)
            total = gqb[rows, :].astype(f32)
            for step in range(1, planes):
                total = total + rqp[block_rows((step - 1) * n + s, 2 * rq), :].astype(f32)
            gqb[rows, :] = total.astype(bf16)
            return carry

        lax.fori_loop(0, n, add_q, 0)
        for l in range(half):
            row = ((1 - at.team) * half + l) * m + 2 * at.plane
            send(gqb.at[block_rows(row, rq, 2)], rqh.at[block_rows(l, 2 * rq)], (m_s, m_r), 2, at.across())

        settle(smz, m_r.at[1])
        total = sm[:, block_rows(at.s, lanes_s)]
        for step in range(1, n):
            total = total + smz[step - 1]
        small_r[...] = total
        for step in range(1, planes):
            send(small_r, smp.at[step - 1], (m_s, m_r), 3, (at.s, 2 * at.beside(step) + core))

        settle(rqh, m_r.at[2])
        for l in range(half):
            rows = block_rows((at.team * half + l) * m + 2 * at.plane, rq, 2)
            gqb[rows, :] = (
                gqb[rows, :].astype(f32) + rqh[block_rows(l, 2 * rq), :].astype(f32)
            ).astype(bf16)

        def member_rows(r):
            return block_rows((at.team * half + lax.rem(r, half)) * m + 2 * at.plane + r // half, rq)

        for step in range(1, n):
            other = lax.rem(rank + step, n)
            send(gqb.at[member_rows(other)], gq_r.at[rank], (m_s, m_r), 4, at.member(other))
        pltpu.make_async_copy(gqb.at[member_rows(rank)], gq_r.at[rank], loc.at[0]).start()

        for c in range(nc):
            z_to_out(c)

        settle(smp, m_r.at[3])
        settle(smp, m_s.at[3])
        total = small_r[...]
        for step in range(1, planes):
            total = total + smp[step - 1]
        small_r[...] = total
        send(small_r, smc, (m_s, m_r), 5, at.partner())
        settle(smc, m_r.at[5])
        settle(smc, m_s.at[5])
        small_r[...] = small_r[...] + smc[...]

        settle(gq_r.at[pl.ds(0, n - 1)], m_r.at[4])
        settle(gq_r.at[0], loc.at[0])

        @pl.when(away)
        def _():
            settle(rg, x_r.at[1])
            settle(reso_r, x_r.at[0])
            settle(reso_r, x_s.at[0])
            settle(rg, x_s.at[1])

            def widen(t, carry):
                rows = pl.ds(pl.multiple_of(t * 128, 128), 128)
                gt_r[rows, :] = rg[rows, :].astype(f32)
                return carry

            lax.fori_loop(0, size // 128, widen, 0)

        @pl.when(jnp.logical_not(away))
        def _():
            settle(reso_r, loc.at[1])

        settle(do.at[pl.ds(0, (n - 1) * size)], d_s.at[0])
        for c in range(nc):
            settle(rc[c], c_s.at[c])
            settle(rp[c], p_s.at[c])
            settle(rz[c], z_s.at[c])
        for l in range(half):
            settle(rd.at[0], y_s.at[l])
        if half > 1:
            settle(rzd, e_s.at[0])
        settle(rqp, m_s.at[0])
        settle(smz, m_s.at[1])
        settle(rqh, m_s.at[2])
        settle(gq_r.at[pl.ds(0, n - 1)], m_s.at[4])

    def sds(shape, dtype=bf16):
        return jax.ShapeDtypeStruct(shape, dtype)

    def per_chunk(count, dtype=bf16):
        return [pltpu.VMEM((count * c[3], c[5]), dtype) for c in chunks]

    sems = pltpu.SemaphoreType.DMA
    return pl.pallas_call(
        kernel,
        name="attend_back_reduce",
        out_shape=(
            sds((size, d)),
            sds((size, d), f32),
            sds((n, rq, 3 * width)),
            sds((ro, gwo.shape[1]), f32),
            sds((ri, gwi.shape[1]), f32),
            sds((rb, gwb.shape[1]), f32),
            sds((16, lanes_s), f32),
        ),
        in_specs=[HB] * 3 + [VM] * 3 + [HB, VM, HB, VM, HB] + [VM] * 2 + [HB] * 3,
        out_specs=(HB,) + (VM,) * 6,
        scratch_shapes=[
            pltpu.VMEM((length, width), bf16),
            pltpu.VMEM((8, length), f32),
            pltpu.VMEM((length, width), f32),
            pltpu.VMEM((size, width), f32),
            pltpu.VMEM((size, width), f32),
            pltpu.VMEM((size, 3 * width), bf16),
            pltpu.VMEM((d, 3 * width), f32),
            pltpu.VMEM(((planes - 1) * n * 2 * rq, 3 * width), bf16),
            pltpu.VMEM((half * 2 * rq, 3 * width), bf16),
            pltpu.VMEM((size, d), f32),
            pltpu.VMEM((half, size, d), bf16),
            pltpu.VMEM((half, size, d), bf16),
            pltpu.VMEM((max(half - 1, 1), size, d), bf16),
            pltpu.VMEM((size, d), bf16),
            pltpu.VMEM((16, d), f32),
            pltpu.VMEM((n - 1, 16, lanes_s), f32),
            pltpu.VMEM((planes - 1, 16, lanes_s), f32),
            pltpu.VMEM((16, lanes_s), f32),
        ]
        + per_chunk(n * planes)
        + per_chunk(n * planes)
        + per_chunk((planes - 1) * n)
        + per_chunk(n - 1)
        + [
            sems((1,)), sems((1,)),
            sems((2,)), sems((2,)),
            sems((half,)), sems((half,)),
            sems((1,)), sems((1,)),
            sems((nc,)), sems((nc,)),
            sems((nc,)), sems((nc,)),
            sems((nc,)), sems((nc,)),
            sems((6,)), sems((6,)),
            sems((4 + nc,)),
        ],
        compiler_params=pltpu.CompilerParams(
            collective_id=1, has_side_effects=True, vmem_limit_bytes=67043328
        ),
    )(res, dat, dres, q, k, v, o, lse, h1, wq, tb, sv, gsm, gwo, gwi, gwb)


def solution(mesh):
    n, m = mesh.shape["seq"], mesh.shape["shard"]
    nd = n * m

    def per_device(
        tokens, ln1_gain, ln1_bias, w_qkv, bias_query, bias_value, w_out, bias_out,
        ln2_gain, ln2_bias, w_in, bias_in, w_back, bias_back, cotangent,
    ):
        d = tokens.shape[2]
        width = d // n
        index = lax.axis_index("seq") * m + lax.axis_index("shard")
        pack = small_pack(
            index,
            [ln1_gain, ln1_bias, bias_query, bias_value, bias_out, ln2_gain, ln2_bias, bias_back, bias_in],
        )
        rq = w_qkv.shape[0]
        by_rank = w_qkv.reshape(rq, 3, n, width).transpose(2, 0, 1, 3).reshape(n, rq, 3 * width)
        (full_out, full_in, full_back, q, k, v, o, lse, att_tok, h1, wq, tb, cot_b, sv) = forward_call(
            n, m, tokens[0], cotangent[0], by_rank, pack, w_out, w_in, w_back
        )
        per = d // nd
        parts = bias_in.shape[0] // per
        full_bin = sv[8 : 8 + parts].reshape(parts, nd, per).transpose(1, 0, 2).reshape(-1)
        g_two, s_two = sv[5], sv[6]

        x_f = tb.astype(f32)
        resid = x_f + dot(att_tok, full_out) + sv[4]
        normed2, scale2 = normalize(resid)
        h_two = (normed2 * g_two + s_two).astype(bf16)
        pre = dot(h_two, full_in) + full_bin
        act_val, slope = gelu_pair(pre)
        act = act_val.astype(bf16)
        result = (resid + dot(act, full_back) + sv[7]).astype(bf16)
        cot_f = cot_b.astype(f32)
        g_w_back = col_dot(act, cot_b).astype(bf16)
        g_b_back = jnp.sum(cot_f, axis=0)
        d_pre = (row_dot(cot_b, full_back) * slope).astype(bf16)
        g_w_in = col_dot(h_two, d_pre).astype(bf16)
        g_b_in = jnp.sum(d_pre.astype(f32), axis=0)
        d_h2 = row_dot(d_pre, full_in)
        g_g2 = jnp.sum(d_h2 * normed2, axis=0)
        g_s2 = jnp.sum(d_h2, axis=0)
        d_resid = cot_f + norm_back(d_h2 * g_two, normed2, scale2)
        d_resid_b = d_resid.astype(bf16)
        g_w_out = col_dot(att_tok, d_resid_b).astype(bf16)
        g_b_out = jnp.sum(d_resid, axis=0)
        d_att_tok = row_dot(d_resid_b, full_out).astype(bf16)
        bin_rows = g_b_in.reshape(nd, parts, per).transpose(1, 0, 2).reshape(parts, d)
        gsm = jnp.concatenate([jnp.stack([g_b_out, g_g2, g_s2, g_b_back]), bin_rows])

        (own_result, g_tok, gq, go, gi, gb, small) = backward_call(
            n, m, result, d_att_tok, d_resid, q, k, v, o, lse, h1, wq, tb, sv, gsm, g_w_out, g_w_in, g_w_back
        )
        g_qkv = gq.reshape(n, rq, 3, width).transpose(1, 2, 0, 3).reshape(rq, 3 * d).astype(f32)
        mine = lax.dynamic_slice_in_dim(small, lax.axis_index("shard") * per, per, 1)
        return (
            own_result[None], g_tok[None], mine[0], mine[1], g_qkv, mine[2], mine[3], go, mine[4],
            mine[5], mine[6], gi, mine[8 : 8 + parts].reshape(-1), gb, mine[7],
        )

    every = ("seq", "shard")
    whole, vector, matrix = P("shard", "seq", None), P(every), P(every, None)
    return jax.shard_map(
        per_device,
        mesh=mesh,
        in_specs=(
            whole, vector, vector, matrix, vector, vector, matrix, vector, vector, vector, matrix, vector,
            matrix, vector, whole,
        ),
        out_specs=(
            whole, whole, vector, vector, matrix, vector, vector, matrix, vector, vector, vector, matrix,
            vector, matrix, vector,
        ),
        check_vma=False,
    )
```

time: 1250 us -> 461 us (0.37)
  the two profiles are of different devices: /device:TPU:1 before, /device:TPU:17 now
where the time goes in v1:
time: 461 us; the launch traced here: 453 us
  Pallas kernels  361 us (78%)
  matrix products  68.2 us (15%)
  local copies, waits for them, and re-layouts  18.4 us (4%)
    pallas_call x1, Pallas kernels, forward_call(): pl.pallas_call(kernel, name='gather_attend', out_shape=(sds((nd * wo_s.sh...  191 us
    pallas_call x1, Pallas kernels, backward_call(): pl.pallas_call(kernel, name='attend_back_reduce', out_shape=(sds((size, d...  170 us
    dot_general x3, matrix products, dot(): return jnp.dot(a, b, preferred_element_type=f32)  23.2 us
    dot_general x3, matrix products, row_dot(): return lax.dot_general(a, b, NT, preferred_element_type=f32)  22.9 us
    dot_general x3, matrix products, col_dot(): return lax.dot_general(a, b, TN, preferred_element_type=f32)  22 us

profile of v1, /device:TPU:17, one launch (start us, length us, event | category | flops | bytes accessed | tf_op | source)
XLA Modules:
  0.0 452.8 jit_solution(13021917343565925083)
XLA Ops:
  0.6 1.1 reshape.108
  1.8 0.9 reshape.109.wqs_r
  2.7 0.9 slice_bitcast_fusion
  3.6 0.8 stack.19
  5.1 191.1 %gather_attend.1 = (bf16[1024,1024]{1,0:T(8,128)(2,1)}, bf16[1024,4096]{1,0:T(8,128)(2,1)}, bf16[4096,1024]{1,0:T(8,128)(2,1)}, bf16[2048,256]{1,0:T(8,128)(2,1)...) custom-call(bf16[512,1024]{1,0:T(8,128)(2,1)} %bitcast.67, ...), custom_call_target="tpu_custom_call" | custom-call | tf_op jit(solution)/shard_map/gather_attend/pallas_call | solution.py:434
  196.2 0.9 fusion.12
  197.2 3.7 fusion.13
  201.8 7.2 %fusion.10 = f32[512,4096]{1,0:T(8,128)} fusion(bf16[1024,4096]{1,0:T(8,128)(2,1)S(1)} %copy-done.8, f32[512,1024]{1,0:T(8,128)S(1)} %get-tuple-element.81, f32[1024]{0:T(1024)S(1)} %bitcast.80, f32[1024]{0:T(1024)S(1)} %bitcast.74, f32[512]{0:T(512)S(1)} %add_rsqrt_fusion, f32[512]{0:T(512)S(1)} %broadcast_multiply_fusion.2), kind=kOutput, calls=%fused_computation.52 | convolution fusion | flops 4297588736 | bytes 18886656 | tf_op jit(solution)/shard_map/dot_general | solution.py:27
  210.1 12.3 %add_convert_fusion.refs_0_ = bf16[512,1024]{1,0:T(8,128)(2,1)} fusion(f32[512,1024]{1,0:T(8,128)S(1)} %get-tuple-element.81, bf16[4096,1024]{1,0:T(8,128)(2,1)} %get-tuple-element.41, f32[1024]{0:T(1024)S(1)} %bitcast.82, f32[512,4096]{1,0:T(8,128)} %fusion.10, f32[4096]{0:T(1024)S(1)} %add.91), kind=kOutput, calls=%fused_computation.17 | convolution fusion | flops 4317511680 | bytes 19943424 | tf_op jit(solution)/shard_map/dot_general | solution.py:27
  222.4 11.4 %convert_reduce_fusion = (f32[4096]{0:T(1024)S(1)}, bf16[512,4096]{1,0:T(8,128)(2,1)S(1)}) fusion(f32[512,4096]{1,0:T(8,128)S(1)} %copy-done.10, f32[4096]{0:T(1024)S(1)} %add.91, bf16[512,1024]{1,0:T(8,128)(2,1)S(1)} %copy-done.4, bf16[4096,1024]{1,0:T(8,128)(2,1)} %get-tuple-element.41), kind=kOutput, calls=%fused_computation.9 | convolution fusion | flops 4341100544 | bytes 22052864 | tf_op jit(solution)/shard_map/dot_general | solution.py:31
  233.8 9.2 %multiply_reduce_fusion = (f32[1024]{0:T(1024)S(1)}, f32[512]{0:T(512)S(1)}, f32[512]{0:T(512)S(1)}, f32[1024]{0:T(1024)S(1)}, f32[512,1024]{1,0:T(8,128)S(1)}) fusion(f32[512,1024]{1,0:T(8,128)S(1)} %get-tuple-element.81, f32[512]{0:T(512)S(1)} %add_rsqrt_fusion, f32[512]{0:T(512)S(1)} %broadcast_multiply_fusion.2, f32[1024]{0:T(1024)S(1)} %bitcast.75, ...), kind=kOutput, calls=%fused_computation.15 | convolution fusion | flops 4299682816 | bytes 16797696 | tf_op jit(solution)/shard_map/dot_general | solution.py:31
  243.1 2.8 fusion.11
  245.9 2.3 convolution_convert_fusion.3.refs_1_
  249.1 4.0 convolution_convert_fusion.2.refs_13_
  253.1 9.4 %convolution_convert_fusion.1.refs_14_ = bf16[1024,4096]{1,0:T(8,128)(2,1)} fusion(bf16[512,4096]{1,0:T(8,128)(2,1)} %copy-done.11, f32[512,1024]{1,0:T(8,128)S(1)} %copy-done.2, f32[1024]{0:T(1024)S(1)} %bitcast.81, f32[1024]{0:T(1024)S(1)} %bitcast.77, f32[512]{0:T(512)S(1)} %add_rsqrt_fusion, f32[512]{0:T(512)S(1)} %broadcast_multiply_fusion.2), kind=kOutput, calls=%fused_computation.12 | convolution fusion | flops 4301783040 | bytes 14692352 | tf_op jit(solution)/shard_map/dot_general | solution.py:35
  262.5 8.6 %convolution_convert_fusion.refs_15_ = bf16[4096,1024]{1,0:T(8,128)(2,1)} fusion(bf16[512,1024]{1,0:T(8,128)(2,1)S(1)} %copy-done.4, f32[512,4096]{1,0:T(8,128)S(1)} %bitcast.93, f32[4096]{0:T(1024)S(1)} %add.91), kind=kOutput, calls=%fused_computation.11 | convolution fusion | flops 4320133120 | bytes 17842176 | tf_op jit(solution)/shard_map/dot_general | solution.py:35
  271.1 170.0 %attend_back_reduce.1 = (bf16[512,1024]{1,0:T(8,128)(2,1)}, f32[512,1024]{1,0:T(8,128)}, bf16[4,32,768]{2,1,0:T(8,128)(2,1)}, f32[32,1024]{1,0:T(8,128)}, f32[32...) custom-call(bf16[512,1024]{1,0:T(8,128)(2,1)} %add_convert_fusion.refs_0_, ...), custom_call_target="tpu_custom_call" | custom-call | tf_op jit(solution)/shard_map/attend_back_reduce/pallas_call | solution.py:873
  441.1 1.6 dynamic-slice_bitcast_fusion
  442.7 1.1 reshape.123
  444.1 0.9 reshape.122
  446.5 2.3 copy.48
  448.7 1.3 copy.49
  450.7 0.8 copy.51
  451.5 0.8 copy.52
  (53 shorter events, 5.9 us)
Async XLA Ops:
  197.2 4.6 %copy-start.8 = (bf16[1024,4096]{1,0:T(8,128)(2,1)S(1)}, bf16[1024,4096]{1,0:T(8,128)(2,1)}, u32[]{:S(2)}) copy-start(bf16[1024,4096]{1,0:T(8,128)(2,1)} %get-tuple-element.40) | copy-start | bytes 25165828
  200.9 32.9 %copy-start.1 = (f32[512,1024]{1,0:T(8,128)}, f32[512,1024]{1,0:T(8,128)S(1)}, u32[]{:S(2)}) copy-start(f32[512,1024]{1,0:T(8,128)S(1)} %get-tuple-element.81) | copy-start | bytes 6291460
  210.1 12.4 %copy-start.4 = (bf16[512,1024]{1,0:T(8,128)(2,1)S(1)}, bf16[512,1024]{1,0:T(8,128)(2,1)}, u32[]{:S(2)}) copy-start(bf16[512,1024]{1,0:T(8,128)(2,1)} %get-tuple-element.42) | copy-start | bytes 3145732
  210.1 12.3 %copy-start.10 = (f32[512,4096]{1,0:T(8,128)S(1)}, f32[512,4096]{1,0:T(8,128)}, u32[]{:S(2)}) copy-start(f32[512,4096]{1,0:T(8,128)} %fusion.10) | copy-start | bytes 25165828
  233.8 9.3 %copy-start.11 = (bf16[512,4096]{1,0:T(8,128)(2,1)}, bf16[512,4096]{1,0:T(8,128)(2,1)S(1)}, u32[]{:S(2)}) copy-start(bf16[512,4096]{1,0:T(8,128)(2,1)S(1)} %get-tuple-element.84) | copy-start | bytes 12582916
  243.1 2.8 copy-start.9
  245.9 7.2 %copy-start = (f32[512,1024]{1,0:T(8,128)}, f32[512,1024]{1,0:T(8,128)S(1)}, u32[]{:S(2)}) copy-start(f32[512,1024]{1,0:T(8,128)S(1)} %get-tuple-element.62.refs_2_) | copy-start | bytes 6291460
  249.1 4.0 copy-start.2
  249.1 13.4 %slice-start = ((s8[8388608]{0:T(1024)(128)(4,1)}), s8[4194304]{0:T(1024)(128)(4,1)S(1)}, s32[]{:S(2)}) async-start(s8[8388608]{0:T(1024)(128)(4,1)} %bitcast.92), calls=%async_computation | async-start | bytes 8388608
  253.1 9.4 %slice-start.1 = ((s8[8388608]{0:T(1024)(128)(4,1)}), s8[4194304]{0:T(1024)(128)(4,1)S(1)}, s32[]{:S(2)}) async-start(s8[8388608]{0:T(1024)(128)(4,1)} %bitcast.92), calls=%async_computation.1 | async-start | bytes 8388608
  441.1 7.6 %copy-start.3 = (f32[512,1024]{1,0:T(8,128)S(1)}, f32[512,1024]{1,0:T(8,128)}, u32[]{:S(2)}) copy-start(f32[512,1024]{1,0:T(8,128)} %get-tuple-element.51) | copy-start | bytes 6291460
  443.9 6.9 %copy-start.6 = (f32[32,4096]{1,0:T(8,128)S(1)}, f32[32,4096]{1,0:T(8,128)}, u32[]{:S(2)}) copy-start(f32[32,4096]{1,0:T(8,128)} %get-tuple-element.113) | copy-start | bytes 1572868
  444.1 7.4 %copy-start.5 = (f32[128,1024]{1,0:T(8,128)S(1)}, f32[128,1024]{1,0:T(8,128)}, u32[]{:S(2)}) copy-start(f32[128,1024]{1,0:T(8,128)} %get-tuple-element.115) | copy-start | bytes 1572868
  445.1 5.0 %copy-start.7 = (f32[32,1024]{1,0:T(8,128)S(1)}, f32[32,1024]{1,0:T(8,128)}, u32[]{:S(2)}) copy-start(f32[32,1024]{1,0:T(8,128)} %get-tuple-element.109) | copy-start | bytes 393220

commit v2 on v1

v2 whole, which is shorter than its diff:
```python
import math

import jax
import jax.numpy as jnp
from jax import lax
from jax.experimental import pallas as pl
from jax.experimental.pallas import tpu as pltpu
from jax.sharding import PartitionSpec as P

HEAD_DIM = 64
PUMPS = ((('b', 0), ('b', 1)), (('z', 2),), ())
TAIL = (('a', 2), ('b', 2))
LANES = 128
PIECE = 128
MESH = pl.DeviceIdType.MESH
NT = (((1,), (1,)), ((), ()))
TN = (((0,), (0,)), ((), ()))
f32 = jnp.float32
bf16 = jnp.bfloat16

norm_eps = 1e-05
gelu_c = math.sqrt(2.0 / math.pi)
scale = 1.0 / math.sqrt(HEAD_DIM)

VM = pl.BlockSpec(memory_space=pltpu.VMEM)
HB = pl.BlockSpec(memory_space=pl.ANY)


def dot(a, b):
    return jnp.dot(a, b, preferred_element_type=f32)


def row_dot(a, b):
    return lax.dot_general(a, b, NT, preferred_element_type=f32)


def col_dot(a, b):
    return lax.dot_general(a, b, TN, preferred_element_type=f32)


def normalize(values):
    mean_row = jnp.mean(values, axis=-1, keepdims=True)
    centred = values - mean_row
    var_row = jnp.mean(centred * centred, axis=-1, keepdims=True)
    scale_row = lax.rsqrt(var_row + norm_eps)
    return (centred * scale_row, scale_row)


def norm_back(dnormed, normed, scale_row):
    return scale_row * (
        dnormed
        - jnp.mean(dnormed, axis=-1, keepdims=True)
        - normed * jnp.mean(dnormed * normed, axis=-1, keepdims=True)
    )


def gelu_pair(inputs):
    inner = gelu_c * (inputs + 0.044715 * inputs * inputs * inputs)
    tanh_val = jnp.tanh(inner)
    value = 0.5 * inputs * (1.0 + tanh_val)
    slope = 0.5 * (1.0 + tanh_val) + 0.5 * inputs * (1.0 - tanh_val * tanh_val) * gelu_c * (
        1.0 + 3.0 * 0.044715 * inputs * inputs
    )
    return (value, slope)


def block_rows(index, size, count=1):
    return pl.ds(pl.multiple_of(index * size, size), size * count)


def head_lanes(shape, head):
    return lax.broadcasted_iota(jnp.int32, shape, len(shape) - 1) // HEAD_DIM == head


def only_head(values, head):
    return jnp.where(head_lanes(values.shape, head), values, jnp.zeros_like(values))


def spread_heads(columns, rows, width):
    out = None
    for head in range(width // HEAD_DIM):
        one = jnp.broadcast_to(columns[:, head : head + 1], (rows, width))
        out = one if out is None else jnp.where(head_lanes((rows, width), head), one, out)
    return out


class Place:
    def __init__(self, n, m):
        self.n, self.m, self.half, self.planes = n, m, n // 2, m // 2
        self.s, self.k = lax.axis_index("seq"), lax.axis_index("shard")
        self.core, self.plane = lax.rem(self.k, 2), self.k // 2
        self.team, self.low = self.s // self.half, lax.rem(self.s, self.half)
        self.rank = self.low + self.half * self.core
        self.index = self.s * m + self.k
        self.odd = lax.rem(self.low, 2)

    def member(self, rank):
        return (self.team * self.half + lax.rem(rank, self.half), 2 * self.plane + rank // self.half)

    def across(self):
        return (lax.rem(self.s + self.half, self.n), self.k)

    def swap(self):
        return (lax.rem(self.s + self.half, self.n), 2 * self.plane + 1 - self.core)

    def partner(self):
        return (self.s, 2 * self.plane + 1 - self.core)

    def along(self, step):
        return lax.rem(self.s + step, self.n)

    def neighbour(self):
        return (self.team * self.half + self.low + 1 - 2 * lax.rem(self.low, 2), self.k)

    def beside(self, step):
        return lax.rem(self.plane + step, self.planes)

    def near_plane(self):
        return self.plane + 1 - 2 * lax.rem(self.plane, 2)

    def far_plane(self, step):
        return 2 * lax.rem(self.plane // 2 + step, self.planes // 2) + lax.rem(self.plane, 2)

    def greet(self):
        barrier = pltpu.get_barrier_semaphore()
        count = 0

        def signal(device):
            pl.semaphore_signal(barrier, inc=1, device_id=device, device_id_type=MESH)

        for step in range(1, self.n):
            signal((self.along(step), self.k))
            count += 1
        for step in range(self.n):
            signal((self.along(step), 2 * self.plane + 1 - self.core))
            count += 1
        for step in range(1, self.planes):
            signal((self.s, 2 * self.beside(step) + self.core))
            count += 1
        pl.semaphore_wait(barrier, count)


def send(src, dst, sems, at, device):
    pltpu.make_async_remote_copy(
        src_ref=src,
        dst_ref=dst,
        send_sem=sems[0].at[at],
        recv_sem=sems[1].at[at],
        device_id=device,
        device_id_type=MESH,
    ).start()


def settle(view, sem):
    pltpu.make_async_copy(view, view, sem).wait()


def attend_row(i, q_ref, k_ref, v_ref, o_ref, lse_ref, qm, m_s, l_s, acc, size):
    width = q_ref.shape[1]
    heads = width // HEAD_DIM
    rows = block_rows(i, size)
    q = q_ref[rows, :] * jnp.asarray(scale, bf16)
    for h in range(heads):
        qm[h] = only_head(q, h)

    def step(j, diagonal):
        at = block_rows(j, size)
        k = k_ref[at, :]
        v = v_ref[at, :]
        old = m_s[...]
        tops, sums, total = [], [], None
        for h in range(heads):
            s = row_dot(k, qm[h])
            if diagonal:
                k_pos = lax.broadcasted_iota(jnp.int32, (size, size), 0)
                q_pos = lax.broadcasted_iota(jnp.int32, (size, size), 1)
                s = jnp.where(k_pos <= q_pos, s, -1e30)
            top = jnp.max(s, axis=0, keepdims=True)
            if not diagonal:
                top = jnp.maximum(old[h : h + 1], top)
            p = jnp.exp(s - top)
            tops.append(top)
            sums.append(jnp.sum(p, axis=0, keepdims=True))
            part = col_dot(p.astype(bf16), only_head(v, h))
            total = part if total is None else total + part
        rest = [jnp.zeros((8 - heads, size), f32)] if heads < 8 else []
        top = jnp.concatenate(tops + rest, 0)
        add = jnp.concatenate(sums + rest, 0)
        if diagonal:
            l_s[...] = add
            acc[...] = total
        else:
            fade = jnp.exp(old - top)
            l_s[...] = l_s[...] * fade + add
            acc[...] = acc[...] * spread_heads(jnp.transpose(fade), size, width) + total
        m_s[...] = top

    step(i, True)

    def body(j, carry):
        step(j, False)
        return carry

    lax.fori_loop(0, i, body, 0)
    l = l_s[...]
    lse_ref[:, rows] = m_s[...] + jnp.log(l)
    o_ref[rows, :] = (acc[...] * spread_heads(jnp.transpose(1.0 / l), size, width)).astype(bf16)


def forward_call(n, m, tok, cot, wq_s, sm_s, wo_s, wi_s, wb_s):
    size, d = tok.shape
    nd = n * m
    length = n * size
    width = d // n
    half = n // 2
    rq = wq_s.shape[0]
    ff_half = wi_s.shape[1] // 2
    cells = (n, n, half)
    nc = len(cells)

    def kernel(
        tok_r, cot_r, wqs_r, sms_r, wos_r, wis_r, wbs_r,
        wo_r, wi_r, wb_r, q_r, k_r, v_r, o_r, lse_r, att_r, h1_r, wq_r, tb_r, cb_r, sv_r,
        q_v, k_v, v_v, h1_v, wq_v, tokf, sma, qm, m_s, l_s, acc, vec,
        t_send, t_recv, w_send, w_recv, a_send, a_recv, z_send, z_recv,
        lo_send, lo_recv, hi_send, hi_recv, b_send, b_recv, c_send, c_recv, loc,
    ):
        at = Place(n, m)
        planes, rank, core = at.planes, at.rank, at.core
        fulls, shards = (wo_r, wi_r, wb_r), (wos_r, wis_r, wbs_r)
        ts, ws, zs, cs = (t_send, t_recv), (w_send, w_recv), (z_send, z_recv), (c_send, c_recv)
        los, his, bs = (lo_send, lo_recv), (hi_send, hi_recv), (b_send, b_recv)
        rows_p = planes // 2
        near = 2 * at.near_plane() + core
        far = [2 * at.far_plane(step) + core for step in range(1, rows_p)]
        at.greet()
        away = core != at.team

        own = [(at.s, at.plane, core), (at.s, at.plane, core), (at.low, at.plane, core)]
        near_p = at.near_plane()
        far_p = [at.far_plane(step) for step in range(1, rows_p)]

        def half_of(odd):
            return wis_r.at[:, pl.ds(pl.multiple_of(odd * ff_half, ff_half), ff_half)]

        def start_z(c):
            dst = fulls[c].at[own[c]]
            if c < 2:
                for step in range(1, n):
                    s = at.along(step)
                    src = shards[c] if c == 0 else half_of(lax.rem(lax.rem(s, half), 2))
                    send(src, dst, zs, c, (s, at.k))
                src = shards[c] if c == 0 else half_of(at.odd)
                pltpu.make_async_copy(src, dst, loc.at[4 + c]).start()
                return
            for team in range(2):
                for pair in range(half // 2):
                    s = team * half + 2 * pair + at.team

                    @pl.when(s != at.s)
                    def _(s=s):
                        send(shards[c], dst, zs, c, (s, at.k))

            @pl.when(at.odd == at.team)
            def _():
                pltpu.make_async_copy(shards[c], dst, loc.at[4 + c]).start()

        def settle_z(c, sem):
            if c < 2:
                settle(fulls[c].at[pl.ds(0, n - 1), 0, 0], sem.at[c])
                return

            @pl.when(at.odd == at.team)
            def _():
                settle(fulls[c].at[pl.ds(0, half - 1), 0, 0], sem.at[c])

            @pl.when(at.odd != at.team)
            def _():
                settle(fulls[c].at[pl.ds(0, half), 0, 0], sem.at[c])

        def z_to_a(c):
            if c < 2:
                settle(fulls[c].at[own[c]], loc.at[4 + c])
            else:

                @pl.when(at.odd == at.team)
                def _():
                    settle(fulls[c].at[own[c]], loc.at[4 + c])

            settle_z(c, z_recv)
            part = fulls[c].at[:, at.plane, core]
            send(part, part, los, c, (at.s, near))
            for there in far:
                send(part, part, his, c, (at.s, there))

        def settle_far(c, sem):
            if far:
                settle(fulls[c].at[:, pl.ds(0, len(far)), 0], sem.at[c])

        def a_to_b(c):
            first = cells[c] // 2
            settle(fulls[c].at[:, 0, 0], lo_recv.at[c])
            part = fulls[c].at[pl.ds(0, first), near_p, core]
            for there in far:
                send(part, part, bs, c, (at.s, there))
            settle_far(c, hi_recv)
            for p in far_p:
                part = fulls[c].at[pl.ds(first, cells[c] - first), p, core]
                send(part, part, bs, c, (at.s, near))

        def b_to_c(c):
            settle_far(c, b_recv)
            part = fulls[c].at[:, :, core]
            send(part, part, cs, c, at.partner())

        def of_rank(r, part):
            return wqs_r.at[:, pl.ds(pl.multiple_of(part * d + r * width, width), width)]

        def to_part(part):
            return wq_v.at[block_rows(at.index, rq), pl.ds(part * width, width)]

        for part in range(3):
            pltpu.make_async_copy(of_rank(rank, part), to_part(part), loc.at[0]).start()
        own_s = pltpu.make_async_copy(sms_r, sma.at[at.index], loc.at[1])
        own_s.start()
        for step in range(1, n):
            other = lax.rem(rank + step, n)
            for part in range(3):
                send(of_rank(other, part), to_part(part), ws, 0, at.member(other))
            send(sms_r, sma.at[at.index], ws, 1, at.member(other))
        settle(wq_v.at[pl.ds(0, rq)], loc.at[0])
        own_s.wait()
        settle(wq_v.at[pl.ds(0, (n - 1) * rq)], w_recv.at[0])
        settle(sma.at[pl.ds(0, n - 1)], w_recv.at[1])
        for low in range(half):
            row = (at.team * half + low) * m + 2 * at.plane
            send(wq_v.at[block_rows(row, rq, 2)], wq_v.at[block_rows(row, rq, 2)], ws, 2, at.across())
            send(sma.at[pl.ds(row, 2)], sma.at[pl.ds(row, 2)], ws, 3, at.across())
        start_z(0)
        start_z(1)

        @pl.when(jnp.logical_not(away))
        def _():
            pltpu.make_async_copy(tok_r, tokf.at[rank], loc.at[2]).start()

        settle(wq_v.at[pl.ds(0, half * 2 * rq)], w_recv.at[2])
        settle(sma.at[pl.ds(0, half * 2)], w_recv.at[3])
        @pl.when(away)
        def _():
            send(tok_r, tokf.at[at.low + half * (1 - core)], ts, 0, at.swap())

        for step in range(1, planes):
            there = (at.s, 2 * at.beside(step) + core)
            for other in range(n):
                row = other * m + 2 * at.plane
                send(wq_v.at[block_rows(row, rq, 2)], wq_v.at[block_rows(row, rq, 2)], ws, 4, there)
                send(sma.at[pl.ds(row, 2)], sma.at[pl.ds(row, 2)], ws, 5, there)
        z_to_a(0)

        @pl.when(away)
        def _():
            settle(tokf.at[0], t_recv.at[0])

        @pl.when(jnp.logical_not(away))
        def _():
            settle(tokf.at[0], loc.at[2])

        for step in range(1, half):
            low = lax.rem(at.low + step, half)
            send(tokf.at[rank], tokf.at[rank], ts, 1, (at.team * half + low, at.k))
        send(tokf.at[rank], tokf.at[rank], ts, 2, at.partner())

        settle(wq_v.at[pl.ds(0, (planes - 1) * n * 2 * rq)], w_recv.at[4])
        settle(sma.at[pl.ds(0, (planes - 1) * n * 2)], w_recv.at[5])
        per = LANES // (d // nd)
        for group in range(d // LANES):
            total = sma[group * per].astype(f32)
            for other in range(1, per):
                total = total + sma[group * per + other].astype(f32)
            sv_r[:, group * LANES : (group + 1) * LANES] = total
            vec[0, group : group + 1, :] = total[2:3]
            vec[1, group : group + 1, :] = total[3:4]

        def norm_block(b):
            def body(t, carry):
                part = pl.ds(pl.multiple_of(t * 128, 128), 128)
                x = tokf[b, part, :].astype(f32)
                normed, _ = normalize(x)
                h1_v[pl.ds(pl.multiple_of(b * size + t * 128, 128), 128), :] = (
                    normed * sv_r[0:1, :] + sv_r[1:2, :]
                ).astype(bf16)
                return carry

            lax.fori_loop(0, size // 128, body, 0)

        groups = width // LANES
        bias_q = jnp.concatenate([vec[0, pl.ds(rank * groups + g, 1), :] for g in range(groups)], 1)
        bias_v = jnp.concatenate([vec[1, pl.ds(rank * groups + g, 1), :] for g in range(groups)], 1)

        def project_block(b):
            def body(t, carry):
                part = pl.ds(pl.multiple_of(b * size + t * 256, 256), 256)
                h = h1_v[part, :]
                q_v[part, :] = (dot(h, wq_v[:, 0:width]) + bias_q).astype(bf16)
                k_v[part, :] = dot(h, wq_v[:, width : 2 * width]).astype(bf16)
                v_v[part, :] = (dot(h, wq_v[:, 2 * width : 3 * width]) + bias_v).astype(bf16)
                return carry

            lax.fori_loop(0, size // 256, body, 0)

        def later_z():
            start_z(2)

            @pl.when(away)
            def _():
                send(cot_r, cb_r, ts, 4, at.swap())

            @pl.when(jnp.logical_not(away))
            def _():
                pltpu.make_async_copy(cot_r, cb_r, loc.at[3]).start()

        def take(t, carry):
            @pl.when(t == 1)
            def _():
                z_to_a(1)
                settle(tokf.at[0], t_recv.at[2])
                a_to_b(0)

            if half > 1:

                @pl.when(t == 2)
                def _():
                    a_to_b(1)
                    settle(tokf.at[pl.ds(0, half - 1)], t_recv.at[1])
                    for step in range(1, half):
                        b = lax.rem(at.low + step, half) + half * core
                        send(tokf.at[b], tokf.at[b], ts, 3, at.partner())

                @pl.when(t == 1 + half)
                def _():
                    settle(tokf.at[pl.ds(0, half - 1)], t_recv.at[3])
                    later_z()

            step = jnp.where(t < 2, 0, lax.rem(t - 2, max(half - 1, 1)) + 1)
            other_core = jnp.where(t < 2, t, (t - 2) // max(half - 1, 1))
            side = core + other_core - 2 * core * other_core
            b = lax.rem(at.low + step, half) + half * side
            norm_block(b)
            project_block(b)
            return carry

        lax.fori_loop(0, n, take, 0)
        beside = rank + 1 - 2 * lax.rem(rank, 2)
        leaving = [
            (tokf.at[rank], tb_r.at[0]), (tokf.at[beside], tb_r.at[1]),
            (q_v, q_r), (k_v, k_r), (v_v, v_r), (h1_v, h1_r), (wq_v, wq_r),
        ]
        for i, (src, dst) in enumerate(leaving):
            pltpu.make_async_copy(src, dst, loc.at[4 + nc + i]).start()

        pumps = PUMPS

        def row(i, carry):
            attend_row(i, q_v, k_v, v_v, o_r, lse_r, qm, m_s, l_s, acc, size)
            src = o_r.at[block_rows(i, size)]
            for which, owner in ((0, i), (1, i + 1 - 2 * lax.rem(i, 2))):
                dst = att_r.at[which, :, block_rows(rank, width)]

                @pl.when(owner != rank)
                def _(dst=dst, which=which, owner=owner):
                    send(src, dst, (a_send, a_recv), which, at.member(owner))

                @pl.when(owner == rank)
                def _(dst=dst, which=which):
                    pltpu.make_async_copy(src, dst, loc.at[which]).start()

            for when, todo in enumerate(pumps):

                @pl.when(i == n - len(pumps) + when)
                def _(todo=todo):
                    for what, c in todo:
                        {"z": z_to_a, "a": a_to_b, "b": b_to_c}[what](c)

            return carry

        lax.fori_loop(0, n, row, 0)
        for what, c in TAIL:
            {"z": z_to_a, "a": a_to_b, "b": b_to_c}[what](c)
        others = att_r.at[0, :, pl.ds(0, (n - 1) * width)]
        for which in range(2):
            settle(att_r.at[0, :, pl.ds(0, width)], loc.at[which])
            settle(others, a_recv.at[which])
        for i, (src, dst) in enumerate(leaving):
            settle(src, loc.at[4 + nc + i])
        for c in range(nc):
            settle(fulls[c].at[:, :, 0], c_recv.at[c])

        for which in range(2):
            settle(others, a_send.at[which])
        for c in range(nc):
            settle_z(c, z_send)
            settle(fulls[c].at[:, 0, 0], lo_send.at[c])
            settle_far(c, hi_send)
            settle_far(c, b_send)
            settle(fulls[c].at[:, :, 0], c_send.at[c])
        for at_sem, count in ((0, n - 1), (2, half * 2), (4, (planes - 1) * n * 2)):
            settle(wq_v.at[pl.ds(0, count * rq)], w_send.at[at_sem])
            settle(sma.at[pl.ds(0, count)], w_send.at[at_sem + 1])

        @pl.when(away)
        def _():
            settle(tokf.at[0], t_send.at[0])
            settle(cb_r, t_recv.at[4])
            settle(cb_r, t_send.at[4])

        @pl.when(jnp.logical_not(away))
        def _():
            settle(cb_r, loc.at[3])

        settle(tokf.at[0], t_send.at[2])
        if half > 1:
            settle(tokf.at[pl.ds(0, half - 1)], t_send.at[1])
            settle(tokf.at[pl.ds(0, half - 1)], t_send.at[3])

    def sds(shape, dtype=bf16):
        return jax.ShapeDtypeStruct(shape, dtype)

    sems = pltpu.SemaphoreType.DMA
    return pl.pallas_call(
        kernel,
        name="gather_attend",
        out_shape=(
            sds((n, m // 2, 2, *wo_s.shape)),
            sds((n, m // 2, 2, wi_s.shape[0], ff_half)),
            sds((half, m // 2, 2, *wb_s.shape)),
            sds((length, width)), sds((length, width)), sds((length, width)), sds((length, width)),
            sds((8, length), f32),
            sds((2, size, d)),
            sds((length, d)),
            sds((d, 3 * width)),
            sds((2, size, d)), sds((size, d)),
            sds((16, d), f32),
        ),
        in_specs=[HB] * 7,
        out_specs=(HB,) * 6 + (VM,) * 3 + (HB,) * 3 + (VM,) * 2,
        scratch_shapes=[
            pltpu.VMEM((length, width), bf16),
            pltpu.VMEM((length, width), bf16),
            pltpu.VMEM((length, width), bf16),
            pltpu.VMEM((length, d), bf16),
            pltpu.VMEM((d, 3 * width), bf16),
            pltpu.VMEM((n, size, d), bf16),
            pltpu.VMEM((nd, 16, LANES), bf16),
            pltpu.VMEM((width // HEAD_DIM, size, width), bf16),
            pltpu.VMEM((8, size), f32),
            pltpu.VMEM((8, size), f32),
            pltpu.VMEM((size, width), f32),
            pltpu.VMEM((2, max(8, d // LANES), LANES), f32),
            sems((6,)), sems((6,)),
            sems((6,)), sems((6,)),
            sems((2,)), sems((2,)),
            sems((nc,)), sems((nc,)),
            sems((nc,)), sems((nc,)),
            sems((nc,)), sems((nc,)),
            sems((nc,)), sems((nc,)),
            sems((nc,)), sems((nc,)),
            sems((11 + nc,)),
        ],
        compiler_params=pltpu.CompilerParams(
            collective_id=0, has_side_effects=True, vmem_limit_bytes=62 << 20
        ),
        cost_estimate=pl.CostEstimate(
            flops=6 * length * d * width + 2 * length * length * d // n, bytes_accessed=80 << 20, transcendentals=0
        ),
    )(tok, cot, wq_s, sm_s, wo_s, wi_s, wb_s)


def small_pack(index, vectors):
    per = vectors[0].shape[0]
    rows = [part for v in vectors for part in v.reshape(-1, per)]
    rows = jnp.stack(rows + [jnp.zeros_like(rows[0])] * (16 - len(rows)))
    lane = lax.broadcasted_iota(jnp.int32, (16, LANES), 1)
    spread = jnp.tile(rows, (1, LANES // per))
    return jnp.where(lane // per == lax.rem(index, LANES // per), spread, jnp.zeros_like(spread))


def backward_call(n, m, res, dat, dres, q, k, v, o, lse, h1, wq, tb, sv, gsm, gwo, gwi, gwb):
    size, d = dat.shape
    nd = n * m
    length = n * size
    width = d // n
    heads = width // HEAD_DIM
    half, planes = n // 2, m // 2
    rq = d // nd
    quarter = gwi.shape[4] // 2
    parts = [
        (half, *gwb.shape[3:]), (n, gwi.shape[3], quarter), (n, gwi.shape[3], quarter), (n, *gwo.shape[3:]),
    ]
    cells = [p[0] for p in parts]
    nc = len(cells)
    lanes_s = d // n

    def kernel(*refs):
        (res_r, dat_r, dres_r, q_h, k_h, v_h, o_r, lse_r, h1_r, wq_h, tb_r, sv_r, gsm_r, gwo_r, gwi_r, gwb_r) = refs[:16]
        (reso_r, gt_r, gq_r, go_r, gi_r, gb_r, small_r) = refs[16:23]
        (do, delta, dqa, dka, dva, dqkv, gacc, rqp, rqh, pf, sd, rd, rzd, rg, sm, smz, smp, smc) = refs[23:41]
        gqb, hb, sg, tb_v, o_v, q_r, k_r, v_r, wq_r = refs[41:50]
        rest = refs[50:]
        ga, rc, rp, rz = (rest[i * nc : (i + 1) * nc] for i in range(4))
        (d_s, d_r, x_s, x_r, y_s, y_r, e_s, e_r, c_s, c_r, p_s, p_r, z_s, z_r, m_s, m_r, yl_s, yl_r, el_s, el_r, loc) = rest[4 * nc :]
        at = Place(n, m)
        rank, core, low = at.rank, at.core, at.low
        left, right = (gwi_r.at[:, :, :, :, pl.ds(p * quarter, quarter)] for p in range(2))
        grads = (gwb_r, left, right, gwo_r)
        at.greet()
        away = core != at.team

        for step in range(1, n):
            other = lax.rem(rank + step, n)
            send(dat_r.at[:, block_rows(other, width)], do.at[block_rows(rank, size)], (d_s, d_r), 0, at.member(other))
        own_do = pltpu.make_async_copy(dat_r.at[:, block_rows(rank, width)], do.at[block_rows(rank, size)], loc.at[0])
        own_do.start()

        for c in range(nc):
            send(grads[c].at[:, :, 1 - core], rc[c], (c_s, c_r), c, at.partner())
            pltpu.make_async_copy(grads[c].at[:, :, core], ga[c], loc.at[6 + c]).start()
        fetch_tb = pltpu.make_async_copy(tb_r, tb_v, loc.at[4])
        fetch_tb.start()
        for i in range(n):
            pltpu.make_async_copy(o_r.at[pl.ds(i * size, size)], o_v.at[:, pl.ds(i * width, width)], loc.at[5]).start()

        arriving = [(q_h, q_r), (k_h, k_r), (v_h, v_r), (wq_h, wq_r)]
        for i, (src, dst) in enumerate(arriving):
            pltpu.make_async_copy(src, dst, loc.at[6 + nc + i]).start()

        own_dres = pltpu.make_async_copy(dres_r, gt_r, loc.at[2])
        own_dres.start()

        def fetch_h1(b):
            return pltpu.make_async_copy(h1_r.at[block_rows(b, size)], hb.at[block_rows(lax.rem(b, 2), size)], loc.at[3])

        def c_to_p(c):
            settle(ga[c], loc.at[6 + c])
            settle(rc[c], c_r.at[c])

            def add(t, carry):
                s, p = t // planes, lax.rem(t, planes)
                ga[c][s, p] = (ga[c][s, p].astype(f32) + rc[c][s, p].astype(f32)).astype(bf16)
                return carry

            lax.fori_loop(0, cells[c] * planes, add, 0)
            for step in range(1, planes):
                other = at.beside(step)
                send(ga[c].at[:, other], rp[c].at[step - 1], (p_s, p_r), c, (at.s, 2 * other + core))

        def p_to_z(c):
            settle(rp[c], p_r.at[c])

            def add(s, carry):
                total = ga[c][s, at.plane].astype(f32)
                for step in range(1, planes):
                    total = total + rp[c][step - 1, s].astype(f32)
                ga[c][s, at.plane] = total.astype(bf16)
                return carry

            lax.fori_loop(0, cells[c], add, 0)
            if c > 0:
                for step in range(1, n):
                    s = at.along(step)
                    send(ga[c].at[s, at.plane], rz[c].at[at.s], (z_s, z_r), c, (s, at.k))
                rz[c][at.s] = ga[c][at.s, at.plane]
                return
            source = at.team * (half // 2) + at.low // 2
            for place in range(half):
                s = at.odd * half + place

                @pl.when(s != at.s)
                def _(s=s, place=place):
                    send(ga[c].at[place, at.plane], rz[c].at[source], (z_s, z_r), c, (s, at.k))

                @pl.when(s == at.s)
                def _(place=place):
                    rz[c][source] = ga[c][place, at.plane]

        def settle_z(c, sem):
            if c > 0:
                settle(rz[c].at[pl.ds(0, n - 1)], sem.at[c])
                return

            @pl.when(at.odd == at.team)
            def _():
                settle(rz[c].at[pl.ds(0, half - 1)], sem.at[c])

            @pl.when(at.odd != at.team)
            def _():
                settle(rz[c].at[pl.ds(0, half)], sem.at[c])

        def z_to_out(c):
            settle_z(c, z_r)

            def total(sources):
                out = rz[c][sources[0]].astype(f32)
                for s in sources[1:]:
                    out = out + rz[c][s].astype(f32)
                return out

            if c == 0:
                gb_r[...] = total(range(half))
            elif c < 3:
                for odd in range(2):
                    first = (2 * odd + c - 1) * quarter
                    gi_r[:, first : first + quarter] = total([s for s in range(n) if s % half % 2 == odd])
            else:
                go_r[...] = total(range(n))

        for c in range(nc):
            c_to_p(c)
        fetch_h1(0).start()

        own_do.wait()
        settle(do.at[pl.ds(0, (n - 1) * size)], d_r.at[0])
        for i, (src, dst) in enumerate(arriving):
            settle(dst, loc.at[6 + nc + i])

        @pl.when(away)
        def _():
            send(res_r, reso_r, (x_s, x_r), 0, at.swap())

        @pl.when(jnp.logical_not(away))
        def _():
            pltpu.make_async_copy(res_r, reso_r, loc.at[1]).start()

        settle(o_v.at[:, pl.ds(0, n * width)], loc.at[5])
        pick = (
            lax.broadcasted_iota(jnp.int32, (8, width), 1) // HEAD_DIM
            == lax.broadcasted_iota(jnp.int32, (8, width), 0)
        ).astype(f32)

        def prepare(i, carry):
            rows = block_rows(i, size)
            product = do[rows, :].astype(f32) * o_v[:, block_rows(i, width)].astype(f32)
            delta[:, rows] = lax.dot_general(
                pick, product, NT, preferred_element_type=f32, precision=lax.Precision.HIGHEST
            )
            dqa[rows, :] = jnp.zeros((size, width), f32)
            return carry

        lax.fori_loop(0, n, prepare, 0)
        gacc[...] = jnp.zeros_like(gacc)
        sm[...] = jnp.zeros_like(sm)
        sm[4:12, :] = gsm_r[...]

        def pair(i, j, diagonal):
            rows, at_k = block_rows(i, size), block_rows(j, size)
            kk, vv = k_r[at_k, :], v_r[at_k, :]
            qs, dd = q_r[rows, :] * jnp.asarray(scale, bf16), do[rows, :]
            dq = dk = dv = None
            for h in range(heads):
                qh, dh_, kh = only_head(qs, h), only_head(dd, h), only_head(kk, h)
                p = jnp.exp(row_dot(kk, qh) - lse_r[h : h + 1, rows])
                if diagonal:
                    k_pos = lax.broadcasted_iota(jnp.int32, (size, size), 0)
                    q_pos = lax.broadcasted_iota(jnp.int32, (size, size), 1)
                    p = jnp.where(k_pos <= q_pos, p, 0.0)
                dp = row_dot(vv, dh_)
                ds = (p * (dp - delta[h : h + 1, rows])).astype(bf16)
                one, two, three = dot(p.astype(bf16), dh_), dot(ds, qh), col_dot(ds, kh)
                dv = one if dv is None else dv + one
                dk = two if dk is None else dk + two
                dq = three if dq is None else dq + three
            dva[...] += dv
            dka[...] += dk
            dqa[rows, :] += dq

        def owner(j):
            return j // half, lax.rem(j, half)

        def finish_block(j):
            core_j, low_j = owner(j)

            @pl.when(core_j == core)
            def _():
                settle(rd.at[0], y_r.at[low_j])

                def add(t, carry):
                    rows = pl.ds(pl.multiple_of(t * 128, 128), 128)
                    rd[low_j, rows, :] = (pf[rows, :] + rd[low_j, rows, :].astype(f32)).astype(bf16)
                    return carry

                lax.fori_loop(0, size // 128, add, 0)

                @pl.when(low_j != low)
                def _():
                    slot = lax.rem(low_j - low + half, half) - 1
                    send(rd.at[low_j], rzd.at[slot], (e_s, e_r), 0, (at.team * half + low_j, at.k))

        def column(j, carry):
            fetch_h1(j).wait()

            @pl.when(j + 1 < n)
            def _():
                fetch_h1(j + 1).start()

            dka[...] = jnp.zeros_like(dka)
            dva[...] = jnp.zeros_like(dva)
            pair(j, j, True)

            def inner(i, c2):
                pair(i, j, False)
                return c2

            lax.fori_loop(j + 1, n, inner, 0)
            dqb = (dqa[block_rows(j, size), :] * scale).astype(bf16)
            dkb, dvb = dka[...].astype(bf16), dva[...].astype(bf16)
            dqkv[:, 0:width] = dqb
            dqkv[:, width : 2 * width] = dkb
            dqkv[:, 2 * width : 3 * width] = dvb
            mine = block_rows(rank, width)
            sm[2:3, mine] += jnp.sum(dqb.astype(f32), axis=0, keepdims=True)
            sm[3:4, mine] += jnp.sum(dvb.astype(f32), axis=0, keepdims=True)

            @pl.when(j > 0)
            def _():
                finish_block(j - 1)

            core_j, low_j = owner(j)

            def project(t, c2):
                rows = pl.ds(pl.multiple_of(t * PIECE, PIECE), PIECE)
                part = row_dot(dqkv[rows, :], wq_r[...])

                @pl.when(core_j == core)
                def _():
                    pf[rows, :] = part

                @pl.when(core_j != core)
                def _():
                    sd[low_j, rows, :] = part.astype(bf16)

                    @pl.when(j == n - 1)
                    def _():
                        send(sd.at[low_j, rows], rd.at[low_j, rows], (yl_s, yl_r), t, at.partner())

                return c2

            lax.fori_loop(0, size // PIECE, project, 0)

            @pl.when(jnp.logical_and(core_j != core, j < n - 1))
            def _():
                send(sd.at[low_j], rd.at[low_j], (y_s, y_r), low_j, at.partner())

            slot = lax.rem(j, 2)
            for t in range(3):
                cols = slice(t * width, (t + 1) * width)
                gacc[:, cols] += col_dot(hb[block_rows(slot, size), :], dqkv[:, cols])
            for c in range(nc - 1):

                @pl.when(j == min(c, n - 2))
                def _(c=c):
                    p_to_z(c)

            return carry

        lax.fori_loop(0, n, column, 0)
        gqb[...] = gacc[...].astype(bf16)
        for step in range(1, planes):
            other = at.beside(step)
            for s in range(n):
                send(
                    gqb.at[block_rows(s * m + 2 * other, rq, 2)],
                    rqp.at[block_rows((step - 1) * n + s, 2 * rq)],
                    (m_s, m_r), 0, (at.s, 2 * other + core),
                )
        pieces = size // PIECE
        last = half - 1
        owner_last = (at.team * half + last, at.k)

        def pair_piece(rows):
            rd[last, rows, :] = (pf[rows, :] + rd[last, rows, :].astype(f32)).astype(bf16)

        @pl.when(jnp.logical_and(core == 1, low != last))
        def _():
            def pass_on(t, carry):
                rows = pl.ds(pl.multiple_of(t * PIECE, PIECE), PIECE)
                settle(rd.at[last, rows], yl_r.at[t])
                pair_piece(rows)
                send(rd.at[last, rows], rzd.at[last - low - 1, rows], (el_s, el_r), t, owner_last)
                return carry

            lax.fori_loop(0, pieces, pass_on, 0)

        own_dres.wait()
        fetch_tb.wait()
        if half > 1:

            @pl.when(rank != n - 1)
            def _():
                settle(rzd, e_r.at[0])

        def norm_step(t, carry):
            sum_g, sum_s = carry
            rows = pl.ds(pl.multiple_of(t * PIECE, PIECE), PIECE)

            @pl.when(rank == n - 1)
            def _():
                settle(rd.at[last, rows], yl_r.at[t])
                pair_piece(rows)
                if half > 1:
                    settle(rzd.at[:, rows], el_r.at[t])

            dh1 = rd[low, rows, :].astype(f32)
            for slot in range(half - 1):
                dh1 = dh1 + rzd[slot, rows, :].astype(f32)
            normed, inv = normalize(tb_v[rows, :].astype(f32))
            grad = gt_r[rows, :] + norm_back(dh1 * sv_r[0:1, :], normed, inv)
            gt_r[rows, :] = grad
            sg[rows, :] = grad.astype(bf16)

            @pl.when(away)
            def _():
                send(sg.at[rows], rg.at[rows], (x_s, x_r), 1, at.swap())

            return (
                sum_g + jnp.sum(dh1 * normed, axis=0, keepdims=True),
                sum_s + jnp.sum(dh1, axis=0, keepdims=True),
            )

        zero = jnp.zeros((1, d), f32)
        sum_g, sum_s = lax.fori_loop(0, pieces, norm_step, (zero, zero))
        sm[0:1, :] = sum_g
        sm[1:2, :] = sum_s

        settle(rqp, m_r.at[0])

        def add_q(s, carry):
            rows = block_rows(s * m + 2 * at.plane, rq, 2)
            total = gqb[rows, :].astype(f32)
            for step in range(1, planes):
                total = total + rqp[block_rows((step - 1) * n + s, 2 * rq), :].astype(f32)
            gqb[rows, :] = total.astype(bf16)
            return carry

        lax.fori_loop(0, n, add_q, 0)
        for l in range(half):
            row = ((1 - at.team) * half + l) * m + 2 * at.plane
            send(gqb.at[block_rows(row, rq, 2)], rqh.at[block_rows(l, 2 * rq)], (m_s, m_r), 2, at.across())

        p_to_z(nc - 1)
        send(sm, smc, (m_s, m_r), 1, at.partner())
        settle(rqh, m_r.at[2])
        for l in range(half):
            rows = block_rows((at.team * half + l) * m + 2 * at.plane, rq, 2)
            gqb[rows, :] = (
                gqb[rows, :].astype(f32) + rqh[block_rows(l, 2 * rq), :].astype(f32)
            ).astype(bf16)

        def member_rows(r):
            return block_rows((at.team * half + lax.rem(r, half)) * m + 2 * at.plane + r // half, rq)

        for step in range(1, n):
            other = lax.rem(rank + step, n)
            send(gqb.at[member_rows(other)], gq_r.at[rank], (m_s, m_r), 4, at.member(other))
        pltpu.make_async_copy(gqb.at[member_rows(rank)], gq_r.at[rank], loc.at[0]).start()

        settle(smc, m_r.at[1])
        settle(smc, m_s.at[1])
        sm[...] = sm[...] + smc[...]
        for step in range(1, planes):
            send(sm, smp.at[step - 1], (m_s, m_r), 3, (at.s, 2 * at.beside(step) + core))
        for c in range(nc):
            z_to_out(c)
        settle(smp, m_r.at[3])
        settle(smp, m_s.at[3])
        total = sm[...]
        for step in range(1, planes):
            total = total + smp[step - 1]
        sm[...] = total
        for step in range(1, n):
            s = at.along(step)
            send(sm.at[:, block_rows(s, lanes_s)], smz.at[step - 1], (m_s, m_r), 5, (s, at.k))
        settle(smz, m_r.at[5])
        total = sm[:, block_rows(at.s, lanes_s)]
        for step in range(1, n):
            total = total + smz[step - 1]
        small_r[...] = total

        settle(gq_r.at[pl.ds(0, n - 1)], m_r.at[4])
        settle(gq_r.at[0], loc.at[0])

        @pl.when(away)
        def _():
            settle(rg, x_r.at[1])
            settle(rg, x_s.at[1])
            settle(reso_r, x_r.at[0])
            settle(reso_r, x_s.at[0])

            def widen(t, carry):
                rows = pl.ds(pl.multiple_of(t * 128, 128), 128)
                gt_r[rows, :] = rg[rows, :].astype(f32)
                return carry

            lax.fori_loop(0, size // 128, widen, 0)

        @pl.when(jnp.logical_not(away))
        def _():
            settle(reso_r, loc.at[1])

        settle(do.at[pl.ds(0, (n - 1) * size)], d_s.at[0])
        for c in range(nc):
            settle(rc[c], c_s.at[c])
            settle(rp[c], p_s.at[c])
            settle_z(c, z_s)
        for l in range(half - 1):
            settle(rd.at[0], y_s.at[l])

        @pl.when(core == 1)
        def _():
            settle(rd.at[0], y_s.at[last])

        @pl.when(core == 0)
        def _():
            for t in range(pieces):
                settle(rd.at[0, pl.ds(0, PIECE)], yl_s.at[t])

        passes = jnp.logical_and(core == 1, low != last)

        @pl.when(passes)
        def _():
            for t in range(pieces):
                settle(rd.at[0, pl.ds(0, PIECE)], el_s.at[t])

        if half > 2:

            @pl.when(passes)
            def _():
                settle(rzd.at[pl.ds(0, half - 2)], e_s.at[0])

        if half > 1:

            @pl.when(jnp.logical_not(passes))
            def _():
                settle(rzd, e_s.at[0])

        settle(rqp, m_s.at[0])
        settle(smz, m_s.at[5])
        settle(rqh, m_s.at[2])
        settle(gq_r.at[pl.ds(0, n - 1)], m_s.at[4])

    def sds(shape, dtype=bf16):
        return jax.ShapeDtypeStruct(shape, dtype)

    sems = pltpu.SemaphoreType.DMA
    return pl.pallas_call(
        kernel,
        name="attend_back_reduce",
        out_shape=(
            sds((size, d)),
            sds((size, d), f32),
            sds((n, rq, 3 * width)),
            sds(gwo.shape[3:], f32),
            sds((gwi.shape[3], 2 * gwi.shape[4]), f32),
            sds(gwb.shape[3:], f32),
            sds((16, lanes_s), f32),
        ),
        in_specs=[HB] * 7 + [VM, HB, HB, HB] + [VM] * 2 + [HB] * 3,
        out_specs=(HB,) + (VM,) * 6,
        scratch_shapes=[
            pltpu.VMEM((length, width), bf16),
            pltpu.VMEM((8, length), f32),
            pltpu.VMEM((length, width), f32),
            pltpu.VMEM((size, width), f32),
            pltpu.VMEM((size, width), f32),
            pltpu.VMEM((size, 3 * width), bf16),
            pltpu.VMEM((d, 3 * width), f32),
            pltpu.VMEM(((planes - 1) * n * 2 * rq, 3 * width), bf16),
            pltpu.VMEM((half * 2 * rq, 3 * width), bf16),
            pltpu.VMEM((size, d), f32),
            pltpu.VMEM((half, size, d), bf16),
            pltpu.VMEM((half, size, d), bf16),
            pltpu.VMEM((max(half - 1, 1), size, d), bf16),
            pltpu.VMEM((size, d), bf16),
            pltpu.VMEM((16, d), f32),
            pltpu.VMEM((n - 1, 16, lanes_s), f32),
            pltpu.VMEM((planes - 1, 16, d), f32),
            pltpu.VMEM((16, d), f32),
        ]
        + [
            pltpu.VMEM((d, 3 * width), bf16),
            pltpu.VMEM((2 * size, d), bf16),
            pltpu.VMEM((size, d), bf16),
            pltpu.VMEM((size, d), bf16),
            pltpu.VMEM((size, d), bf16),
            pltpu.VMEM((length, width), bf16),
            pltpu.VMEM((length, width), bf16),
            pltpu.VMEM((length, width), bf16),
            pltpu.VMEM((d, 3 * width), bf16),
        ]
        + [pltpu.VMEM((count, planes, rows, cols), bf16) for count, rows, cols in parts] * 2
        + [pltpu.VMEM((planes - 1, *part), bf16) for part in parts]
        + [pltpu.VMEM(part, bf16) for part in parts]
        + [
            sems((1,)), sems((1,)),
            sems((2,)), sems((2,)),
            sems((half,)), sems((half,)),
            sems((1,)), sems((1,)),
            sems((nc,)), sems((nc,)),
            sems((nc,)), sems((nc,)),
            sems((nc,)), sems((nc,)),
            sems((6,)), sems((6,)),
            sems((size // PIECE,)), sems((size // PIECE,)),
            sems((size // PIECE,)), sems((size // PIECE,)),
            sems((10 + nc,)),
        ],
        compiler_params=pltpu.CompilerParams(
            collective_id=1, has_side_effects=True, vmem_limit_bytes=67043328
        ),
        cost_estimate=pl.CostEstimate(
            flops=12 * length * d * width + 5 * length * length * d // n, bytes_accessed=80 << 20, transcendentals=0
        ),
    )(res, dat, dres, q, k, v, o, lse, h1, wq, tb, sv, gsm, gwo, gwi, gwb)


def solution(mesh):
    n, m = mesh.shape["seq"], mesh.shape["shard"]
    nd = n * m
    every = ("seq", "shard")

    def per_device(
        tokens, ln1_gain, ln1_bias, w_qkv, bias_query, bias_value, w_out, bias_out,
        ln2_gain, ln2_bias, w_in, bias_in, w_back, bias_back, cotangent,
    ):
        d = tokens.shape[2]
        width = d // n
        index = lax.axis_index("seq") * m + lax.axis_index("shard")
        pack = small_pack(
            index,
            [ln1_gain, ln1_bias, bias_query, bias_value, bias_out, ln2_gain, ln2_bias, bias_back, bias_in],
        )
        rq = w_qkv.shape[0]
        ff = w_in.shape[1]
        rq = w_qkv.shape[0]
        (full_out, full_in, full_back, q, k, v, o, lse, att_two, h1, wq, tb, cot_own, sv) = forward_call(
            n, m, tokens[0], cotangent[0], w_qkv, pack, w_out, w_in, w_back
        )
        full_out = full_out.reshape(d, d)
        half_in = full_in.reshape(d, ff // 2)
        half_back = full_back.reshape(ff // 2, d)
        odd = lax.rem(lax.rem(lax.axis_index("seq"), n // 2), 2)
        per = d // nd
        parts = bias_in.shape[0] // per
        half_bin = lax.dynamic_slice_in_dim(sv[8 : 8 + parts], odd * (d // 2), d // 2, 1)
        half_bin = half_bin.reshape(parts, nd // 2, per).transpose(1, 0, 2).reshape(-1)
        g_two, s_two = sv[5], sv[6]

        def to_neighbour(values):
            pairs = []
            for s in range(n):
                there = s // 2 * 2 + 1 - s % 2
                pairs += [(s * m + k, there * m + k) for k in range(m)]
            return lax.ppermute(values.astype(bf16), every, pairs).astype(f32)

        size = tokens.shape[1]
        cot_two = jnp.concatenate([cot_own, to_neighbour(cot_own).astype(bf16)])
        x_f = tb.reshape(2 * size, d).astype(f32)
        att_two = att_two.reshape(2 * size, d)
        resid = x_f + dot(att_two, full_out) + sv[4]
        normed2, scale2 = normalize(resid)
        h_two = (normed2 * g_two + s_two).astype(bf16)
        pre = dot(h_two, half_in) + half_bin
        act = gelu_pair(pre)[0].astype(bf16)
        out_part = dot(act, half_back)
        leaves = out_part[size:].astype(bf16)
        others_out = to_neighbour(leaves)
        pre, leaves = lax.optimization_barrier((pre, leaves))
        d_pre = (row_dot(cot_two, half_back) * gelu_pair(pre)[1]).astype(bf16)
        g_b_in = jnp.sum(d_pre.astype(f32), axis=0)
        d_h2_part = row_dot(d_pre, half_in)
        leaves = d_h2_part[size:].astype(bf16)
        others_d = to_neighbour(leaves)
        pre, d_pre, leaves = lax.optimization_barrier((pre, d_pre, leaves))
        g_w_back = col_dot(gelu_pair(pre)[0].astype(bf16), cot_two).astype(bf16)
        g_w_in = col_dot(h_two, d_pre).astype(bf16)

        resid, normed2, scale2 = resid[:size], normed2[:size], scale2[:size]
        att_tok, cot_f = att_two[:size], cot_two[:size].astype(f32)
        result = (resid + out_part[:size] + others_out + sv[7]).astype(bf16)
        g_b_back = jnp.sum(cot_f, axis=0)
        d_h2 = d_h2_part[:size] + others_d
        g_g2 = jnp.sum(d_h2 * normed2, axis=0)
        g_s2 = jnp.sum(d_h2, axis=0)
        d_resid = cot_f + norm_back(d_h2 * g_two, normed2, scale2)
        d_resid_b = d_resid.astype(bf16)
        g_w_out = col_dot(att_tok, d_resid_b).astype(bf16)
        g_b_out = jnp.sum(d_resid, axis=0)
        d_att_tok = row_dot(d_resid_b, full_out).astype(bf16)
        bin_rows = g_b_in.reshape(nd // 2, parts, per).transpose(1, 0, 2).reshape(parts, d // 2)
        bin_rows = jnp.where(
            lax.broadcasted_iota(jnp.int32, (parts, d), 1) // (d // 2) == odd, jnp.tile(bin_rows, (1, 2)), 0.0
        )
        gsm = jnp.concatenate([jnp.stack([g_b_out, g_g2, g_s2, g_b_back]), bin_rows])

        (own_result, g_tok, gq, go, gi, gb, small) = backward_call(
            n, m, result, d_att_tok, d_resid, q, k, v, o, lse, h1, wq, tb[0], sv, gsm,
            g_w_out.reshape(n, m // 2, 2, d // nd, d),
            g_w_in.reshape(n, m // 2, 2, d // nd, ff // 2),
            g_w_back.reshape(n // 2, m // 2, 2, ff // nd, d),
        )
        g_qkv = gq.reshape(n, rq, 3, width).transpose(1, 2, 0, 3).reshape(rq, 3 * d).astype(f32)
        mine = lax.dynamic_slice_in_dim(small, lax.axis_index("shard") * per, per, 1)
        return (
            own_result[None], g_tok[None], mine[0], mine[1], g_qkv, mine[2], mine[3], go, mine[4],
            mine[5], mine[6], gi, mine[8 : 8 + parts].reshape(-1), gb, mine[7],
        )

    whole, vector, matrix = P("shard", "seq", None), P(every), P(every, None)
    return jax.shard_map(
        per_device,
        mesh=mesh,
        in_specs=(
            whole, vector, vector, matrix, vector, vector, matrix, vector, vector, vector, matrix, vector,
            matrix, vector, whole,
        ),
        out_specs=(
            whole, whole, vector, vector, matrix, vector, vector, matrix, vector, vector, vector, matrix,
            vector, matrix, vector,
        ),
        check_vma=False,
    )
```

time: 461 us -> 347 us (0.75)
  the two profiles are of different devices: /device:TPU:17 before, /device:TPU:1 now
where the time goes in v2:
time: 347 us; the launch traced here: 342 us
  Pallas kernels  247 us (71%)
  matrix products  55.2 us (16%)
  local copies, waits for them, and re-layouts  28.3 us (8%)
  other arithmetic  6.48 us (2%)
    pallas_call x1, Pallas kernels, backward_call(): pl.pallas_call(kernel, name='attend_back_reduce', out_shape=(sds((size, d...  127 us
    pallas_call x1, Pallas kernels, forward_call(): pl.pallas_call(kernel, name='gather_attend', out_shape=(sds((n, m // 2, 2...  120 us
    dot_general x3, matrix products, col_dot(): return lax.dot_general(a, b, TN, preferred_element_type=f32)  21.3 us
    dot_general x3, matrix products, row_dot(): return lax.dot_general(a, b, NT, preferred_element_type=f32)  19 us
    dot_general x3, matrix products, dot(): return jnp.dot(a, b, preferred_element_type=f32)  14.9 us
    unnamed x58, local copies, waits for them, and re-layouts  14.5 us
  transfers between devices with their start and end apart: 3, of which 1 were waited for; matrix products, arithmetic and copies ran while one was open for 18% of the time, Pallas kernels for 0%

profile of v2, /device:TPU:1, one launch (start us, length us, event | category | flops | bytes accessed | tf_op | source)
XLA Modules:
  0.0 342.1 jit_solution(15415331811292600407)
XLA Ops:
  3.1 119.5 %gather_attend.1 = (bf16[4,4,2,32,1024]{4,3,2,1,0:T(8,128)(2,1)}, bf16[4,4,2,32,2048]{4,3,2,1,0:T(8,128)(2,1)}, bf16[2,4,2,128,1024]{4,3,2,1,0:T(8,128)(2,1)}, b...) custom-call(bf16[512,1024]{1,0:T(8,128)(2,1)} %bitcast.102, ...), custom_call_target="tpu_custom_call" | custom-call | flops 5368709120 | bytes 83886080 | tf_op jit(solution)/shard_map/gather_attend/pallas_call | solution.py:529
  122.6 1.4 collective-permute-start.1
  124.8 1.0 fusion.51
  126.0 5.3 %fusion.52 = (f32[1024]{0:T(1024)S(1)}, f32[1024,1024]{1,0:T(8,128)S(1)}) fusion(f32[1024]{0:T(1024)S(1)} %bitcast.93, bf16[1024,1024]{1,0:T(8,128)(2,1)} %bitcast.110, bf16[1024,1024]{1,0:T(8,128)(2,1)} %bitcast.111, bf16[2,512,1024]{2,1,0:T(8,128)(2,1)} %get-tuple-element.39), kind=kOutput, calls=%fused_computation.102 | convolution fusion | flops 2151676928 | bytes 10493952 | tf_op jit(solution)/shard_map/dot_general | solution.py:30
  133.3 3.1 copy-done.16
  136.4 4.5 %broadcast_add_fusion = f32[1024,2048]{1,0:T(8,128)S(1)} fusion(f32[2048]{0:T(1024)S(1)} %add.119, bf16[1024,2048]{1,0:T(8,128)(2,1)S(1)} %bitcast.104, f32[1024,1024]{1,0:T(8,128)S(1)} %subtract_multiply_fusion, f32[1024]{0:T(1024)S(1)} %bitcast.91, f32[1024]{0:T(1024)S(1)} %bitcast.82), kind=kOutput, calls=%fused_computation.29 | convolution fusion | flops 4300210176 | bytes 16793600 | tf_op jit(solution)/shard_map/dot_general | solution.py:30
  140.9 5.1 %fusion.24 = f32[1024,1024]{1,0:T(8,128)S(1)} fusion(bf16[2048,1024]{1,0:T(8,128)(2,1)S(1)} %bitcast.106, f32[1024,2048]{1,0:T(8,128)S(1)} %broadcast_add_fusion), kind=kOutput, calls=%fused_computation.32 | convolution fusion | flops 4313841664 | bytes 16777216 | tf_op jit(solution)/shard_map/dot_general | solution.py:30
  146.1 1.9 copy-done.7
  148.4 2.4 slice_bitcast_fusion.refs_10_
  150.9 12.1 %convert_reduce_fusion = (f32[2048]{0:T(1024)S(1)}, bf16[1024,2048]{1,0:T(8,128)(2,1)S(1)}) fusion(f32[1024,2048]{1,0:T(8,128)} %copy-done.22, bf16[1024,1024]{1,0:T(8,128)(2,1)S(1)} %constant_dynamic-update-slice_fusion, bf16[2048,1024]{1,0:T(8,128)(2,1)S(1)} %bitcast.107), kind=kOutput, calls=%fused_computation.21 | convolution fusion | flops 4339005440 | bytes 18882560 | tf_op jit(solution)/shard_map/dot_general | solution.py:34
  163.1 4.5 %fusion.53 = f32[1024,1024]{1,0:T(8,128)S(1)} fusion(bf16[1024,2048]{1,0:T(8,128)(2,1)S(1)} %get-tuple-element.54, bf16[1024,2048]{1,0:T(8,128)(2,1)S(1)} %bitcast.105), kind=kOutput, calls=%fused_computation.103 | convolution fusion | flops 4294967296 | bytes 12582912 | tf_op jit(solution)/shard_map/dot_general | solution.py:34
  167.7 1.9 copy-done.4
  169.6 1.1 slice.138
  170.8 1.4 collective-permute-start.2
  172.4 12.0 %fusion.26 = bf16[2048,1024]{1,0:T(8,128)(2,1)} fusion(bf16[1024,1024]{1,0:T(8,128)(2,1)} %copy-done.11, f32[1024,2048]{1,0:T(8,128)} %copy-done.22), kind=kOutput, calls=%fused_computation.34 | convolution fusion | flops 4315938816 | bytes 14680064 | tf_op jit(solution)/shard_map/dot_general | solution.py:38
  184.4 3.0 fusion.31.refs_0_
  187.4 6.7 %convolution_convert_fusion = bf16[1024,2048]{1,0:T(8,128)(2,1)} fusion(bf16[1024,2048]{1,0:T(8,128)(2,1)S(1)} %copy-done.24, f32[1024,1024]{1,0:T(8,128)S(1)} %copy-done.3, f32[1024]{0:T(1024)S(1)} %bitcast.92, f32[1024]{0:T(1024)S(1)} %bitcast.83), kind=kOutput, calls=%fused_computation.35 | convolution fusion | flops 4300210176 | bytes 12591104 | tf_op jit(solution)/shard_map/dot_general | solution.py:38
  197.5 2.3 convolution_convert_fusion.2.refs_1_
  199.8 2.6 convolution_convert_fusion.1
  203.1 127.5 %attend_back_reduce.1 = (bf16[512,1024]{1,0:T(8,128)(2,1)}, f32[512,1024]{1,0:T(8,128)}, bf16[4,32,768]{2,1,0:T(8,128)(2,1)}, f32[32,1024]{1,0:T(8,128)}, f32[32...) custom-call(bf16[512,1024]{1,0:T(8,128)(2,1)} %fusion.31.refs_0_, ...), custom_call_target="tpu_custom_call" | custom-call | flops 11811160064 | bytes 83886080 | tf_op jit(solution)/shard_map/attend_back_reduce/pallas_call | solution.py:1053
  330.6 1.3 reshape.163
  334.5 1.6 dynamic-slice_bitcast_fusion
  336.1 2.3 copy.45
  338.3 1.3 copy.46
  (93 shorter events, 14.9 us)
Async XLA Ops:
  122.6 28.2 %collective-permute-start.1 = (bf16[512,1024]{1,0:T(8,128)(2,1)}, bf16[512,1024]{1,0:T(8,128)(2,1)S(1)}, u32[]{:S(2)}, u32[]{:S(2)}) collective-permute-start(bf16[512,1024]{1,0:T(8,128)(2,1)} %get-tuple-element.45), channel_id=1, source_target_pairs={{0,8},{1,9},{2,10},{3,11},{4,12},{5,13},{6,14},{7,15},{8,0},{9,1},... | collective-permute-start | bytes 3145736 | tf_op jit(solution)/shard_map/ppermute | solution.py:1160
  131.9 16.4 %copy-start.15 = (f32[1024]{0:T(1024)}, f32[1024]{0:T(1024)S(1)}, u32[]{:S(2)}) copy-start(f32[1024]{0:T(1024)S(1)} %add_rsqrt_fusion) | copy-start | bytes 12292
  131.9 4.5 %copy-start.16 = (bf16[4,4,2,32,2048]{4,3,2,1,0:T(8,128)(2,1)S(1)}, bf16[4,4,2,32,2048]{4,3,2,1,0:T(8,128)(2,1)}, u32[]{:S(2)}) copy-start(bf16[4,4,2,32,2048]{4,3,2,1,0:T(8,128)(2,1)} %get-tuple-element.43) | copy-start | bytes 12582916
  133.3 7.6 %copy-start.2 = (f32[1024,1024]{1,0:T(8,128)}, f32[1024,1024]{1,0:T(8,128)S(1)}, u32[]{:S(2)}) copy-start(f32[1024,1024]{1,0:T(8,128)S(1)} %subtract_multiply_fusion) | copy-start | bytes 12582916
  136.4 4.6 %copy-start.18 = (bf16[2,4,2,128,1024]{4,3,2,1,0:T(8,128)(2,1)S(1)}, bf16[2,4,2,128,1024]{4,3,2,1,0:T(8,128)(2,1)}, u32[]{:S(2)}) copy-start(bf16[2,4,2,128,1024]{4,3,2,1,0:T(8,128)(2,1)} %get-tuple-element.44) | copy-start | bytes 12582916
  140.9 5.1 %copy-start.22 = (f32[1024,2048]{1,0:T(8,128)}, f32[1024,2048]{1,0:T(8,128)S(1)}, u32[]{:S(2)}) copy-start(f32[1024,2048]{1,0:T(8,128)S(1)} %broadcast_add_fusion) | copy-start | bytes 25165828
  140.9 7.4 %copy-start.6 = (bf16[512,1024]{1,0:T(8,128)(2,1)S(1)}, bf16[512,1024]{1,0:T(8,128)(2,1)}, u32[]{:S(2)}) copy-start(bf16[512,1024]{1,0:T(8,128)(2,1)} %get-tuple-element.45) | copy-start | bytes 3145732
  148.1 36.2 %collective-permute-start = (bf16[512,1024]{1,0:T(8,128)(2,1)S(1)}, bf16[512,1024]{1,0:T(8,128)(2,1)}, u32[]{:S(2)}, u32[]{:S(2)}) collective-permute-start(bf16[512,1024]{1,0:T(8,128)(2,1)S(1)} %slice.139), channel_id=1, source_target_pairs={{0,8},{1,9},{2,10},{3,11},{4,12},{5,13},{6,14},{7,15},{8,0},{9,1},... | collective-permute-start | bytes 3145736 | tf_op jit(solution)/shard_map/ppermute | solution.py:1160
  148.3 2.6 copy-start.19
  150.9 12.2 %copy-start.11 = (bf16[1024,1024]{1,0:T(8,128)(2,1)}, bf16[1024,1024]{1,0:T(8,128)(2,1)S(1)}, u32[]{:S(2)}) copy-start(bf16[1024,1024]{1,0:T(8,128)(2,1)S(1)} %constant_dynamic-update-slice_fusion) | copy-start | bytes 6291460
  150.9 12.2 %copy-start.17 = (bf16[4,4,2,32,2048]{4,3,2,1,0:T(8,128)(2,1)S(1)}, bf16[4,4,2,32,2048]{4,3,2,1,0:T(8,128)(2,1)}, u32[]{:S(2)}) copy-start(bf16[4,4,2,32,2048]{4,3,2,1,0:T(8,128)(2,1)} %get-tuple-element.43) | copy-start | bytes 12582916
  163.1 4.6 %copy-start.23 = (bf16[1024,2048]{1,0:T(8,128)(2,1)}, bf16[1024,2048]{1,0:T(8,128)(2,1)S(1)}, u32[]{:S(2)}) copy-start(bf16[1024,2048]{1,0:T(8,128)(2,1)S(1)} %get-tuple-element.54) | copy-start | bytes 12582916
  170.8 24.3 %collective-permute-start.2 = (bf16[512,1024]{1,0:T(8,128)(2,1)}, bf16[512,1024]{1,0:T(8,128)(2,1)S(1)}, u32[]{:S(2)}, u32[]{:S(2)}) collective-permute-start(bf16[512,1024]{1,0:T(8,128)(2,1)} %slice.138), channel_id=1, source_target_pairs={{0,8},{1,9},{2,10},{3,11},{4,12},{5,13},{6,14},{7,15},{8,0},{9,1},... | collective-permute-start | bytes 3145736 | tf_op jit(solution)/shard_map/ppermute | solution.py:1160
  172.3 12.0 %copy-start.1 = (f32[1024,1024]{1,0:T(8,128)S(1)}, f32[1024,1024]{1,0:T(8,128)}, u32[]{:S(2)}) copy-start(f32[1024,1024]{1,0:T(8,128)} %copy-done) | copy-start | bytes 12582916
  172.4 12.0 %copy-start.8 = (f32[1024,1024]{1,0:T(8,128)S(1)}, f32[1024,1024]{1,0:T(8,128)}, u32[]{:S(2)}) copy-start(f32[1024,1024]{1,0:T(8,128)} %copy-done.7) | copy-start | bytes 12582916
  172.4 15.0 %copy-start.24 = (bf16[1024,2048]{1,0:T(8,128)(2,1)S(1)}, bf16[1024,2048]{1,0:T(8,128)(2,1)}, u32[]{:S(2)}) copy-start(bf16[1024,2048]{1,0:T(8,128)(2,1)} %copy-done.23) | copy-start | bytes 12582916
  184.3 3.1 copy-start.3
  187.4 7.6 %copy-start.5 = (f32[1024,1024]{1,0:T(8,128)S(1)}, f32[1024,1024]{1,0:T(8,128)}, u32[]{:S(2)}) copy-start(f32[1024,1024]{1,0:T(8,128)} %copy-done.4) | copy-start | bytes 12582916
  196.9 5.6 %copy-start.9 = (f32[512,1024]{1,0:T(8,128)}, f32[512,1024]{1,0:T(8,128)S(1)}, u32[]{:S(2)}) copy-start(f32[512,1024]{1,0:T(8,128)S(1)} %get-tuple-element.68.refs_2_) | copy-start | bytes 6291460
  196.9 2.9 copy-start.20
  330.6 7.8 %copy-start.10 = (f32[512,1024]{1,0:T(8,128)S(1)}, f32[512,1024]{1,0:T(8,128)}, u32[]{:S(2)}) copy-start(f32[512,1024]{1,0:T(8,128)} %get-tuple-element.57) | copy-start | bytes 6291460
  331.9 8.4 %copy-start.13 = (f32[32,4096]{1,0:T(8,128)S(1)}, f32[32,4096]{1,0:T(8,128)}, u32[]{:S(2)}) copy-start(f32[32,4096]{1,0:T(8,128)} %get-tuple-element.120) | copy-start | bytes 1572868
  332.2 9.0 %copy-start.12 = (f32[128,1024]{1,0:T(8,128)S(1)}, f32[128,1024]{1,0:T(8,128)}, u32[]{:S(2)}) copy-start(f32[128,1024]{1,0:T(8,128)} %get-tuple-element.122) | copy-start | bytes 1572868
  333.1 6.6 %copy-start.14 = (f32[32,1024]{1,0:T(8,128)S(1)}, f32[32,1024]{1,0:T(8,128)}, u32[]{:S(2)}) copy-start(f32[32,1024]{1,0:T(8,128)} %get-tuple-element.116) | copy-start | bytes 393220
  (5 other events, 9.3 us)

commit v3 on v2

--- a/solution.py
+++ b/solution.py
@@ -345,9 +345,13 @@
 
         settle(wq_v.at[pl.ds(0, half * 2 * rq)], w_recv.at[2])
         settle(sma.at[pl.ds(0, half * 2)], w_recv.at[3])
+        def cut(block, h):
+            return block.at[pl.ds(h * (size // 2), size // 2)]
+
         @pl.when(away)
         def _():
-            send(tok_r, tokf.at[at.low + half * (1 - core)], ts, 0, at.swap())
+            for h in range(2):
+                send(cut(tok_r, h), cut(tokf.at[at.low + half * (1 - core)], h), ts, h, at.swap())
 
         for step in range(1, planes):
             there = (at.s, 2 * at.beside(step) + core)
@@ -357,18 +361,22 @@
                 send(sma.at[pl.ds(row, 2)], sma.at[pl.ds(row, 2)], ws, 5, there)
         z_to_a(0)
 
-        @pl.when(away)
-        def _():
-            settle(tokf.at[0], t_recv.at[0])
-
         @pl.when(jnp.logical_not(away))
         def _():
             settle(tokf.at[0], loc.at[2])
 
-        for step in range(1, half):
-            low = lax.rem(at.low + step, half)
-            send(tokf.at[rank], tokf.at[rank], ts, 1, (at.team * half + low, at.k))
-        send(tokf.at[rank], tokf.at[rank], ts, 2, at.partner())
+        def own_half(h):
+            @pl.when(away)
+            def _():
+                settle(cut(tokf.at[0], h), t_recv.at[h])
+
+            part = cut(tokf.at[rank], h)
+            for step in range(1, half):
+                low = lax.rem(at.low + step, half)
+                send(part, part, ts, 2 + h, (at.team * half + low, at.k))
+            send(part, part, ts, 4, at.partner())
+
+        own_half(0)
 
         settle(wq_v.at[pl.ds(0, (planes - 1) * n * 2 * rq)], w_recv.at[4])
         settle(sma.at[pl.ds(0, (planes - 1) * n * 2)], w_recv.at[5])
@@ -413,17 +421,19 @@
 
             @pl.when(away)
             def _():
-                send(cot_r, cb_r, ts, 4, at.swap())
+                send(cot_r, cb_r, ts, 6, at.swap())
 
             @pl.when(jnp.logical_not(away))
             def _():
                 pltpu.make_async_copy(cot_r, cb_r, loc.at[3]).start()
+
+        own_half(1)
 
         def take(t, carry):
             @pl.when(t == 1)
             def _():
                 z_to_a(1)
-                settle(tokf.at[0], t_recv.at[2])
+                settle(tokf.at[0], t_recv.at[4])
                 a_to_b(0)
 
             if half > 1:
@@ -431,14 +441,15 @@
                 @pl.when(t == 2)
                 def _():
                     a_to_b(1)
-                    settle(tokf.at[pl.ds(0, half - 1)], t_recv.at[1])
-                    for step in range(1, half):
-                        b = lax.rem(at.low + step, half) + half * core
-                        send(tokf.at[b], tokf.at[b], ts, 3, at.partner())
+                    for h in range(2):
+                        settle(tokf.at[pl.ds(0, half - 1), pl.ds(0, size // 2)], t_recv.at[2 + h])
+                        for step in range(1, half):
+                            part = cut(tokf.at[lax.rem(at.low + step, half) + half * core], h)
+                            send(part, part, ts, 5, at.partner())
 
                 @pl.when(t == 1 + half)
                 def _():
-                    settle(tokf.at[pl.ds(0, half - 1)], t_recv.at[3])
+                    settle(tokf.at[pl.ds(0, half - 1)], t_recv.at[5])
                     later_z()
 
             step = jnp.where(t < 2, 0, lax.rem(t - 2, max(half - 1, 1)) + 1)
@@ -509,18 +520,20 @@
 
         @pl.when(away)
         def _():
-            settle(tokf.at[0], t_send.at[0])
-            settle(cb_r, t_recv.at[4])
-            settle(cb_r, t_send.at[4])
+            for h in range(2):
+                settle(cut(tokf.at[0], h), t_send.at[h])
+            settle(cb_r, t_recv.at[6])
+            settle(cb_r, t_send.at[6])
 
         @pl.when(jnp.logical_not(away))
         def _():
             settle(cb_r, loc.at[3])
 
-        settle(tokf.at[0], t_send.at[2])
+        settle(tokf.at[0], t_send.at[4])
         if half > 1:
-            settle(tokf.at[pl.ds(0, half - 1)], t_send.at[1])
-            settle(tokf.at[pl.ds(0, half - 1)], t_send.at[3])
+            for h in range(2):
+                settle(tokf.at[pl.ds(0, half - 1), pl.ds(0, size // 2)], t_send.at[2 + h])
+            settle(tokf.at[pl.ds(0, half - 1)], t_send.at[5])
 
     def sds(shape, dtype=bf16):
         return jax.ShapeDtypeStruct(shape, dtype)
@@ -556,7 +569,7 @@
             pltpu.VMEM((8, size), f32),
             pltpu.VMEM((size, width), f32),
             pltpu.VMEM((2, max(8, d // LANES), LANES), f32),
-            sems((6,)), sems((6,)),
+            sems((7,)), sems((7,)),
             sems((6,)), sems((6,)),
             sems((2,)), sems((2,)),
             sems((nc,)), sems((nc,)),
@@ -602,10 +615,10 @@
 
     def kernel(*refs):
         (res_r, dat_r, dres_r, q_h, k_h, v_h, o_r, lse_r, h1_r, wq_h, tb_r, sv_r, gsm_r, gwo_r, gwi_r, gwb_r) = refs[:16]
-        (reso_r, gt_r, gq_r, go_r, gi_r, gb_r, small_r) = refs[16:23]
-        (do, delta, dqa, dka, dva, dqkv, gacc, rqp, rqh, pf, sd, rd, rzd, rg, sm, smz, smp, smc) = refs[23:41]
-        gqb, hb, sg, tb_v, o_v, q_r, k_r, v_r, wq_r = refs[41:50]
-        rest = refs[50:]
+        (reso_r, gt_r, rg, gqo_r, go_r, gi_r, gb_r, small_r) = refs[16:24]
+        (do, delta, dqa, dka, dva, dqkv, gacc, rqp, rqh, pf, sd, rd, rzd, sm, smz, smp, smc) = refs[24:41]
+        gqb, hb, sg, tb_v, o_v, q_r, k_r, v_r, wq_r, gq_r = refs[41:51]
+        rest = refs[51:]
         ga, rc, rp, rz = (rest[i * nc : (i + 1) * nc] for i in range(4))
         (d_s, d_r, x_s, x_r, y_s, y_r, e_s, e_r, c_s, c_r, p_s, p_r, z_s, z_r, m_s, m_r, yl_s, yl_r, el_s, el_r, loc) = rest[4 * nc :]
         at = Place(n, m)
@@ -624,7 +637,7 @@
         for c in range(nc):
             send(grads[c].at[:, :, 1 - core], rc[c], (c_s, c_r), c, at.partner())
             pltpu.make_async_copy(grads[c].at[:, :, core], ga[c], loc.at[6 + c]).start()
-        fetch_tb = pltpu.make_async_copy(tb_r, tb_v, loc.at[4])
+        fetch_tb = pltpu.make_async_copy(tb_r.at[0], tb_v, loc.at[4])
         fetch_tb.start()
         for i in range(n):
             pltpu.make_async_copy(o_r.at[pl.ds(i * size, size)], o_v.at[:, pl.ds(i * width, width)], loc.at[5]).start()
@@ -986,6 +999,10 @@
 
         settle(gq_r.at[pl.ds(0, n - 1)], m_r.at[4])
         settle(gq_r.at[0], loc.at[0])
+        for r in range(n):
+            for part in range(3):
+                first = part * d + r * width
+                gqo_r[:, first : first + width] = gq_r[r, :, part * width : (part + 1) * width].astype(f32)
 
         @pl.when(away)
         def _():
@@ -993,13 +1010,6 @@
             settle(rg, x_s.at[1])
             settle(reso_r, x_r.at[0])
             settle(reso_r, x_s.at[0])
-
-            def widen(t, carry):
-                rows = pl.ds(pl.multiple_of(t * 128, 128), 128)
-                gt_r[rows, :] = rg[rows, :].astype(f32)
-                return carry
-
-            lax.fori_loop(0, size // 128, widen, 0)
 
         @pl.when(jnp.logical_not(away))
         def _():
@@ -1056,14 +1066,15 @@
         out_shape=(
             sds((size, d)),
             sds((size, d), f32),
-            sds((n, rq, 3 * width)),
+            sds((size, d)),
+            sds((rq, 3 * d), f32),
             sds(gwo.shape[3:], f32),
             sds((gwi.shape[3], 2 * gwi.shape[4]), f32),
             sds(gwb.shape[3:], f32),
             sds((16, lanes_s), f32),
         ),
         in_specs=[HB] * 7 + [VM, HB, HB, HB] + [VM] * 2 + [HB] * 3,
-        out_specs=(HB,) + (VM,) * 6,
+        out_specs=(HB, VM, HB) + (VM,) * 5,
         scratch_shapes=[
             pltpu.VMEM((length, width), bf16),
             pltpu.VMEM((8, length), f32),
@@ -1078,7 +1089,6 @@
             pltpu.VMEM((half, size, d), bf16),
             pltpu.VMEM((half, size, d), bf16),
             pltpu.VMEM((max(half - 1, 1), size, d), bf16),
-            pltpu.VMEM((size, d), bf16),
             pltpu.VMEM((16, d), f32),
             pltpu.VMEM((n - 1, 16, lanes_s), f32),
             pltpu.VMEM((planes - 1, 16, d), f32),
@@ -1094,6 +1104,7 @@
             pltpu.VMEM((length, width), bf16),
             pltpu.VMEM((length, width), bf16),
             pltpu.VMEM((d, 3 * width), bf16),
+            pltpu.VMEM((n, rq, 3 * width), bf16),
         ]
         + [pltpu.VMEM((count, planes, rows, cols), bf16) for count, rows, cols in parts] * 2
         + [pltpu.VMEM((planes - 1, *part), bf16) for part in parts]
@@ -1118,6 +1129,172 @@
             flops=12 * length * d * width + 5 * length * length * d // n, bytes_accessed=80 << 20, transcendentals=0
         ),
     )(res, dat, dres, q, k, v, o, lse, h1, wq, tb, sv, gsm, gwo, gwi, gwb)
+
+
+def hidden_forward_call(att, tokens, wo, wi, wb, sv, bias):
+    size, d = att.shape[1:]
+    rows, hidden = 2 * size, wi.shape[1]
+    some, columns = 512, hidden // 4
+    blocks = size // some
+
+    def kernel(
+        att_h, tok_h, wo_h, wi_h, wb_h, sv_r, bias_r, norm_r, inv_r, h2_h, act_h, slope_h, own_r, other_r,
+        att_v, tok_v, wo_v, wi_v, wb_v, h2_v, act_v, slope_v, loc,
+    ):
+        loads = ((att_h, att_v), (wo_h, wo_v), (tok_h, tok_v), (wi_h, wi_v), (wb_h, wb_v))
+        for i, (src, dst) in enumerate(loads):
+            pltpu.make_async_copy(src, dst, loc.at[i]).start()
+        for i in range(3):
+            settle(loads[i][1], loc.at[i])
+
+        def first(t, carry):
+            b = t // blocks
+            part = pl.ds(pl.multiple_of(lax.rem(t, blocks) * some, some), some)
+            resid = tok_v[b, part, :].astype(f32) + dot(att_v[b, part, :], wo_v[...]) + sv_r[4:5, :]
+
+            normed, inv = normalize(resid)
+
+            @pl.when(b == 0)
+            def _():
+                own_r[part, :] = resid + sv_r[7:8, :]
+                norm_r[part, :] = normed
+                inv_r[part, :] = jnp.broadcast_to(inv, (some, LANES))
+
+            h2_v[pl.ds(pl.multiple_of(t * some, some), some), :] = (normed * sv_r[5:6, :] + sv_r[6:7, :]).astype(bf16)
+            return carry
+
+        lax.fori_loop(0, rows // some, first, 0)
+        pltpu.make_async_copy(h2_v, h2_h, loc.at[5]).start()
+        settle(wi_v, loc.at[3])
+
+        def second(t, carry):
+            part = pl.ds(pl.multiple_of(t * some, some), some)
+            h = h2_v[part, :]
+            for c in range(4):
+                cols = slice(c * columns, (c + 1) * columns)
+                act, slope = gelu_pair(dot(h, wi_v[:, cols]) + bias_r[:, cols])
+                act_v[part, cols] = act.astype(bf16)
+                slope_v[part, cols] = slope
+            pltpu.make_async_copy(act_v.at[part], act_h.at[part], loc.at[6]).start()
+            pltpu.make_async_copy(slope_v.at[part], slope_h.at[part], loc.at[7]).start()
+
+            @pl.when(t == 0)
+            def _():
+                settle(wb_v, loc.at[4])
+
+            out = dot(act_v[part, :], wb_v[...])
+
+            @pl.when(t < blocks)
+            def _():
+                own_r[part, :] += out
+
+            @pl.when(t >= blocks)
+            def _():
+                other_r[pl.ds(pl.multiple_of(t * some - size, some), some), :] = out.astype(bf16)
+
+            return carry
+
+        lax.fori_loop(0, rows // some, second, 0)
+        settle(h2_v, loc.at[5])
+        settle(act_v, loc.at[6])
+        settle(slope_v, loc.at[7])
+
+    def sds(shape, dtype=bf16):
+        return jax.ShapeDtypeStruct(shape, dtype)
+
+    return pl.pallas_call(
+        kernel,
+        name="hidden_forward",
+        out_shape=(
+            sds((size, d), f32), sds((size, LANES), f32), sds((rows, d)), sds((rows, hidden)), sds((rows, hidden), f32),
+            sds((size, d), f32), sds((size, d)),
+        ),
+        in_specs=[HB] * 5 + [VM] * 2,
+        out_specs=(VM,) * 2 + (HB,) * 3 + (VM,) * 2,
+        scratch_shapes=[
+            pltpu.VMEM(att.shape, bf16),
+            pltpu.VMEM(tokens.shape, bf16),
+            pltpu.VMEM(wo.shape, bf16),
+            pltpu.VMEM(wi.shape, bf16),
+            pltpu.VMEM(wb.shape, bf16),
+            pltpu.VMEM((rows, d), bf16),
+            pltpu.VMEM((rows, hidden), bf16),
+            pltpu.VMEM((rows, hidden), f32),
+            pltpu.SemaphoreType.DMA((8,)),
+        ],
+        compiler_params=pltpu.CompilerParams(vmem_limit_bytes=56 << 20),
+        cost_estimate=pl.CostEstimate(
+            flops=2 * rows * d * (d + 2 * hidden), bytes_accessed=40 << 20, transcendentals=rows * hidden
+        ),
+    )(att, tokens, wo, wi, wb, sv, bias)
+
+
+def hidden_back_call(slopes, cot, wb, wi):
+    rows, hidden = slopes.shape
+    d = cot.shape[1]
+    some, columns = 512, hidden // 4
+
+    def kernel(slope_h, cot_h, wb_h, wi_h, dp_h, own_r, other_r, gb_r, slope_v, cot_v, wb_v, wi_v, dp_v, loc):
+        steps = rows // some
+        for i, (src, dst) in enumerate(((cot_h, cot_v), (wb_h, wb_v), (wi_h, wi_v))):
+            pltpu.make_async_copy(src, dst, loc.at[i]).start()
+        for t in range(steps):
+            part = pl.ds(t * some, some)
+            pltpu.make_async_copy(slope_h.at[part], slope_v.at[part], loc.at[5 + t]).start()
+        gb_r[...] = jnp.zeros_like(gb_r)
+        settle(cot_v, loc.at[0])
+        settle(wb_v, loc.at[1])
+
+        def body(t, carry):
+            part = pl.ds(pl.multiple_of(t * some, some), some)
+            settle(slope_v.at[part], loc.at[5 + t])
+            c_rows = cot_v[part, :]
+            for c in range(4):
+                cols = slice(c * columns, (c + 1) * columns)
+                grad = (row_dot(c_rows, wb_v[cols, :]) * slope_v[part, cols]).astype(bf16)
+                dp_v[part, cols] = grad
+                gb_r[:, cols] += jnp.sum(grad.astype(f32), axis=0, keepdims=True)
+            pltpu.make_async_copy(dp_v.at[part], dp_h.at[part], loc.at[4]).start()
+
+            @pl.when(t == 0)
+            def _():
+                settle(wi_v, loc.at[2])
+
+            back = row_dot(dp_v[part, :], wi_v[...])
+
+            @pl.when(t < steps // 2)
+            def _():
+                own_r[part, :] = back
+
+            @pl.when(t >= steps // 2)
+            def _():
+                other_r[pl.ds(pl.multiple_of(t * some - rows // 2, some), some), :] = back.astype(bf16)
+
+            return carry
+
+        lax.fori_loop(0, steps, body, 0)
+        settle(dp_v, loc.at[4])
+
+    def sds(shape, dtype=bf16):
+        return jax.ShapeDtypeStruct(shape, dtype)
+
+    return pl.pallas_call(
+        kernel,
+        name="hidden_back",
+        out_shape=(sds(slopes.shape), sds((rows // 2, d), f32), sds((rows // 2, d)), sds((1, hidden), f32)),
+        in_specs=[HB] * 4,
+        out_specs=(HB,) + (VM,) * 3,
+        scratch_shapes=[
+            pltpu.VMEM(slopes.shape, f32),
+            pltpu.VMEM(cot.shape, bf16),
+            pltpu.VMEM(wb.shape, bf16),
+            pltpu.VMEM(wi.shape, bf16),
+            pltpu.VMEM(slopes.shape, bf16),
+            pltpu.SemaphoreType.DMA((5 + rows // some,)),
+        ],
+        compiler_params=pltpu.CompilerParams(vmem_limit_bytes=56 << 20),
+        cost_estimate=pl.CostEstimate(flops=4 * rows * d * hidden, bytes_accessed=28 << 20, transcendentals=0),
+    )(slopes, cot, wb, wi)
 
 
 def solution(mesh):
@@ -1150,7 +1327,7 @@
         parts = bias_in.shape[0] // per
         half_bin = lax.dynamic_slice_in_dim(sv[8 : 8 + parts], odd * (d // 2), d // 2, 1)
         half_bin = half_bin.reshape(parts, nd // 2, per).transpose(1, 0, 2).reshape(-1)
-        g_two, s_two = sv[5], sv[6]
+        g_two = sv[5]
 
         def to_neighbour(values):
             pairs = []
@@ -1161,31 +1338,22 @@
 
         size = tokens.shape[1]
         cot_two = jnp.concatenate([cot_own, to_neighbour(cot_own).astype(bf16)])
-        x_f = tb.reshape(2 * size, d).astype(f32)
-        att_two = att_two.reshape(2 * size, d)
-        resid = x_f + dot(att_two, full_out) + sv[4]
-        normed2, scale2 = normalize(resid)
-        h_two = (normed2 * g_two + s_two).astype(bf16)
-        pre = dot(h_two, half_in) + half_bin
-        act = gelu_pair(pre)[0].astype(bf16)
-        out_part = dot(act, half_back)
-        leaves = out_part[size:].astype(bf16)
+        normed2, scale2, h_two, act, slopes, own_out, leaves = hidden_forward_call(
+            att_two, tb, full_out, half_in, half_back, sv, half_bin.reshape(1, -1)
+        )
         others_out = to_neighbour(leaves)
-        pre, leaves = lax.optimization_barrier((pre, leaves))
-        d_pre = (row_dot(cot_two, half_back) * gelu_pair(pre)[1]).astype(bf16)
-        g_b_in = jnp.sum(d_pre.astype(f32), axis=0)
-        d_h2_part = row_dot(d_pre, half_in)
-        leaves = d_h2_part[size:].astype(bf16)
+        slopes, leaves = lax.optimization_barrier((slopes, leaves))
+        d_pre, d_h2_own, leaves, g_b_in = hidden_back_call(slopes, cot_two, half_back, half_in)
         others_d = to_neighbour(leaves)
-        pre, d_pre, leaves = lax.optimization_barrier((pre, d_pre, leaves))
-        g_w_back = col_dot(gelu_pair(pre)[0].astype(bf16), cot_two).astype(bf16)
+        act, d_pre, leaves = lax.optimization_barrier((act, d_pre, leaves))
+        g_w_back = col_dot(act, cot_two).astype(bf16)
         g_w_in = col_dot(h_two, d_pre).astype(bf16)
 
-        resid, normed2, scale2 = resid[:size], normed2[:size], scale2[:size]
-        att_tok, cot_f = att_two[:size], cot_two[:size].astype(f32)
-        result = (resid + out_part[:size] + others_out + sv[7]).astype(bf16)
+        scale2 = scale2[:, :1]
+        att_tok, cot_f = att_two[0], cot_own.astype(f32)
+        result = (own_out + others_out).astype(bf16)
         g_b_back = jnp.sum(cot_f, axis=0)
-        d_h2 = d_h2_part[:size] + others_d
+        d_h2 = d_h2_own + others_d
         g_g2 = jnp.sum(d_h2 * normed2, axis=0)
         g_s2 = jnp.sum(d_h2, axis=0)
         d_resid = cot_f + norm_back(d_h2 * g_two, normed2, scale2)
@@ -1199,13 +1367,14 @@
         )
         gsm = jnp.concatenate([jnp.stack([g_b_out, g_g2, g_s2, g_b_back]), bin_rows])
 
-        (own_result, g_tok, gq, go, gi, gb, small) = backward_call(
-            n, m, result, d_att_tok, d_resid, q, k, v, o, lse, h1, wq, tb[0], sv, gsm,
+        (own_result, g_tok, swapped, g_qkv, go, gi, gb, small) = backward_call(
+            n, m, result, d_att_tok, d_resid, q, k, v, o, lse, h1, wq, tb, sv, gsm,
             g_w_out.reshape(n, m // 2, 2, d // nd, d),
             g_w_in.reshape(n, m // 2, 2, d // nd, ff // 2),
             g_w_back.reshape(n // 2, m // 2, 2, ff // nd, d),
         )
-        g_qkv = gq.reshape(n, rq, 3, width).transpose(1, 2, 0, 3).reshape(rq, 3 * d).astype(f32)
+        away = lax.rem(lax.axis_index("shard"), 2) != lax.axis_index("seq") // (n // 2)
+        g_tok = jnp.where(away, swapped.astype(f32), g_tok)
         mine = lax.dynamic_slice_in_dim(small, lax.axis_index("shard") * per, per, 1)
         return (
             own_result[None], g_tok[None], mine[0], mine[1], g_qkv, mine[2], mine[3], go, mine[4],

time: 347 us -> 349 us (level)
  Pallas kernels: 247 us -> 289 us
  matrix products: 55.2 us -> 20.7 us
  local copies, waits for them, and re-layouts: 28.3 us -> 16.8 us
  waiting for transfers between devices: 0.92 us -> 5.06 us
    pallas_call x0 -> x2, Pallas kernels: none -> 42.2 us  [the longest x1 25.3 us: hidden_forward_call(): pl.pallas_call(kernel, name='hidden_forward', out_shape=(sds((size, d), f...]
    dot_general x3 -> x1, matrix products: 19 us -> 2.27 us  [row_dot(): return lax.dot_general(a, b, NT, preferred_element_type=f32)]
    dot_general x3 -> x0, matrix products: 14.9 us -> none  [dot(): return jnp.dot(a, b, preferred_element_type=f32)]
    unnamed x58 -> x38, local copies, waits for them, and re-layouts: 14.5 us -> 7.24 us
    ppermute x3, waiting for transfers between devices: 0.92 us -> 5.06 us  [to_neighbour(): return lax.ppermute(values.astype(bf16), every, pairs).astype(f32)]
  transfers between devices with their start and end apart: 3 -> 3, of which waited for: 1 -> 1; matrix products, arithmetic and copies ran while one was open for 18% -> 7% of each run, Pallas kernels for 0% -> 12%
where the time goes in v3:
time: 349 us; the launch traced here: 343 us
  Pallas kernels  289 us (83%)
  matrix products  20.7 us (6%)
  local copies, waits for them, and re-layouts  16.8 us (5%)
  other arithmetic  8.29 us (2%)
  waiting for transfers between devices  5.06 us (1%)
    pallas_call x1, Pallas kernels, backward_call(): pl.pallas_call(kernel, name='attend_back_reduce', out_shape=(sds((size, d...  127 us
    pallas_call x1, Pallas kernels, forward_call(): pl.pallas_call(kernel, name='gather_attend', out_shape=(sds((n, m // 2, 2...  119 us
    pallas_call x1, Pallas kernels, hidden_forward_call(): pl.pallas_call(kernel, name='hidden_forward', out_shape=(sds((size, d), f...  25.3 us
    dot_general x3, matrix products, col_dot(): return lax.dot_general(a, b, TN, preferred_element_type=f32)  18.4 us
    pallas_call x1, Pallas kernels, hidden_back_call(): pl.pallas_call(kernel, name='hidden_back', out_shape=(sds(slopes.shape),...  16.9 us
    unnamed x38, local copies, waits for them, and re-layouts  7.24 us
  transfers between devices with their start and end apart: 3, of which 1 were waited for; matrix products, arithmetic and copies ran while one was open for 7% of the time, Pallas kernels for 12%

profile of v3, /device:TPU:1, one launch (start us, length us, event | category | flops | bytes accessed | tf_op | source)
XLA Modules:
  0.0 342.7 jit_solution(7614347369943996447)
XLA Ops:
  0.7 0.9 slice_bitcast_fusion
  1.6 0.8 stack.19
  3.1 119.5 %gather_attend.1 = (bf16[4,4,2,32,1024]{4,3,2,1,0:T(8,128)(2,1)}, bf16[4,4,2,32,2048]{4,3,2,1,0:T(8,128)(2,1)}, bf16[2,4,2,128,1024]{4,3,2,1,0:T(8,128)(2,1)}, b...) custom-call(bf16[512,1024]{1,0:T(8,128)(2,1)} %bitcast.81, ...), custom_call_target="tpu_custom_call" | custom-call | flops 5368709120 | bytes 83886080 | tf_op jit(solution)/shard_map/gather_attend/pallas_call | solution.py:542
  124.2 25.3 %hidden_forward.1 = (f32[512,1024]{1,0:T(8,128)}, f32[512,128]{1,0:T(8,128)}, bf16[1024,1024]{1,0:T(8,128)(2,1)}, bf16[1024,2048]{1,0:T(8,128)(2,1)}, f32[1024,2...) custom-call(bf16[2,512,1024]{2,1,0:T(8,128)(2,1)} %get-tuple-element.51.att_h, ...), custom_call_target="tpu_custom_call" | custom-call | flops 10737418240 | bytes 41943040 | tf_op jit(solution)/shard_map/hidden_forward/pallas_call | solution.py:1205
  149.5 1.5 collective-permute-start
  151.8 1.1 slice_reduce_fusion
  153.1 1.3 copy-done.6
  154.4 16.9 %hidden_back.1 = (bf16[1024,2048]{1,0:T(8,128)(2,1)}, f32[512,1024]{1,0:T(8,128)}, bf16[512,1024]{1,0:T(8,128)(2,1)}, f32[1,2048]{1,0:T(1,128)}) custom-call(f32[1024,2048]{1,0:T(8,128)} %get-tuple-element.62.slope_h, bf16[1024,1024]{1,0:T(8,128)(2,1)} %copy-done.6, bf16[2048,1024]{1,0:T(8,128)(2,1)} %bitcast.86, bf16[1024,2048]{1,0:T(8,128)(2,1)} %bitcast.84), custom_call_target="tpu_custom_call" | custom-call | flops 8589934592 | bytes 29360128 | tf_op jit(solution)/shard_map/hidden_back/pallas_call | solution.py:1281
  171.9 1.4 reduce.5
  173.5 9.5 %convolution_convert_fusion = bf16[2048,1024]{1,0:T(8,128)(2,1)} fusion(bf16[1024,2048]{1,0:T(8,128)(2,1)} %get-tuple-element.78, bf16[1024,1024]{1,0:T(8,128)(2,1)} %copy-done.6), kind=kOutput, calls=%fused_computation | convolution fusion | flops 4297064448 | bytes 10485760 | tf_op jit(solution)/shard_map/dot_general | solution.py:38
  183.0 1.4 add_convert_fusion.refs_0_
  184.4 1.2 copy-done.13
  185.6 6.2 %convolution_convert_fusion.1 = bf16[1024,2048]{1,0:T(8,128)(2,1)} fusion(bf16[1024,1024]{1,0:T(8,128)(2,1)S(1)} %copy-done.14, bf16[1024,2048]{1,0:T(8,128)(2,1)S(1)} %copy-done.13), kind=kOutput, calls=%fused_computation.1 | convolution fusion | flops 4297064448 | bytes 10485760 | tf_op jit(solution)/shard_map/dot_general | solution.py:38
  191.8 5.1 %collective-permute-done.2 = bf16[512,1024]{1,0:T(8,128)(2,1)S(1)} collective-permute-done((bf16[512,1024]{1,0:T(8,128)(2,1)}, bf16[512,1024]{1,0:T(8,128)(2,1)S(1)}, u32[]{:S(2)}, u32[]{:S(2)}) %collective-permute-start.2) | collective-permute-done | bytes 1048608 | tf_op jit(solution)/shard_map/ppermute | solution.py:1337
  196.9 0.9 multiply_reduce_fusion
  197.8 0.9 fusion.10
  199.4 2.3 convolution_convert_fusion.3.refs_1_
  201.7 2.7 convolution_convert_fusion.2
  205.0 127.3 %attend_back_reduce.1 = (bf16[512,1024]{1,0:T(8,128)(2,1)}, f32[512,1024]{1,0:T(8,128)}, bf16[512,1024]{1,0:T(8,128)(2,1)}, f32[32,3072]{1,0:T(8,128)}, f32[32,1...) custom-call(bf16[512,1024]{1,0:T(8,128)(2,1)} %add_convert_fusion.refs_0_, ...), custom_call_target="tpu_custom_call" | custom-call | flops 11811160064 | bytes 83886080 | tf_op jit(solution)/shard_map/attend_back_reduce/pallas_call | solution.py:1063
  333.6 3.1 select_bitcast_fusion
  336.7 1.6 dynamic-slice_bitcast_fusion
  338.3 1.0 copy.41
  340.7 0.8 copy.44
  341.5 0.8 copy.45
  (62 shorter events, 8.2 us)
Async XLA Ops:
  122.6 30.4 %collective-permute-start.1 = (bf16[512,1024]{1,0:T(8,128)(2,1)}, bf16[512,1024]{1,0:T(8,128)(2,1)S(1)}, u32[]{:S(2)}, u32[]{:S(2)}) collective-permute-start(bf16[512,1024]{1,0:T(8,128)(2,1)} %get-tuple-element.59), channel_id=1, source_target_pairs={{0,8},{1,9},{2,10},{3,11},{4,12},{5,13},{6,14},{7,15},{8,0},{9,1},... | collective-permute-start | bytes 3145736 | tf_op jit(solution)/shard_map/ppermute | solution.py:1337
  124.2 28.7 %copy-start.2 = (bf16[512,1024]{1,0:T(8,128)(2,1)S(1)}, bf16[512,1024]{1,0:T(8,128)(2,1)}, u32[]{:S(2)}) copy-start(bf16[512,1024]{1,0:T(8,128)(2,1)} %get-tuple-element.59) | copy-start | bytes 3145732
  149.5 33.5 %collective-permute-start = (bf16[512,1024]{1,0:T(8,128)(2,1)}, bf16[512,1024]{1,0:T(8,128)(2,1)S(1)}, u32[]{:S(2)}, u32[]{:S(2)}) collective-permute-start(bf16[512,1024]{1,0:T(8,128)(2,1)} %get-tuple-element.58), channel_id=1, source_target_pairs={{0,8},{1,9},{2,10},{3,11},{4,12},{5,13},{6,14},{7,15},{8,0},{9,1},... | collective-permute-start | bytes 3145736 | tf_op jit(solution)/shard_map/ppermute | solution.py:1337
  153.1 1.3 copy-start.6
  171.3 25.6 %collective-permute-start.2 = (bf16[512,1024]{1,0:T(8,128)(2,1)}, bf16[512,1024]{1,0:T(8,128)(2,1)S(1)}, u32[]{:S(2)}, u32[]{:S(2)}) collective-permute-start(bf16[512,1024]{1,0:T(8,128)(2,1)} %get-tuple-element.64), channel_id=1, source_target_pairs={{0,8},{1,9},{2,10},{3,11},{4,12},{5,13},{6,14},{7,15},{8,0},{9,1},... | collective-permute-start | bytes 3145736 | tf_op jit(solution)/shard_map/ppermute | solution.py:1337
  173.5 9.5 %copy-start.4 = (f32[512,1024]{1,0:T(8,128)S(1)}, f32[512,1024]{1,0:T(8,128)}, u32[]{:S(2)}) copy-start(f32[512,1024]{1,0:T(8,128)} %get-tuple-element.57) | copy-start | bytes 6291460
  173.5 10.9 %copy-start.14 = (bf16[1024,1024]{1,0:T(8,128)(2,1)S(1)}, bf16[1024,1024]{1,0:T(8,128)(2,1)}, u32[]{:S(2)}) copy-start(bf16[1024,1024]{1,0:T(8,128)(2,1)} %get-tuple-element.74) | copy-start | bytes 6291460
  183.0 2.6 copy-start.13
  185.6 11.3 %copy-start = (f32[512,1024]{1,0:T(8,128)S(1)}, f32[512,1024]{1,0:T(8,128)}, u32[]{:S(2)}) copy-start(f32[512,1024]{1,0:T(8,128)} %get-tuple-element.65) | copy-start | bytes 6291460
  185.6 11.3 %copy-start.1 = (f32[512,1024]{1,0:T(8,128)S(1)}, f32[512,1024]{1,0:T(8,128)}, u32[]{:S(2)}) copy-start(f32[512,1024]{1,0:T(8,128)} %get-tuple-element.63) | copy-start | bytes 6291460
  197.8 1.6 copy-start.11
  198.7 2.9 copy-start.3
  199.4 2.3 copy-start.12
  333.6 4.7 %copy-start.5 = (bf16[512,1024]{1,0:T(8,128)(2,1)S(1)}, bf16[512,1024]{1,0:T(8,128)(2,1)}, u32[]{:S(2)}) copy-start(bf16[512,1024]{1,0:T(8,128)(2,1)} %get-tuple-element.79) | copy-start | bytes 3145732
  336.7 2.6 copy-start.9
  336.7 3.3 copy-start.10
  336.7 4.0 %copy-start.8 = (f32[32,4096]{1,0:T(8,128)S(1)}, f32[32,4096]{1,0:T(8,128)}, u32[]{:S(2)}) copy-start(f32[32,4096]{1,0:T(8,128)} %get-tuple-element.136) | copy-start | bytes 1572868
  338.3 3.2 copy-start.7

commit v4 on v3

--- a/solution.py
+++ b/solution.py
@@ -1134,7 +1134,7 @@
 def hidden_forward_call(att, tokens, wo, wi, wb, sv, bias):
     size, d = att.shape[1:]
     rows, hidden = 2 * size, wi.shape[1]
-    some, columns = 512, hidden // 4
+    some, columns = 256, hidden // 4
     blocks = size // some
 
     def kernel(
@@ -1232,7 +1232,7 @@
 def hidden_back_call(slopes, cot, wb, wi):
     rows, hidden = slopes.shape
     d = cot.shape[1]
-    some, columns = 512, hidden // 4
+    some, columns = 256, hidden // 4
 
     def kernel(slope_h, cot_h, wb_h, wi_h, dp_h, own_r, other_r, gb_r, slope_v, cot_v, wb_v, wi_v, dp_v, loc):
         steps = rows // some

time: 349 us -> 343 us (0.983); the launches traced: 343 us -> 343 us
  transfers between devices with their start and end apart: 3 -> 3, of which waited for: 1 -> 1; matrix products, arithmetic and copies ran while one was open for 7% -> 7% of each run, Pallas kernels for 12% -> 13%
where the time goes in v4:
time: 343 us
  Pallas kernels  289 us (84%)
  matrix products  20.7 us (6%)
  local copies, waits for them, and re-layouts  16.8 us (5%)
  other arithmetic  8.29 us (2%)
  waiting for transfers between devices  5.01 us (1%)
    pallas_call x1, Pallas kernels, backward_call(): pl.pallas_call(kernel, name='attend_back_reduce', out_shape=(sds((size, d...  126 us
    pallas_call x1, Pallas kernels, forward_call(): pl.pallas_call(kernel, name='gather_attend', out_shape=(sds((n, m // 2, 2...  119 us
    pallas_call x1, Pallas kernels, hidden_forward_call(): pl.pallas_call(kernel, name='hidden_forward', out_shape=(sds((size, d), f...  26.6 us
    dot_general x3, matrix products, col_dot(): return lax.dot_general(a, b, TN, preferred_element_type=f32)  18.4 us
    pallas_call x1, Pallas kernels, hidden_back_call(): pl.pallas_call(kernel, name='hidden_back', out_shape=(sds(slopes.shape),...  16.9 us
    unnamed x38, local copies, waits for them, and re-layouts  7.24 us
  transfers between devices with their start and end apart: 3, of which 1 were waited for; matrix products, arithmetic and copies ran while one was open for 7% of the time, Pallas kernels for 13%

profile of v4, /device:TPU:1, one launch (start us, length us, event | category | flops | bytes accessed | tf_op | source)
XLA Modules:
  0.0 342.7 jit_solution(13724703451558359246)
XLA Ops:
  0.7 0.9 slice_bitcast_fusion
  1.6 0.8 stack.19
  3.1 119.5 %gather_attend.1 = (bf16[4,4,2,32,1024]{4,3,2,1,0:T(8,128)(2,1)}, bf16[4,4,2,32,2048]{4,3,2,1,0:T(8,128)(2,1)}, bf16[2,4,2,128,1024]{4,3,2,1,0:T(8,128)(2,1)}, b...) custom-call(bf16[512,1024]{1,0:T(8,128)(2,1)} %bitcast.81, ...), custom_call_target="tpu_custom_call" | custom-call | flops 5368709120 | bytes 83886080 | tf_op jit(solution)/shard_map/gather_attend/pallas_call | solution.py:542
  124.2 26.6 %hidden_forward.1 = (f32[512,1024]{1,0:T(8,128)}, f32[512,128]{1,0:T(8,128)}, bf16[1024,1024]{1,0:T(8,128)(2,1)}, bf16[1024,2048]{1,0:T(8,128)(2,1)}, f32[1024,2...) custom-call(bf16[2,512,1024]{2,1,0:T(8,128)(2,1)} %get-tuple-element.51.att_h, ...), custom_call_target="tpu_custom_call" | custom-call | flops 10737418240 | bytes 41943040 | tf_op jit(solution)/shard_map/hidden_forward/pallas_call | solution.py:1205
  150.8 1.5 collective-permute-start
  153.1 1.1 slice_reduce_fusion
  154.4 1.3 copy-done.6
  155.7 16.9 %hidden_back.1 = (bf16[1024,2048]{1,0:T(8,128)(2,1)}, f32[512,1024]{1,0:T(8,128)}, bf16[512,1024]{1,0:T(8,128)(2,1)}, f32[1,2048]{1,0:T(1,128)}) custom-call(f32[1024,2048]{1,0:T(8,128)} %get-tuple-element.62.slope_h, bf16[1024,1024]{1,0:T(8,128)(2,1)} %copy-done.6, bf16[2048,1024]{1,0:T(8,128)(2,1)} %bitcast.86, bf16[1024,2048]{1,0:T(8,128)(2,1)} %bitcast.84), custom_call_target="tpu_custom_call" | custom-call | flops 8589934592 | bytes 29360128 | tf_op jit(solution)/shard_map/hidden_back/pallas_call | solution.py:1281
  173.2 1.4 reduce.5
  174.8 9.5 %convolution_convert_fusion = bf16[2048,1024]{1,0:T(8,128)(2,1)} fusion(bf16[1024,2048]{1,0:T(8,128)(2,1)} %get-tuple-element.78, bf16[1024,1024]{1,0:T(8,128)(2,1)} %copy-done.6), kind=kOutput, calls=%fused_computation | convolution fusion | flops 4297064448 | bytes 10485760 | tf_op jit(solution)/shard_map/dot_general | solution.py:38
  184.3 1.4 add_convert_fusion.refs_0_
  185.7 1.2 copy-done.13
  186.9 6.2 %convolution_convert_fusion.1 = bf16[1024,2048]{1,0:T(8,128)(2,1)} fusion(bf16[1024,1024]{1,0:T(8,128)(2,1)S(1)} %copy-done.14, bf16[1024,2048]{1,0:T(8,128)(2,1)S(1)} %copy-done.13), kind=kOutput, calls=%fused_computation.1 | convolution fusion | flops 4297064448 | bytes 10485760 | tf_op jit(solution)/shard_map/dot_general | solution.py:38
  193.2 5.0 %collective-permute-done.2 = bf16[512,1024]{1,0:T(8,128)(2,1)S(1)} collective-permute-done((bf16[512,1024]{1,0:T(8,128)(2,1)}, bf16[512,1024]{1,0:T(8,128)(2,1)S(1)}, u32[]{:S(2)}, u32[]{:S(2)}) %collective-permute-start.2) | collective-permute-done | bytes 1048608 | tf_op jit(solution)/shard_map/ppermute | solution.py:1337
  198.2 0.9 multiply_reduce_fusion
  199.1 0.9 fusion.10
  200.7 2.3 convolution_convert_fusion.3.refs_1_
  202.9 2.7 convolution_convert_fusion.2
  206.3 126.4 %attend_back_reduce.1 = (bf16[512,1024]{1,0:T(8,128)(2,1)}, f32[512,1024]{1,0:T(8,128)}, bf16[512,1024]{1,0:T(8,128)(2,1)}, f32[32,3072]{1,0:T(8,128)}, f32[32,1...) custom-call(bf16[512,1024]{1,0:T(8,128)(2,1)} %add_convert_fusion.refs_0_, ...), custom_call_target="tpu_custom_call" | custom-call | flops 11811160064 | bytes 83886080 | tf_op jit(solution)/shard_map/attend_back_reduce/pallas_call | solution.py:1063
  334.1 3.1 select_bitcast_fusion
  337.1 1.6 dynamic-slice_bitcast_fusion
  338.7 1.0 copy.41
  341.1 0.8 copy.44
  341.9 0.8 copy.45
  (62 shorter events, 8.2 us)
Async XLA Ops:
  122.6 31.7 %collective-permute-start.1 = (bf16[512,1024]{1,0:T(8,128)(2,1)}, bf16[512,1024]{1,0:T(8,128)(2,1)S(1)}, u32[]{:S(2)}, u32[]{:S(2)}) collective-permute-start(bf16[512,1024]{1,0:T(8,128)(2,1)} %get-tuple-element.59), channel_id=1, source_target_pairs={{0,8},{1,9},{2,10},{3,11},{4,12},{5,13},{6,14},{7,15},{8,0},{9,1},... | collective-permute-start | bytes 3145736 | tf_op jit(solution)/shard_map/ppermute | solution.py:1337
  124.2 30.0 %copy-start.2 = (bf16[512,1024]{1,0:T(8,128)(2,1)S(1)}, bf16[512,1024]{1,0:T(8,128)(2,1)}, u32[]{:S(2)}) copy-start(bf16[512,1024]{1,0:T(8,128)(2,1)} %get-tuple-element.59) | copy-start | bytes 3145732
  150.8 33.5 %collective-permute-start = (bf16[512,1024]{1,0:T(8,128)(2,1)}, bf16[512,1024]{1,0:T(8,128)(2,1)S(1)}, u32[]{:S(2)}, u32[]{:S(2)}) collective-permute-start(bf16[512,1024]{1,0:T(8,128)(2,1)} %get-tuple-element.58), channel_id=1, source_target_pairs={{0,8},{1,9},{2,10},{3,11},{4,12},{5,13},{6,14},{7,15},{8,0},{9,1},... | collective-permute-start | bytes 3145736 | tf_op jit(solution)/shard_map/ppermute | solution.py:1337
  154.4 1.3 copy-start.6
  172.6 25.5 %collective-permute-start.2 = (bf16[512,1024]{1,0:T(8,128)(2,1)}, bf16[512,1024]{1,0:T(8,128)(2,1)S(1)}, u32[]{:S(2)}, u32[]{:S(2)}) collective-permute-start(bf16[512,1024]{1,0:T(8,128)(2,1)} %get-tuple-element.64), channel_id=1, source_target_pairs={{0,8},{1,9},{2,10},{3,11},{4,12},{5,13},{6,14},{7,15},{8,0},{9,1},... | collective-permute-start | bytes 3145736 | tf_op jit(solution)/shard_map/ppermute | solution.py:1337
  174.8 9.5 %copy-start.4 = (f32[512,1024]{1,0:T(8,128)S(1)}, f32[512,1024]{1,0:T(8,128)}, u32[]{:S(2)}) copy-start(f32[512,1024]{1,0:T(8,128)} %get-tuple-element.57) | copy-start | bytes 6291460
  174.8 10.9 %copy-start.14 = (bf16[1024,1024]{1,0:T(8,128)(2,1)S(1)}, bf16[1024,1024]{1,0:T(8,128)(2,1)}, u32[]{:S(2)}) copy-start(bf16[1024,1024]{1,0:T(8,128)(2,1)} %get-tuple-element.74) | copy-start | bytes 6291460
  184.3 2.6 copy-start.13
  186.9 11.3 %copy-start = (f32[512,1024]{1,0:T(8,128)S(1)}, f32[512,1024]{1,0:T(8,128)}, u32[]{:S(2)}) copy-start(f32[512,1024]{1,0:T(8,128)} %get-tuple-element.65) | copy-start | bytes 6291460
  186.9 11.3 %copy-start.1 = (f32[512,1024]{1,0:T(8,128)S(1)}, f32[512,1024]{1,0:T(8,128)}, u32[]{:S(2)}) copy-start(f32[512,1024]{1,0:T(8,128)} %get-tuple-element.63) | copy-start | bytes 6291460
  199.1 1.6 copy-start.11
  200.0 2.9 copy-start.3
  200.7 2.3 copy-start.12
  334.1 4.7 %copy-start.5 = (bf16[512,1024]{1,0:T(8,128)(2,1)S(1)}, bf16[512,1024]{1,0:T(8,128)(2,1)}, u32[]{:S(2)}) copy-start(bf16[512,1024]{1,0:T(8,128)(2,1)} %get-tuple-element.79) | copy-start | bytes 3145732
  337.1 2.6 copy-start.9
  337.1 3.3 copy-start.10
  337.1 4.0 %copy-start.8 = (f32[32,4096]{1,0:T(8,128)S(1)}, f32[32,4096]{1,0:T(8,128)}, u32[]{:S(2)}) copy-start(f32[32,4096]{1,0:T(8,128)} %get-tuple-element.136) | copy-start | bytes 1572868
  338.7 3.2 copy-start.7

commit v5 on v2

--- a/solution.py
+++ b/solution.py
@@ -345,9 +345,13 @@
 
         settle(wq_v.at[pl.ds(0, half * 2 * rq)], w_recv.at[2])
         settle(sma.at[pl.ds(0, half * 2)], w_recv.at[3])
+        def cut(block, h):
+            return block.at[pl.ds(h * (size // 2), size // 2)]
+
         @pl.when(away)
         def _():
-            send(tok_r, tokf.at[at.low + half * (1 - core)], ts, 0, at.swap())
+            for h in range(2):
+                send(cut(tok_r, h), cut(tokf.at[at.low + half * (1 - core)], h), ts, h, at.swap())
 
         for step in range(1, planes):
             there = (at.s, 2 * at.beside(step) + core)
@@ -357,18 +361,22 @@
                 send(sma.at[pl.ds(row, 2)], sma.at[pl.ds(row, 2)], ws, 5, there)
         z_to_a(0)
 
-        @pl.when(away)
-        def _():
-            settle(tokf.at[0], t_recv.at[0])
-
         @pl.when(jnp.logical_not(away))
         def _():
             settle(tokf.at[0], loc.at[2])
 
-        for step in range(1, half):
-            low = lax.rem(at.low + step, half)
-            send(tokf.at[rank], tokf.at[rank], ts, 1, (at.team * half + low, at.k))
-        send(tokf.at[rank], tokf.at[rank], ts, 2, at.partner())
+        def own_half(h):
+            @pl.when(away)
+            def _():
+                settle(cut(tokf.at[0], h), t_recv.at[h])
+
+            part = cut(tokf.at[rank], h)
+            for step in range(1, half):
+                low = lax.rem(at.low + step, half)
+                send(part, part, ts, 2 + h, (at.team * half + low, at.k))
+            send(part, part, ts, 4, at.partner())
+
+        own_half(0)
 
         settle(wq_v.at[pl.ds(0, (planes - 1) * n * 2 * rq)], w_recv.at[4])
         settle(sma.at[pl.ds(0, (planes - 1) * n * 2)], w_recv.at[5])
@@ -413,17 +421,19 @@
 
             @pl.when(away)
             def _():
-                send(cot_r, cb_r, ts, 4, at.swap())
+                send(cot_r, cb_r, ts, 6, at.swap())
 
             @pl.when(jnp.logical_not(away))
             def _():
                 pltpu.make_async_copy(cot_r, cb_r, loc.at[3]).start()
+
+        own_half(1)
 
         def take(t, carry):
             @pl.when(t == 1)
             def _():
                 z_to_a(1)
-                settle(tokf.at[0], t_recv.at[2])
+                settle(tokf.at[0], t_recv.at[4])
                 a_to_b(0)
 
             if half > 1:
@@ -431,14 +441,15 @@
                 @pl.when(t == 2)
                 def _():
                     a_to_b(1)
-                    settle(tokf.at[pl.ds(0, half - 1)], t_recv.at[1])
-                    for step in range(1, half):
-                        b = lax.rem(at.low + step, half) + half * core
-                        send(tokf.at[b], tokf.at[b], ts, 3, at.partner())
+                    for h in range(2):
+                        settle(tokf.at[pl.ds(0, half - 1), pl.ds(0, size // 2)], t_recv.at[2 + h])
+                        for step in range(1, half):
+                            part = cut(tokf.at[lax.rem(at.low + step, half) + half * core], h)
+                            send(part, part, ts, 5, at.partner())
 
                 @pl.when(t == 1 + half)
                 def _():
-                    settle(tokf.at[pl.ds(0, half - 1)], t_recv.at[3])
+                    settle(tokf.at[pl.ds(0, half - 1)], t_recv.at[5])
                     later_z()
 
             step = jnp.where(t < 2, 0, lax.rem(t - 2, max(half - 1, 1)) + 1)
@@ -509,18 +520,20 @@
 
         @pl.when(away)
         def _():
-            settle(tokf.at[0], t_send.at[0])
-            settle(cb_r, t_recv.at[4])
-            settle(cb_r, t_send.at[4])
+            for h in range(2):
+                settle(cut(tokf.at[0], h), t_send.at[h])
+            settle(cb_r, t_recv.at[6])
+            settle(cb_r, t_send.at[6])
 
         @pl.when(jnp.logical_not(away))
         def _():
             settle(cb_r, loc.at[3])
 
-        settle(tokf.at[0], t_send.at[2])
+        settle(tokf.at[0], t_send.at[4])
         if half > 1:
-            settle(tokf.at[pl.ds(0, half - 1)], t_send.at[1])
-            settle(tokf.at[pl.ds(0, half - 1)], t_send.at[3])
+            for h in range(2):
+                settle(tokf.at[pl.ds(0, half - 1), pl.ds(0, size // 2)], t_send.at[2 + h])
+            settle(tokf.at[pl.ds(0, half - 1)], t_send.at[5])
 
     def sds(shape, dtype=bf16):
         return jax.ShapeDtypeStruct(shape, dtype)
@@ -556,7 +569,7 @@
             pltpu.VMEM((8, size), f32),
             pltpu.VMEM((size, width), f32),
             pltpu.VMEM((2, max(8, d // LANES), LANES), f32),
-            sems((6,)), sems((6,)),
+            sems((7,)), sems((7,)),
             sems((6,)), sems((6,)),
             sems((2,)), sems((2,)),
             sems((nc,)), sems((nc,)),
@@ -602,10 +615,10 @@
 
     def kernel(*refs):
         (res_r, dat_r, dres_r, q_h, k_h, v_h, o_r, lse_r, h1_r, wq_h, tb_r, sv_r, gsm_r, gwo_r, gwi_r, gwb_r) = refs[:16]
-        (reso_r, gt_r, gq_r, go_r, gi_r, gb_r, small_r) = refs[16:23]
-        (do, delta, dqa, dka, dva, dqkv, gacc, rqp, rqh, pf, sd, rd, rzd, rg, sm, smz, smp, smc) = refs[23:41]
-        gqb, hb, sg, tb_v, o_v, q_r, k_r, v_r, wq_r = refs[41:50]
-        rest = refs[50:]
+        (reso_r, gt_r, rg, gqo_r, go_r, gi_r, gb_r, small_r) = refs[16:24]
+        (do, delta, dqa, dka, dva, dqkv, gacc, rqp, rqh, pf, sd, rd, rzd, sm, smz, smp, smc) = refs[24:41]
+        gqb, hb, sg, tb_v, o_v, q_r, k_r, v_r, wq_r, gq_r = refs[41:51]
+        rest = refs[51:]
         ga, rc, rp, rz = (rest[i * nc : (i + 1) * nc] for i in range(4))
         (d_s, d_r, x_s, x_r, y_s, y_r, e_s, e_r, c_s, c_r, p_s, p_r, z_s, z_r, m_s, m_r, yl_s, yl_r, el_s, el_r, loc) = rest[4 * nc :]
         at = Place(n, m)
@@ -624,7 +637,7 @@
         for c in range(nc):
             send(grads[c].at[:, :, 1 - core], rc[c], (c_s, c_r), c, at.partner())
             pltpu.make_async_copy(grads[c].at[:, :, core], ga[c], loc.at[6 + c]).start()
-        fetch_tb = pltpu.make_async_copy(tb_r, tb_v, loc.at[4])
+        fetch_tb = pltpu.make_async_copy(tb_r.at[0], tb_v, loc.at[4])
         fetch_tb.start()
         for i in range(n):
             pltpu.make_async_copy(o_r.at[pl.ds(i * size, size)], o_v.at[:, pl.ds(i * width, width)], loc.at[5]).start()
@@ -986,6 +999,10 @@
 
         settle(gq_r.at[pl.ds(0, n - 1)], m_r.at[4])
         settle(gq_r.at[0], loc.at[0])
+        for r in range(n):
+            for part in range(3):
+                first = part * d + r * width
+                gqo_r[:, first : first + width] = gq_r[r, :, part * width : (part + 1) * width].astype(f32)
 
         @pl.when(away)
         def _():
@@ -993,13 +1010,6 @@
             settle(rg, x_s.at[1])
             settle(reso_r, x_r.at[0])
             settle(reso_r, x_s.at[0])
-
-            def widen(t, carry):
-                rows = pl.ds(pl.multiple_of(t * 128, 128), 128)
-                gt_r[rows, :] = rg[rows, :].astype(f32)
-                return carry
-
-            lax.fori_loop(0, size // 128, widen, 0)
 
         @pl.when(jnp.logical_not(away))
         def _():
@@ -1056,14 +1066,15 @@
         out_shape=(
             sds((size, d)),
             sds((size, d), f32),
-            sds((n, rq, 3 * width)),
+            sds((size, d)),
+            sds((rq, 3 * d), f32),
             sds(gwo.shape[3:], f32),
             sds((gwi.shape[3], 2 * gwi.shape[4]), f32),
             sds(gwb.shape[3:], f32),
             sds((16, lanes_s), f32),
         ),
         in_specs=[HB] * 7 + [VM, HB, HB, HB] + [VM] * 2 + [HB] * 3,
-        out_specs=(HB,) + (VM,) * 6,
+        out_specs=(HB, VM, HB) + (VM,) * 5,
         scratch_shapes=[
             pltpu.VMEM((length, width), bf16),
             pltpu.VMEM((8, length), f32),
@@ -1078,7 +1089,6 @@
             pltpu.VMEM((half, size, d), bf16),
             pltpu.VMEM((half, size, d), bf16),
             pltpu.VMEM((max(half - 1, 1), size, d), bf16),
-            pltpu.VMEM((size, d), bf16),
             pltpu.VMEM((16, d), f32),
             pltpu.VMEM((n - 1, 16, lanes_s), f32),
             pltpu.VMEM((planes - 1, 16, d), f32),
@@ -1094,6 +1104,7 @@
             pltpu.VMEM((length, width), bf16),
             pltpu.VMEM((length, width), bf16),
             pltpu.VMEM((d, 3 * width), bf16),
+            pltpu.VMEM((n, rq, 3 * width), bf16),
         ]
         + [pltpu.VMEM((count, planes, rows, cols), bf16) for count, rows, cols in parts] * 2
         + [pltpu.VMEM((planes - 1, *part), bf16) for part in parts]
@@ -1199,13 +1210,14 @@
         )
         gsm = jnp.concatenate([jnp.stack([g_b_out, g_g2, g_s2, g_b_back]), bin_rows])
 
-        (own_result, g_tok, gq, go, gi, gb, small) = backward_call(
-            n, m, result, d_att_tok, d_resid, q, k, v, o, lse, h1, wq, tb[0], sv, gsm,
+        (own_result, g_tok, swapped, g_qkv, go, gi, gb, small) = backward_call(
+            n, m, result, d_att_tok, d_resid, q, k, v, o, lse, h1, wq, tb, sv, gsm,
             g_w_out.reshape(n, m // 2, 2, d // nd, d),
             g_w_in.reshape(n, m // 2, 2, d // nd, ff // 2),
             g_w_back.reshape(n // 2, m // 2, 2, ff // nd, d),
         )
-        g_qkv = gq.reshape(n, rq, 3, width).transpose(1, 2, 0, 3).reshape(rq, 3 * d).astype(f32)
+        away = lax.rem(lax.axis_index("shard"), 2) != lax.axis_index("seq") // (n // 2)
+        g_tok = jnp.where(away, swapped.astype(f32), g_tok)
         mine = lax.dynamic_slice_in_dim(small, lax.axis_index("shard") * per, per, 1)
         return (
             own_result[None], g_tok[None], mine[0], mine[1], g_qkv, mine[2], mine[3], go, mine[4],

time: 347 us -> 345 us (level)
  local copies, waits for them, and re-layouts: 28.3 us -> 23.5 us
    unnamed x58 -> x60, local copies, waits for them, and re-layouts: 14.5 us -> 14.6 us
  transfers between devices with their start and end apart: 3 -> 3, of which waited for: 1 -> 1; matrix products, arithmetic and copies ran while one was open for 18% -> 17% of each run, Pallas kernels for 0% -> 0%
where the time goes in v5:
time: 345 us; the launch traced here: 340 us
  Pallas kernels  246 us (71%)
  matrix products  55.2 us (16%)
  local copies, waits for them, and re-layouts  23.5 us (7%)
  other arithmetic  9.56 us (3%)
    pallas_call x1, Pallas kernels, backward_call(): pl.pallas_call(kernel, name='attend_back_reduce', out_shape=(sds((size, d...  127 us
    pallas_call x1, Pallas kernels, forward_call(): pl.pallas_call(kernel, name='gather_attend', out_shape=(sds((n, m // 2, 2...  119 us
    dot_general x3, matrix products, col_dot(): return lax.dot_general(a, b, TN, preferred_element_type=f32)  21.3 us
    dot_general x3, matrix products, row_dot(): return lax.dot_general(a, b, NT, preferred_element_type=f32)  18.9 us
    dot_general x3, matrix products, dot(): return jnp.dot(a, b, preferred_element_type=f32)  14.9 us
    unnamed x60, local copies, waits for them, and re-layouts  14.6 us
  transfers between devices with their start and end apart: 3, of which 1 were waited for; matrix products, arithmetic and copies ran while one was open for 17% of the time, Pallas kernels for 0%

profile of v5, /device:TPU:1, one launch (start us, length us, event | category | flops | bytes accessed | tf_op | source)
XLA Modules:
  0.0 339.7 jit_solution(11120872015882105877)
XLA Ops:
  3.1 119.4 %gather_attend.1 = (bf16[4,4,2,32,1024]{4,3,2,1,0:T(8,128)(2,1)}, bf16[4,4,2,32,2048]{4,3,2,1,0:T(8,128)(2,1)}, bf16[2,4,2,128,1024]{4,3,2,1,0:T(8,128)(2,1)}, b...) custom-call(bf16[512,1024]{1,0:T(8,128)(2,1)} %bitcast.98, ...), custom_call_target="tpu_custom_call" | custom-call | flops 5368709120 | bytes 83886080 | tf_op jit(solution)/shard_map/gather_attend/pallas_call | solution.py:542
  123.4 0.9 fusion.51
  124.5 5.3 %fusion.52 = (f32[1024]{0:T(1024)S(1)}, f32[1024,1024]{1,0:T(8,128)S(1)}) fusion(f32[1024]{0:T(1024)S(1)} %bitcast.89, bf16[1024,1024]{1,0:T(8,128)(2,1)} %bitcast.106, bf16[1024,1024]{1,0:T(8,128)(2,1)} %bitcast.107, bf16[2,512,1024]{2,1,0:T(8,128)(2,1)} %get-tuple-element.40.refs_10_), kind=kOutput, calls=%fused_computation.102 | convolution fusion | flops 2151676928 | bytes 10493952 | tf_op jit(solution)/shard_map/dot_general | solution.py:30
  131.8 3.1 copy-done.17
  134.9 4.5 %broadcast_add_fusion = f32[1024,2048]{1,0:T(8,128)S(1)} fusion(f32[2048]{0:T(1024)S(1)} %add.120, bf16[1024,2048]{1,0:T(8,128)(2,1)S(1)} %bitcast.100, f32[1024,1024]{1,0:T(8,128)S(1)} %subtract_multiply_fusion, f32[1024]{0:T(1024)S(1)} %bitcast.87, f32[1024]{0:T(1024)S(1)} %bitcast.78), kind=kOutput, calls=%fused_computation.29 | convolution fusion | flops 4300210176 | bytes 16793600 | tf_op jit(solution)/shard_map/dot_general | solution.py:30
  139.5 5.1 %fusion.24 = f32[1024,1024]{1,0:T(8,128)S(1)} fusion(bf16[2048,1024]{1,0:T(8,128)(2,1)S(1)} %bitcast.102, f32[1024,2048]{1,0:T(8,128)S(1)} %broadcast_add_fusion), kind=kOutput, calls=%fused_computation.32 | convolution fusion | flops 4313841664 | bytes 16777216 | tf_op jit(solution)/shard_map/dot_general | solution.py:30
  144.6 1.9 copy-done.7
  146.7 1.5 collective-permute-start
  148.4 2.0 copy-done.20
  150.4 12.1 %convert_reduce_fusion = (f32[2048]{0:T(1024)S(1)}, bf16[1024,2048]{1,0:T(8,128)(2,1)S(1)}) fusion(f32[1024,2048]{1,0:T(8,128)} %copy-done.23, bf16[1024,1024]{1,0:T(8,128)(2,1)S(1)} %constant_dynamic-update-slice_fusion, bf16[2048,1024]{1,0:T(8,128)(2,1)S(1)} %bitcast.103), kind=kOutput, calls=%fused_computation.21 | convolution fusion | flops 4339005440 | bytes 18882560 | tf_op jit(solution)/shard_map/dot_general | solution.py:34
  162.5 4.5 %fusion.53 = f32[1024,1024]{1,0:T(8,128)S(1)} fusion(bf16[1024,2048]{1,0:T(8,128)(2,1)S(1)} %get-tuple-element.55, bf16[1024,2048]{1,0:T(8,128)(2,1)S(1)} %bitcast.101), kind=kOutput, calls=%fused_computation.103 | convolution fusion | flops 4294967296 | bytes 12582912 | tf_op jit(solution)/shard_map/dot_general | solution.py:34
  167.1 1.9 copy-done.4
  169.0 1.1 slice.133
  170.4 12.0 %fusion.26 = bf16[2048,1024]{1,0:T(8,128)(2,1)} fusion(bf16[1024,1024]{1,0:T(8,128)(2,1)} %copy-done.11, f32[1024,2048]{1,0:T(8,128)} %copy-done.23), kind=kOutput, calls=%fused_computation.34 | convolution fusion | flops 4315938816 | bytes 14680064 | tf_op jit(solution)/shard_map/dot_general | solution.py:38
  182.4 3.0 fusion.31.refs_0_
  185.5 6.7 %convolution_convert_fusion = bf16[1024,2048]{1,0:T(8,128)(2,1)} fusion(bf16[1024,2048]{1,0:T(8,128)(2,1)S(1)} %copy-done.25, f32[1024,1024]{1,0:T(8,128)S(1)} %copy-done.3, f32[1024]{0:T(1024)S(1)} %bitcast.88, f32[1024]{0:T(1024)S(1)} %bitcast.79), kind=kOutput, calls=%fused_computation.35 | convolution fusion | flops 4300210176 | bytes 12591104 | tf_op jit(solution)/shard_map/dot_general | solution.py:38
  192.1 2.3 collective-permute-done.2
  195.3 0.9 fusion.50
  196.9 2.3 convolution_convert_fusion.2.refs_1_
  199.2 2.7 convolution_convert_fusion.1
  202.5 126.9 %attend_back_reduce.1 = (bf16[512,1024]{1,0:T(8,128)(2,1)}, f32[512,1024]{1,0:T(8,128)}, bf16[512,1024]{1,0:T(8,128)(2,1)}, f32[32,3072]{1,0:T(8,128)}, f32[32,1...) custom-call(bf16[512,1024]{1,0:T(8,128)(2,1)} %fusion.31.refs_0_, ...), custom_call_target="tpu_custom_call" | custom-call | flops 11811160064 | bytes 83886080 | tf_op jit(solution)/shard_map/attend_back_reduce/pallas_call | solution.py:1063
  330.9 3.1 select_bitcast_fusion
  334.0 1.6 dynamic-slice_bitcast_fusion
  335.5 1.0 copy.43
  (92 shorter events, 12.6 us)
Async XLA Ops:
  122.5 25.8 %collective-permute-start.1 = (bf16[512,1024]{1,0:T(8,128)(2,1)}, bf16[512,1024]{1,0:T(8,128)(2,1)S(1)}, u32[]{:S(2)}, u32[]{:S(2)}) collective-permute-start(bf16[512,1024]{1,0:T(8,128)(2,1)} %get-tuple-element.46), channel_id=1, source_target_pairs={{0,8},{1,9},{2,10},{3,11},{4,12},{5,13},{6,14},{7,15},{8,0},{9,1},... | collective-permute-start | bytes 3145736 | tf_op jit(solution)/shard_map/ppermute | solution.py:1171
  130.4 17.7 %copy-start.16 = (f32[1024]{0:T(1024)}, f32[1024]{0:T(1024)S(1)}, u32[]{:S(2)}) copy-start(f32[1024]{0:T(1024)S(1)} %add_rsqrt_fusion) | copy-start | bytes 12292
  130.4 4.5 %copy-start.17 = (bf16[4,4,2,32,2048]{4,3,2,1,0:T(8,128)(2,1)S(1)}, bf16[4,4,2,32,2048]{4,3,2,1,0:T(8,128)(2,1)}, u32[]{:S(2)}) copy-start(bf16[4,4,2,32,2048]{4,3,2,1,0:T(8,128)(2,1)} %get-tuple-element.44) | copy-start | bytes 12582916
  131.8 7.6 %copy-start.2 = (f32[1024,1024]{1,0:T(8,128)}, f32[1024,1024]{1,0:T(8,128)S(1)}, u32[]{:S(2)}) copy-start(f32[1024,1024]{1,0:T(8,128)S(1)} %subtract_multiply_fusion) | copy-start | bytes 12582916
  134.9 4.6 %copy-start.19 = (bf16[2,4,2,128,1024]{4,3,2,1,0:T(8,128)(2,1)S(1)}, bf16[2,4,2,128,1024]{4,3,2,1,0:T(8,128)(2,1)}, u32[]{:S(2)}) copy-start(bf16[2,4,2,128,1024]{4,3,2,1,0:T(8,128)(2,1)} %get-tuple-element.45) | copy-start | bytes 12582916
  139.5 5.1 %copy-start.23 = (f32[1024,2048]{1,0:T(8,128)}, f32[1024,2048]{1,0:T(8,128)S(1)}, u32[]{:S(2)}) copy-start(f32[1024,2048]{1,0:T(8,128)S(1)} %broadcast_add_fusion) | copy-start | bytes 25165828
  139.5 8.7 %copy-start.6 = (bf16[512,1024]{1,0:T(8,128)(2,1)S(1)}, bf16[512,1024]{1,0:T(8,128)(2,1)}, u32[]{:S(2)}) copy-start(bf16[512,1024]{1,0:T(8,128)(2,1)} %get-tuple-element.46) | copy-start | bytes 3145732
  146.7 35.7 %collective-permute-start = (bf16[512,1024]{1,0:T(8,128)(2,1)S(1)}, bf16[512,1024]{1,0:T(8,128)(2,1)}, u32[]{:S(2)}, u32[]{:S(2)}) collective-permute-start(bf16[512,1024]{1,0:T(8,128)(2,1)S(1)} %slice.134), channel_id=1, source_target_pairs={{0,8},{1,9},{2,10},{3,11},{4,12},{5,13},{6,14},{7,15},{8,0},{9,1},... | collective-permute-start | bytes 3145736 | tf_op jit(solution)/shard_map/ppermute | solution.py:1171
  150.4 12.1 %copy-start.11 = (bf16[1024,1024]{1,0:T(8,128)(2,1)}, bf16[1024,1024]{1,0:T(8,128)(2,1)S(1)}, u32[]{:S(2)}) copy-start(bf16[1024,1024]{1,0:T(8,128)(2,1)S(1)} %constant_dynamic-update-slice_fusion) | copy-start | bytes 6291460
  150.4 12.1 %copy-start.18 = (bf16[4,4,2,32,2048]{4,3,2,1,0:T(8,128)(2,1)S(1)}, bf16[4,4,2,32,2048]{4,3,2,1,0:T(8,128)(2,1)}, u32[]{:S(2)}) copy-start(bf16[4,4,2,32,2048]{4,3,2,1,0:T(8,128)(2,1)} %get-tuple-element.44) | copy-start | bytes 12582916
  162.5 4.6 %copy-start.24 = (bf16[1024,2048]{1,0:T(8,128)(2,1)}, bf16[1024,2048]{1,0:T(8,128)(2,1)S(1)}, u32[]{:S(2)}) copy-start(bf16[1024,2048]{1,0:T(8,128)(2,1)S(1)} %get-tuple-element.55) | copy-start | bytes 12582916
  170.2 24.3 %collective-permute-start.2 = (bf16[512,1024]{1,0:T(8,128)(2,1)}, bf16[512,1024]{1,0:T(8,128)(2,1)S(1)}, u32[]{:S(2)}, u32[]{:S(2)}) collective-permute-start(bf16[512,1024]{1,0:T(8,128)(2,1)} %slice.133), channel_id=1, source_target_pairs={{0,8},{1,9},{2,10},{3,11},{4,12},{5,13},{6,14},{7,15},{8,0},{9,1},... | collective-permute-start | bytes 3145736 | tf_op jit(solution)/shard_map/ppermute | solution.py:1171
  170.4 12.0 %copy-start.1 = (f32[1024,1024]{1,0:T(8,128)S(1)}, f32[1024,1024]{1,0:T(8,128)}, u32[]{:S(2)}) copy-start(f32[1024,1024]{1,0:T(8,128)} %copy-done) | copy-start | bytes 12582916
  170.4 12.0 %copy-start.8 = (f32[1024,1024]{1,0:T(8,128)S(1)}, f32[1024,1024]{1,0:T(8,128)}, u32[]{:S(2)}) copy-start(f32[1024,1024]{1,0:T(8,128)} %copy-done.7) | copy-start | bytes 12582916
  170.4 15.0 %copy-start.25 = (bf16[1024,2048]{1,0:T(8,128)(2,1)S(1)}, bf16[1024,2048]{1,0:T(8,128)(2,1)}, u32[]{:S(2)}) copy-start(bf16[1024,2048]{1,0:T(8,128)(2,1)} %copy-done.24) | copy-start | bytes 12582916
  182.4 3.1 copy-start.3
  185.5 9.0 %copy-start.5 = (f32[1024,1024]{1,0:T(8,128)S(1)}, f32[1024,1024]{1,0:T(8,128)}, u32[]{:S(2)}) copy-start(f32[1024,1024]{1,0:T(8,128)} %copy-done.4) | copy-start | bytes 12582916
  192.1 3.2 slice-start
  196.3 5.6 %copy-start.9 = (f32[512,1024]{1,0:T(8,128)}, f32[512,1024]{1,0:T(8,128)S(1)}, u32[]{:S(2)}) copy-start(f32[512,1024]{1,0:T(8,128)S(1)} %get-tuple-element.70.refs_2_) | copy-start | bytes 6291460
  329.4 6.2 %copy-start.10 = (bf16[512,1024]{1,0:T(8,128)(2,1)S(1)}, bf16[512,1024]{1,0:T(8,128)(2,1)}, u32[]{:S(2)}) copy-start(bf16[512,1024]{1,0:T(8,128)(2,1)} %get-tuple-element.57) | copy-start | bytes 3145732
  329.4 7.1 %copy-start.14 = (f32[32,3072]{1,0:T(8,128)S(1)}, f32[32,3072]{1,0:T(8,128)}, u32[]{:S(2)}) copy-start(f32[32,3072]{1,0:T(8,128)} %get-tuple-element.115) | copy-start | bytes 1179652
  329.4 7.9 %copy-start.15 = (f32[32,1024]{1,0:T(8,128)S(1)}, f32[32,1024]{1,0:T(8,128)}, u32[]{:S(2)}) copy-start(f32[32,1024]{1,0:T(8,128)} %get-tuple-element.118) | copy-start | bytes 393220
  330.9 7.1 %copy-start.13 = (f32[32,4096]{1,0:T(8,128)S(1)}, f32[32,4096]{1,0:T(8,128)}, u32[]{:S(2)}) copy-start(f32[32,4096]{1,0:T(8,128)} %get-tuple-element.122) | copy-start | bytes 1572868
  330.9 7.8 %copy-start.12 = (f32[128,1024]{1,0:T(8,128)S(1)}, f32[128,1024]{1,0:T(8,128)}, u32[]{:S(2)}) copy-start(f32[128,1024]{1,0:T(8,128)} %get-tuple-element.124) | copy-start | bytes 1572868
  (6 other events, 12.5 us)
